TPU v7x, 128 devices: a whole 4x4x4 slice. The times are simulated.
128 devices in a mesh: row: 32 (over y, z, core), col: 4 (over x).
Axes of the slice: x: 4, y: 4, z: 4, core: 2. Of those that a mesh axis runs over, the one named last changes fastest.
Arguments:
- acts_in: bfloat16 [32768, 4608], P('row'), may hold values from -64 to 64
- grad_query: bfloat16 [32768, 4096], P('row', 'col'), may hold values from -1.41421356 to 1.41421356
- attn_out: bfloat16 [32768, 4096], P('row'), may hold values from -64 to 64
- grad_out: bfloat16 [32768, 4608], P('row', 'col'), may hold values from -1.41421356 to 1.41421356
- row_query: float32 [4608], P('row'), may hold values from 0.05 to 18
- col_query: float32 [4096], P('col'), may hold values from 0.05 to 2
- row_output: float32 [4096], P('row'), may hold values from 0.05 to 18
- col_output: float32 [4608], P('col'), may hold values from 0.05 to 2
Outputs:
- update_query: bfloat16 [4608, 4096], P('row', 'col')
- update_output: bfloat16 [4096, 4608], P('row', 'col')
- new_row_query: float32 [4608], P('row')
- new_col_query: float32 [4096], P('col')
- new_row_output: float32 [4096], P('row')
- new_col_output: float32 [4608], P('col')
All inputs are finite; a program needn't handle non-finite values.
Results may differ from a plain program's by a relative error of at most 0.028.
Values may be sent and summed in bfloat16 or wider, within the bound.
No kernel may reach another device: no remote copies, remote signals or barrier semaphores. Data moves between devices by JAX's collectives and lax.ppermute only.
A program may use at most 128 MiB of HBM per device.

v0:
```python
import functools

import jax
import jax.numpy as jnp
from jax import lax
from jax.experimental import pallas as pl
from jax.experimental.pallas import tpu as pltpu
from jax.sharding import Mesh
from jax.sharding import PartitionSpec as P


CLIP = 3072
Y, Z, CORE, X = "row_0", "row_1", "row_2", "col"
ROW = (Y, Z, CORE)

GRANTS = 59, 44, 10, 10, 10, 10
decay_rate = 0.81
epsilon_one = 1e-30


def shift(value, axis, by):
    size = lax.axis_size(axis)
    return lax.ppermute(value, axis, [(i, (i + by) % size) for i in range(size)])


def dot_rows(left, right_ref):
    product = lax.dot_general(
        left, right_ref[...], (((0,), (0,)), ((), ())), preferred_element_type=jnp.float32
    )
    return product.astype(jnp.bfloat16)


def query_kernel(first, group, where_ref, left_ref, right_ref, keep_ref, give_ref):
    core = where_ref[0]
    width = 8 * group // 3

    def block(b, carry):
        start = where_ref[1 + first + 2 * b]
        for side in (0, 1):

            @pl.when(core == side)
            def _(side=side):
                for s in range(3):
                    columns = pl.ds(pl.multiple_of(start + s * width, 128), width)
                    product = dot_rows(left_ref[:, columns], right_ref)
                    for j in range(8):
                        low, high = max(j * group, s * width), min((j + 1) * group, (s + 1) * width)
                        if low < high:
                            target = keep_ref if j % 2 == side else give_ref
                            rows = slice(low - j * group, high - j * group)
                            piece = product[low - s * width : high - s * width]
                            target[b, where_ref[9 + j // 2], rows, :] = piece

        return carry

    lax.fori_loop(0, keep_ref.shape[0], block, 0)


def output_kernel(first, group, where_ref, left_ref, right_ref, keep_ref, give_ref):
    core = where_ref[0]

    def block(b, carry):
        start = where_ref[5 + first + 2 * b]
        for half, target in ((1 - core, give_ref), (core, keep_ref)):
            runs = [
                left_ref[
                    :,
                    pl.ds(
                        pl.multiple_of(
                            start + where_ref[13 + e] * (8 * group) + half * group, 128
                        ),
                        group,
                    ),
                ]
                for e in range(4)
            ]
            product = dot_rows(jnp.concatenate(runs, axis=1), right_ref)
            for e in range(4):
                target[b, e] = product[e * group : (e + 1) * group]
        return carry

    lax.fori_loop(0, keep_ref.shape[0], block, 0)


def first_kernel(
    aligned, first, group, where_ref, left_ref, right_ref,
    keep_ref, give_ref, left_copy, right_copy, total, sem,
):
    core = where_ref[0]
    steps = sem.shape[0] - 1
    tokens = left_ref.shape[0] // steps
    pieces, width = total.shape[:2]
    runs = [pl.ds(i * tokens, tokens) for i in range(steps)]
    loads = [pltpu.make_async_copy(right_ref, right_copy, sem.at[steps])]
    loads += [
        pltpu.make_async_copy(left_ref.at[run], left_copy.at[run], sem.at[i])
        for i, run in enumerate(runs)
    ]
    for load in loads:
        load.start()
    loads[0].wait()
    start = where_ref[(5 if aligned else 1) + first]
    for i, run in enumerate(runs):
        loads[1 + i].wait()

        def slab(s, carry, i=i, run=run):
            if aligned:
                half = lax.rem(1 - core + s, 2)
                starts = [start + where_ref[13 + e] * (8 * group) + half * group for e in range(4)]
            else:
                starts = [start + s * width]
            part = width // len(starts)
            left = [left_copy[run, pl.ds(pl.multiple_of(c, 128), part)] for c in starts]
            product = lax.dot_general(
                left[0] if len(left) == 1 else jnp.concatenate(left, axis=1),
                right_copy[run, :],
                (((0,), (0,)), ((), ())),
                preferred_element_type=jnp.float32,
            )
            total[s] = product if i == 0 else total[s] + product
            return carry

        lax.fori_loop(0, pieces, slab, 0)
    if aligned:
        for e in range(4):
            rows = slice(e * group, (e + 1) * group)
            give_ref[0, e] = total[0, rows].astype(jnp.bfloat16)
            keep_ref[0, e] = total[1, rows].astype(jnp.bfloat16)
        return
    for side in (0, 1):

        @pl.when(core == side)
        def _(side=side):
            for s in range(pieces):
                for j in range(8):
                    low, high = max(j * group, s * width), min((j + 1) * group, (s + 1) * width)
                    if low < high:
                        target = keep_ref if j % 2 == side else give_ref
                        rows = slice(low - j * group, high - j * group)
                        piece = total[s, low - s * width : high - s * width]
                        target[0, where_ref[9 + j // 2], rows, :] = piece.astype(jnp.bfloat16)


def first_blocks(aligned, where, left, right, first, group, vmem):
    tokens, columns = right.shape
    shape = jax.ShapeDtypeStruct((1, 4, group, columns), jnp.bfloat16)
    pieces = 2 if aligned else 3
    return pl.pallas_call(
        functools.partial(first_kernel, aligned, first, group),
        out_shape=[shape, shape],
        in_specs=[pl.BlockSpec(memory_space=pltpu.SMEM)]
        + [pl.BlockSpec(memory_space=pl.ANY)] * 2,
        out_specs=[pl.BlockSpec(memory_space=pltpu.VMEM)] * 2,
        scratch_shapes=[
            pltpu.VMEM(left.shape, left.dtype),
            pltpu.VMEM(right.shape, right.dtype),
            pltpu.VMEM((pieces, 8 * group // pieces, columns), jnp.float32),
            pltpu.SemaphoreType.DMA((5,)),
        ],
        compiler_params=pltpu.CompilerParams(vmem_limit_bytes=vmem * 2**20),
        cost_estimate=pl.CostEstimate(
            flops=16 * group * tokens * columns, bytes_accessed=16 * group * tokens, transcendentals=0
        ),
    )(where, left, right)


def partial_blocks(kernel, where, left, right, blocks, group, vmem):
    tokens, columns = right.shape
    shape = jax.ShapeDtypeStruct((len(blocks), 4, group, columns), jnp.bfloat16)
    rows = 8 * group * len(blocks)
    return pl.pallas_call(
        functools.partial(kernel, blocks[0], group),
        out_shape=[shape, shape],
        in_specs=[pl.BlockSpec(memory_space=pltpu.SMEM)]
        + [pl.BlockSpec(memory_space=pltpu.VMEM)] * 2,
        out_specs=[pl.BlockSpec(memory_space=pltpu.VMEM)] * 2,
        compiler_params=pltpu.CompilerParams(vmem_limit_bytes=vmem * 2**20),
        cost_estimate=pl.CostEstimate(
            flops=2 * rows * tokens * columns, bytes_accessed=2 * rows * tokens, transcendentals=0
        ),
    )(where, left, right)


def add_kernel(plan, step, *refs):
    inputs, outputs = refs[: len(refs) - len(plan)], refs[len(refs) - len(plan) :]
    rows = outputs[0].shape[1]
    for o, entries in enumerate(plan):
        for e, terms in enumerate(entries):

            def chunk(i, carry, o=o, e=e, terms=terms):
                at = pl.ds(pl.multiple_of(i * step, step), step)
                value = None
                for which, entry in terms:
                    term = inputs[which][entry, at, :].astype(jnp.float32)
                    value = term if value is None else value + term
                outputs[o][e, at, :] = value.astype(outputs[o].dtype)
                return carry

            lax.fori_loop(0, rows // step, chunk, 0)


def add_entries(inputs, plan, dtypes=None):
    rows, columns = inputs[0].shape[1:]
    dtypes = dtypes or [jnp.bfloat16] * len(plan)
    return pl.pallas_call(
        functools.partial(add_kernel, plan, 16),
        out_shape=[jax.ShapeDtypeStruct((len(p), rows, columns), d) for p, d in zip(plan, dtypes)],
        in_specs=[pl.BlockSpec(memory_space=pltpu.VMEM)] * len(inputs),
        out_specs=[pl.BlockSpec(memory_space=pltpu.VMEM)] * len(plan),
        cost_estimate=pl.CostEstimate(flops=600_000_000, bytes_accessed=0, transcendentals=0),
        compiler_params=pltpu.CompilerParams(vmem_limit_bytes=12 * 2**20),
    )(*inputs)


def wide(value):
    return value.astype(jnp.float32)


def after(value, *others):
    return lax.optimization_barrier((value, *others))[0]


def flat(value):
    return value.reshape(-1, *value.shape[2:])


def sums_of(gradient):
    square = gradient * gradient
    return jnp.sum(square, axis=1), jnp.sum(square, axis=0)


def pack_kernel(split, *refs):
    rows_refs, (query_cols, output_cols, query_old, output_old, rows_ref, packed_ref) = refs[:4], refs[4:]
    total = rows_refs[0][...] + rows_refs[1][...] + rows_refs[2][...] + rows_refs[3][...]
    rows_ref[...] = total
    lane = lax.broadcasted_iota(jnp.int32, (1, 128), 1)
    scalars = jnp.zeros((1, 128), jnp.float32)
    parts = (total[:, :split], total[:, split:], query_old[...], output_old[...])
    for i, part in enumerate(parts):
        scalars = jnp.where(lane == i, jnp.sum(part, axis=1, keepdims=True), scalars)
    row = jnp.concatenate([query_cols[...], output_cols[...], scalars], axis=1)
    for i in range(packed_ref.shape[0]):
        packed_ref[i] = row


def finish_kernel(
    split,
    across,
    along,
    sums_ref,
    rows_ref,
    query_row,
    query_col,
    output_row,
    output_col,
    query_grad,
    output_grad,
    query_update,
    query_row_new,
    query_col_new,
    output_update,
    output_row_new,
    output_col_new,
):
    sums = sums_ref[0]
    for i in range(1, sums_ref.shape[0]):
        sums = sums + sums_ref[i]
    query_width, output_width = query_col.shape[1], output_col.shape[1]
    lane = lax.broadcasted_iota(jnp.int32, (1, 128), 1)
    tail = sums[:, query_width + output_width :]
    query_squares, output_squares, query_old, output_old = (
        jnp.sum(jnp.where(lane == i, tail, 0.0), axis=1, keepdims=True) for i in range(4)
    )
    norm = jnp.sqrt(query_squares + output_squares)
    clip_scale = CLIP / jnp.maximum(norm, jnp.float32(CLIP))
    squared_scale = clip_scale * clip_scale

    def one(at, offset, squares, old, row, col, grad, update, row_new, col_new):
        rows, columns = grad.shape
        whole_rows, whole_cols = rows * along, columns * across
        fresh = 1.0 - decay_rate

        def mean(value, count):
            return squared_scale * value / count + epsilon_one

        level = decay_rate * old / whole_rows + fresh * mean(squares, whole_rows * whole_cols)
        row_next = decay_rate * row[...] + fresh * mean(rows_ref[:, at : at + rows], whole_cols)
        col_next = decay_rate * col[...] + fresh * mean(sums[:, offset : offset + columns], whole_rows)
        row_new[...] = row_next
        col_new[...] = col_next
        square = (rows, rows)
        diagonal = lax.broadcasted_iota(jnp.int32, square, 0) == lax.broadcasted_iota(
            jnp.int32, square, 1
        )
        down = jnp.sum(jnp.where(diagonal, row_next, 0.0), axis=1, keepdims=True)
        scale = clip_scale * lax.rsqrt(down / level)
        update[...] = (grad[...] * scale * lax.rsqrt(col_next)).astype(jnp.bfloat16)

    one(
        0, 0, query_squares, query_old,
        query_row, query_col, query_grad, query_update, query_row_new, query_col_new,
    )
    one(
        split, query_width, output_squares, output_old,
        output_row, output_col, output_grad, output_update, output_row_new, output_col_new,
    )


def small_call(kernel, outs, *inputs):
    return pl.pallas_call(
        kernel,
        out_shape=[jax.ShapeDtypeStruct(shape, dtype) for shape, dtype in outs],
        in_specs=[pl.BlockSpec(memory_space=pltpu.VMEM)] * len(inputs),
        out_specs=[pl.BlockSpec(memory_space=pltpu.VMEM)] * len(outs),
        compiler_params=pltpu.CompilerParams(vmem_limit_bytes=12 * 2**20),
        cost_estimate=pl.CostEstimate(flops=600_000_000, bytes_accessed=0, transcendentals=0),
    )(*inputs)


def shards(acts_in, grad_query, attn_out, grad_out, row_query, col_query, row_output, col_output):
    query_rows = row_query.shape[0]
    output_rows = row_output.shape[0]
    query_width = col_query.shape[0]
    output_width = col_output.shape[0]
    y, z, core = lax.axis_index(Y), lax.axis_index(Z), lax.axis_index(CORE)
    pair_query, pair_output = 2 * query_rows, 2 * output_rows
    where = jnp.stack(
        [core]
        + [lax.rem(y + k, 4) * (4 * pair_query) for k in range(4)]
        + [lax.rem(z + k, 4) * pair_output for k in range(4)]
        + [lax.rem(k + 4 - z, 4) for k in range(4)]
        + [lax.rem(y + k, 4) for k in range(4)]
    ).astype(jnp.int32)

    def made(kernel, where, left, right, ks, group, vmem):
        kept, give = partial_blocks(kernel, where, left, right, ks, group, vmem)
        return kept, flat(kept), flat(shift(give, CORE, 1))

    def query_blocks(where, ks, vmem):
        return made(query_kernel, where, acts_in, grad_query, ks, query_rows, vmem)

    def output_blocks(where, ks, vmem):
        return made(output_kernel, where, attn_out, grad_out, ks, output_rows, vmem)

    one, two = (2, 1), (3, 0)
    far_plan = [[[(0, e), (1, e)] for e in half] for half in (one, two)]

    def near_plan(half, relayed):
        plan = [[[(0, base + e), (1, base + e)] for e in half] for base in (0, 4)]
        for i, terms in enumerate(plan[relayed]):
            terms.append((2, i))
        return plan

    last_one = [[[(0, e), (1, e), (2, i), (3, i)]] for i, e in enumerate(one)]
    last_two = [[[(0, e), (1, e), (2, i), (3, i)]] for i, e in enumerate(two)]

    keep, give = first_blocks(False, where, acts_in, grad_query, 2, query_rows, GRANTS[0])
    query_block = flat(keep), flat(shift(give, CORE, 1))
    keep, give = first_blocks(
        True, after(where, keep), attn_out, grad_out, 2, output_rows, GRANTS[1]
    )
    output_block = flat(keep), flat(shift(give, CORE, 1))
    query_far_one, query_far_two = add_entries(query_block, far_plan)
    query_low = shift(query_far_one, Y, 1)
    query_high = shift(query_far_two, Y, -1)
    output_far_one, output_far_two = add_entries(output_block, far_plan)
    output_low = shift(output_far_one, Z, 1)
    output_high = shift(output_far_two, Z, -1)

    ready = after(where, query_far_one, output_far_one)
    query_made, *query_block = query_blocks(ready, (1, 3), GRANTS[2])
    output_made, *output_block = output_blocks(after(where, query_made), (1, 3), GRANTS[3])

    def near(block, arrived, half, relayed, axis):
        plus, minus = add_entries((*block, arrived), near_plan(half, relayed))
        return plus, (shift(plus, axis, 1), shift(minus, axis, -1))

    query_plus, query_one = near(query_block, query_low, one, 0, Y)
    output_plus, output_one = near(output_block, output_low, one, 0, Z)
    query_plus, query_two = near(query_block, query_high, two, 1, Y)
    output_plus, output_two = near(output_block, output_high, two, 1, Z)

    ready = after(where, query_plus, output_plus)
    query_made, *query_block = query_blocks(ready, (0,), GRANTS[4])
    output_made, *output_block = output_blocks(after(where, query_made), (0,), GRANTS[5])
    wide_own = [jnp.bfloat16, jnp.float32]
    query_2, query_1 = add_entries((*query_block, *query_one), last_one)
    query_sent = [shift(query_2, Z, 2), shift(query_1, Z, 1)]
    output_2, output_1 = add_entries((*output_block, *output_one), last_one)
    output_sent = [shift(output_2, Y, 2), shift(output_1, Y, 1)]
    query_3, query_own = add_entries((*query_block, *query_two), last_two, wide_own)
    query_sent.append(shift(query_3, Z, 3))
    output_3, output_own = add_entries((*output_block, *output_two), last_two, wide_own)
    output_sent.append(shift(output_3, Y, 3))
    query_grad = query_own[0] + sum(wide(p[0]) for p in query_sent)
    output_grad = output_own[0] + sum(wide(p[0]) for p in output_sent)

    query_rowsum, query_colsum = sums_of(query_grad)
    output_rowsum, output_colsum = sums_of(output_grad)
    line = lambda value: value.reshape(1, -1)
    split = -(-query_rows // 128) * 128
    rows = line(
        jnp.concatenate(
            [query_rowsum, jnp.zeros((split - query_rows,), jnp.float32), output_rowsum]
        )
    )
    others = [shift(rows, X, k) for k in (2, 1, 3)]
    width = query_width + output_width + 128
    rows, packed = small_call(
        functools.partial(pack_kernel, split),
        [(rows.shape, jnp.float32), ((lax.axis_size(ROW), 1, width), jnp.float32)],
        rows,
        *others,
        *(line(v) for v in (query_colsum, output_colsum, row_query, row_output)),
    )
    packed = lax.all_to_all(packed, ROW, 0, 0, tiled=True)
    olds = [line(v) for v in (row_query, col_query, row_output, col_output)]
    update_query, new_row_query, new_col_query, update_output, new_row_output, new_col_output = small_call(
        functools.partial(finish_kernel, split, lax.axis_size(X), lax.axis_size(ROW)),
        [
            (query_grad.shape, jnp.bfloat16),
            (olds[0].shape, jnp.float32),
            (olds[1].shape, jnp.float32),
            (output_grad.shape, jnp.bfloat16),
            (olds[2].shape, jnp.float32),
            (olds[3].shape, jnp.float32),
        ],
        packed,
        rows,
        *olds,
        query_grad,
        output_grad,
    )
    return (
        update_query,
        update_output,
        new_row_query.reshape(-1),
        new_col_query.reshape(-1),
        new_row_output.reshape(-1),
        new_col_output.reshape(-1),
    )


def solution(mesh):
    split = Mesh(
        mesh.devices.reshape(4, 4, 2, mesh.shape[X]), (Y, Z, CORE, X)
    )
    return jax.shard_map(
        shards,
        mesh=split,
        in_specs=(
            P(ROW, None),
            P(ROW, X),
            P(ROW, None),
            P(ROW, X),
            P(ROW),
            P(X),
            P(ROW),
            P(X),
        ),
        out_specs=(P(ROW, X), P(ROW, X), P(ROW), P(X), P(ROW), P(X)),
        check_vma=False,
    )
```

profile of v0, /device:TPU:1, one launch (start us, length us, event | category | flops | bytes accessed | tf_op | source)
XLA Modules:
  0.0 163.8 jit_solution(7201759110100986976)
XLA Ops:
  1.2 9.6 %shard_map.127 = (bf16[1,4,144,1024]{3,2,1,0:T(8,128)(2,1)}, bf16[1,4,144,1024]{3,2,1,0:T(8,128)(2,1)}) custom-call(s32[17]{0:T(128)} %stack.71.where_ref, bf16[1024,4608]{1,0:T(8,128)(2,1)} %left_ref.10, bf16[1024,1024]{1,0:T(8,128)(2,1)} %right_ref.10), custom_call_target="tpu_custom_call" | custom-call | flops 2415919104 | bytes 2359296 | tf_op jit(solution)/shard_map/pallas_call | solution.py:148
  12.3 7.3 %shard_map.129 = (bf16[1,4,128,1152]{3,2,1,0:T(8,128)(2,1)S(1)}, bf16[1,4,128,1152]{3,2,1,0:T(8,128)(2,1)S(1)}) custom-call(s32[17]{0:T(128)S(1)} %copy-done.4, bf16[1024,4096]{1,0:T(8,128)(2,1)} %left_ref.11, bf16[1024,1152]{1,0:T(8,128)(2,1)S(1)} %copy-done.1), custom_call_target="tpu_custom_call" | custom-call | flops 2415919104 | bytes 2097152 | tf_op jit(solution)/shard_map/pallas_call | solution.py:148
  20.2 2.3 %collective-permute-done.1 = bf16[1,4,128,1152]{3,2,1,0:T(8,128)(2,1)S(1)} collective-permute-done((bf16[1,4,128,1152]{3,2,1,0:T(8,128)(2,1)S(1)}, bf16[1,4,128,1152]{3,2,1,0:T(8,128)(2,1)S(1)}, u32[]{:S(2)}, u32[]{:S(2)}) %collective-permute-start.1) | collective-permute-done | bytes 1179680 | tf_op jit(solution)/shard_map/ppermute | solution.py:23
  23.1 5.9 %shard_map.131 = (bf16[2,4,144,1024]{3,2,1,0:T(8,128)(2,1)S(1)}, bf16[2,4,144,1024]{3,2,1,0:T(8,128)(2,1)S(1)}) custom-call(s32[17]{0:T(128)S(1)} %copy-done.4, bf16[1024,4608]{1,0:T(8,128)(2,1)S(1)} %copy-done, bf16[1024,1024]{1,0:T(8,128)(2,1)S(1)} %copy-done.2), custom_call_target="tpu_custom_call" | custom-call | flops 4831838208 | bytes 4718592 | tf_op jit(solution)/shard_map/pallas_call | solution.py:171
  29.2 6.4 %shard_map.133 = (bf16[2,4,128,1152]{3,2,1,0:T(8,128)(2,1)S(1)}, bf16[2,4,128,1152]{3,2,1,0:T(8,128)(2,1)S(1)}) custom-call(s32[17]{0:T(128)S(1)} %copy-done.4, bf16[1024,4096]{1,0:T(8,128)(2,1)S(1)} %bitcast.43, bf16[1024,1152]{1,0:T(8,128)(2,1)S(1)} %copy-done.1), custom_call_target="tpu_custom_call" | custom-call | flops 4831838208 | bytes 4194304 | tf_op jit(solution)/shard_map/pallas_call | solution.py:171
  38.9 3.8 %collective-permute-start.5 = (bf16[2,128,1152]{2,1,0:T(8,128)(2,1)S(1)}, bf16[2,128,1152]{2,1,0:T(8,128)(2,1)S(1)}, u32[]{:S(2)}, u32[]{:S(2)}) collective-permute-start(bf16[2,128,1152]{2,1,0:T(8,128)(2,1)S(1)} %get-tuple-element.66), channel_id=1, source_target_pairs={{0,24},{8,0},{16,8},{24,16},{1,25},{9,1},{17,9},{25,17},{2,26},{10... | collective-permute-start | bytes 1769480 | tf_op jit(solution)/shard_map/ppermute | solution.py:23
  42.7 9.7 %collective-permute-done.9.refs_2_ = bf16[2,144,1024]{2,1,0:T(8,128)(2,1)S(1)} collective-permute-done((bf16[2,144,1024]{2,1,0:T(8,128)(2,1)S(1)}, bf16[2,144,1024]{2,1,0:T(8,128)(2,1)S(1)}, u32[]{:S(2)}, u32[]{:S(2)}) %collective-permute-start.9) | collective-permute-done | bytes 589856 | tf_op jit(solution)/shard_map/ppermute | solution.py:23
  55.7 3.2 %shard_map.135 = (bf16[1,4,144,1024]{3,2,1,0:T(8,128)(2,1)S(1)}, bf16[1,4,144,1024]{3,2,1,0:T(8,128)(2,1)S(1)}) custom-call(s32[17]{0:T(128)S(1)} %copy-done.4, bf16[1024,4608]{1,0:T(8,128)(2,1)S(1)} %copy-done, bf16[1024,1024]{1,0:T(8,128)(2,1)S(1)} %copy-done.2), custom_call_target="tpu_custom_call" | custom-call | flops 2415919104 | bytes 2359296 | tf_op jit(solution)/shard_map/pallas_call | solution.py:171
  60.5 2.6 %collective-permute-start.11 = (bf16[2,144,1024]{2,1,0:T(8,128)(2,1)S(1)}, bf16[2,144,1024]{2,1,0:T(8,128)(2,1)S(1)}, u32[]{:S(2)}, u32[]{:S(2)}) collective-permute-start(bf16[2,144,1024]{2,1,0:T(8,128)(2,1)S(1)} %get-tuple-element.74), channel_id=1, source_target_pairs={{0,96},{32,0},{64,32},{96,64},{1,97},{33,1},{65,33},{97,65},{2,98}... | collective-permute-start | bytes 1769480 | tf_op jit(solution)/shard_map/ppermute | solution.py:23
  63.4 3.5 %shard_map.139 = (bf16[1,4,128,1152]{3,2,1,0:T(8,128)(2,1)S(1)}, bf16[1,4,128,1152]{3,2,1,0:T(8,128)(2,1)S(1)}) custom-call(s32[17]{0:T(128)S(1)} %copy-done.4, bf16[1024,4096]{1,0:T(8,128)(2,1)S(1)} %bitcast.43, bf16[1024,1152]{1,0:T(8,128)(2,1)S(1)} %copy-done.1), custom_call_target="tpu_custom_call" | custom-call | flops 2415919104 | bytes 2097152 | tf_op jit(solution)/shard_map/pallas_call | solution.py:171
  66.9 1.8 %collective-permute-done.18.refs_2_ = bf16[2,128,1152]{2,1,0:T(8,128)(2,1)S(1)} collective-permute-done((bf16[2,128,1152]{2,1,0:T(8,128)(2,1)S(1)}, bf16[2,128,1152]{2,1,0:T(8,128)(2,1)S(1)}, u32[]{:S(2)}, u32[]{:S(2)}) %collective-permute-start.18) | collective-permute-done | bytes 589856 | tf_op jit(solution)/shard_map/ppermute | solution.py:23
  70.8 4.9 %collective-permute-done.11.refs_3_ = bf16[2,144,1024]{2,1,0:T(8,128)(2,1)S(1)} collective-permute-done((bf16[2,144,1024]{2,1,0:T(8,128)(2,1)S(1)}, bf16[2,144,1024]{2,1,0:T(8,128)(2,1)S(1)}, u32[]{:S(2)}, u32[]{:S(2)}) %collective-permute-start.11) | collective-permute-done | bytes 589856 | tf_op jit(solution)/shard_map/ppermute | solution.py:23
  77.4 11.0 %collective-permute-done.8.refs_3_ = bf16[2,144,1024]{2,1,0:T(8,128)(2,1)S(1)} collective-permute-done((bf16[2,144,1024]{2,1,0:T(8,128)(2,1)S(1)}, bf16[2,144,1024]{2,1,0:T(8,128)(2,1)S(1)}, u32[]{:S(2)}, u32[]{:S(2)}) %collective-permute-start.8) | collective-permute-done | bytes 589856 | tf_op jit(solution)/shard_map/ppermute | solution.py:23
  88.4 2.5 %collective-permute-start.20 = (bf16[2,128,1152]{2,1,0:T(8,128)(2,1)S(1)}, bf16[2,128,1152]{2,1,0:T(8,128)(2,1)S(1)}, u32[]{:S(2)}, u32[]{:S(2)}) collective-permute-start(bf16[2,128,1152]{2,1,0:T(8,128)(2,1)S(1)} %get-tuple-element.84), channel_id=1, source_target_pairs={{0,24},{8,0},{16,8},{24,16},{1,25},{9,1},{17,9},{25,17},{2,26},{10... | collective-permute-start | bytes 1769480 | tf_op jit(solution)/shard_map/ppermute | solution.py:23
  94.2 8.5 %collective-permute-done.20.refs_3_ = bf16[2,128,1152]{2,1,0:T(8,128)(2,1)S(1)} collective-permute-done((bf16[2,128,1152]{2,1,0:T(8,128)(2,1)S(1)}, bf16[2,128,1152]{2,1,0:T(8,128)(2,1)S(1)}, u32[]{:S(2)}, u32[]{:S(2)}) %collective-permute-start.20) | collective-permute-done | bytes 589856 | tf_op jit(solution)/shard_map/ppermute | solution.py:23
  104.0 2.1 %collective-permute-start.14 = (bf16[1,144,1024]{2,1,0:T(8,128)(2,1)S(1)}, bf16[1,144,1024]{2,1,0:T(8,128)(2,1)S(1)}, u32[]{:S(2)}, u32[]{:S(2)}) collective-permute-start(bf16[1,144,1024]{2,1,0:T(8,128)(2,1)S(1)} %get-tuple-element.77), channel_id=1, source_target_pairs={{0,24},{8,0},{16,8},{24,16},{1,25},{9,1},{17,9},{25,17},{2,26},{10... | collective-permute-start | bytes 884744 | tf_op jit(solution)/shard_map/ppermute | solution.py:23
  106.5 9.3 %collective-permute-done.17.refs_3_ = bf16[2,128,1152]{2,1,0:T(8,128)(2,1)S(1)} collective-permute-done((bf16[2,128,1152]{2,1,0:T(8,128)(2,1)S(1)}, bf16[2,128,1152]{2,1,0:T(8,128)(2,1)S(1)}, u32[]{:S(2)}, u32[]{:S(2)}) %collective-permute-start.17) | collective-permute-done | bytes 589856 | tf_op jit(solution)/shard_map/ppermute | solution.py:23
  117.5 1.8 %collective-permute-start.22 = (bf16[1,128,1152]{2,1,0:T(8,128)(2,1)S(1)}, bf16[1,128,1152]{2,1,0:T(8,128)(2,1)S(1)}, u32[]{:S(2)}, u32[]{:S(2)}) collective-permute-start(bf16[1,128,1152]{2,1,0:T(8,128)(2,1)S(1)} %get-tuple-element.86), channel_id=1, source_target_pairs={{0,32},{32,64},{64,96},{96,0},{1,33},{33,65},{65,97},{97,1},{2,34}... | collective-permute-start | bytes 884744 | tf_op jit(solution)/shard_map/ppermute | solution.py:23
  120.6 7.4 %collective-permute-done.14 = bf16[1,144,1024]{2,1,0:T(8,128)(2,1)S(1)} collective-permute-done((bf16[1,144,1024]{2,1,0:T(8,128)(2,1)S(1)}, bf16[1,144,1024]{2,1,0:T(8,128)(2,1)S(1)}, u32[]{:S(2)}, u32[]{:S(2)}) %collective-permute-start.14) | collective-permute-done | bytes 294944 | tf_op jit(solution)/shard_map/ppermute | solution.py:23
  128.7 2.5 %collective-permute-start.26 = (f32[1,384]{1,0:T(1,128)S(1)}, f32[1,384]{1,0:T(1,128)S(1)}, u32[]{:S(2)}, u32[]{:S(2)}) collective-permute-start(f32[1,384]{1,0:T(1,128)S(1)} %reshape.107.refs_0_), channel_id=1, source_target_pairs={{0,3},{1,0},{2,1},{3,2},{4,7},{5,4},{6,5},{7,6},{8,11},{9,8},{10,9... | collective-permute-start | bytes 4616 | tf_op jit(solution)/shard_map/ppermute | solution.py:23
  131.2 1.7 %collective-permute-start.24 = (f32[1,384]{1,0:T(1,128)S(1)}, f32[1,384]{1,0:T(1,128)S(1)}, u32[]{:S(2)}, u32[]{:S(2)}) collective-permute-start(f32[1,384]{1,0:T(1,128)S(1)} %reshape.107.refs_0_), channel_id=1, source_target_pairs={{0,2},{1,3},{2,0},{3,1},{4,6},{5,7},{6,4},{7,5},{8,10},{9,11},{10,... | collective-permute-start | bytes 4616 | tf_op jit(solution)/shard_map/ppermute | solution.py:23
  132.9 2.2 %collective-permute-done.25.refs_2_ = f32[1,384]{1,0:T(1,128)S(1)} collective-permute-done((f32[1,384]{1,0:T(1,128)S(1)}, f32[1,384]{1,0:T(1,128)S(1)}, u32[]{:S(2)}, u32[]{:S(2)}) %collective-permute-start.25) | collective-permute-done | bytes 1568 | tf_op jit(solution)/shard_map/ppermute | solution.py:23
  136.0 16.8 %all-to-all-start = ((f32[32,1,2304]{2,1,0:T(1,128)}), f32[32,1,2304]{2,1,0:T(1,128)S(1)}, u32[]{:S(2)}, u32[]{:S(2)}) async-start(f32[32,1,2304]{2,1,0:T(1,128)} %get-tuple-element.88), calls=%async_computation | async-start | bytes 589824 | tf_op jit(solution)/shard_map/all_to_all | solution.py:416
  152.8 9.3 %all-to-all-done.sums_ref = f32[32,1,2304]{2,1,0:T(1,128)S(1)} async-done(((f32[32,1,2304]{2,1,0:T(1,128)}), f32[32,1,2304]{2,1,0:T(1,128)S(1)}, u32[]{:S(2)}, u32[]{:S(2)}) %all-to-all-start) | async-done | bytes 294944 | tf_op jit(solution)/shard_map/all_to_all | solution.py:416
  (82 shorter events, 26.6 us)
Async XLA Ops:
  10.9 8.9 %collective-permute-start = (bf16[1,4,144,1024]{3,2,1,0:T(8,128)(2,1)}, bf16[1,4,144,1024]{3,2,1,0:T(8,128)(2,1)S(1)}, u32[]{:S(2)}, u32[]{:S(2)}) collective-permute-start(bf16[1,4,144,1024]{3,2,1,0:T(8,128)(2,1)} %get-tuple-element.52), channel_id=1, source_target_pairs={{0,4},{4,0},{1,5},{5,1},{2,6},{6,2},{3,7},{7,3},{8,12},{12,8},{9,1... | collective-permute-start | bytes 3538952 | tf_op jit(solution)/shard_map/ppermute | solution.py:23
  29.0 24.9 %collective-permute-start.2 = (bf16[2,4,144,1024]{3,2,1,0:T(8,128)(2,1)S(1)}, bf16[2,4,144,1024]{3,2,1,0:T(8,128)(2,1)S(1)}, u32[]{:S(2)}, u32[]{:S(2)}) collective-permute-start(bf16[2,4,144,1024]{3,2,1,0:T(8,128)(2,1)S(1)} %get-tuple-element.60), channel_id=1, source_target_pairs={{0,4},{4,0},{1,5},{5,1},{2,6},{6,2},{3,7},{7,3},{8,12},{12,8},{9,1... | collective-permute-start | bytes 7077896 | tf_op jit(solution)/shard_map/ppermute | solution.py:23
  35.6 19.5 %collective-permute-start.4 = (bf16[2,4,128,1152]{3,2,1,0:T(8,128)(2,1)S(1)}, bf16[2,4,128,1152]{3,2,1,0:T(8,128)(2,1)S(1)}, u32[]{:S(2)}, u32[]{:S(2)}) collective-permute-start(bf16[2,4,128,1152]{3,2,1,0:T(8,128)(2,1)S(1)} %get-tuple-element.65), channel_id=1, source_target_pairs={{0,4},{4,0},{1,5},{5,1},{2,6},{6,2},{3,7},{7,3},{8,12},{12,8},{9,1... | collective-permute-start | bytes 7077896 | tf_op jit(solution)/shard_map/ppermute | solution.py:23
  36.1 16.3 %collective-permute-start.9 = (bf16[2,144,1024]{2,1,0:T(8,128)(2,1)S(1)}, bf16[2,144,1024]{2,1,0:T(8,128)(2,1)S(1)}, u32[]{:S(2)}, u32[]{:S(2)}) collective-permute-start(bf16[2,144,1024]{2,1,0:T(8,128)(2,1)S(1)} %get-tuple-element.53), channel_id=1, source_target_pairs={{0,32},{32,64},{64,96},{96,0},{1,33},{33,65},{65,97},{97,1},{2,34}... | collective-permute-start | bytes 1769480 | tf_op jit(solution)/shard_map/ppermute | solution.py:23
  37.5 17.0 %collective-permute-start.3 = (bf16[2,144,1024]{2,1,0:T(8,128)(2,1)S(1)}, bf16[2,144,1024]{2,1,0:T(8,128)(2,1)S(1)}, u32[]{:S(2)}, u32[]{:S(2)}) collective-permute-start(bf16[2,144,1024]{2,1,0:T(8,128)(2,1)S(1)} %get-tuple-element.61), channel_id=1, source_target_pairs={{0,96},{32,0},{64,32},{96,64},{1,97},{33,1},{65,33},{97,65},{2,98}... | collective-permute-start | bytes 1769480 | tf_op jit(solution)/shard_map/ppermute | solution.py:23
  38.9 16.2 %collective-permute-start.5 = (bf16[2,128,1152]{2,1,0:T(8,128)(2,1)S(1)}, bf16[2,128,1152]{2,1,0:T(8,128)(2,1)S(1)}, u32[]{:S(2)}, u32[]{:S(2)}) collective-permute-start(bf16[2,128,1152]{2,1,0:T(8,128)(2,1)S(1)} %get-tuple-element.66), channel_id=1, source_target_pairs={{0,24},{8,0},{16,8},{24,16},{1,25},{9,1},{17,9},{25,17},{2,26},{10... | collective-permute-start | bytes 1769480 | tf_op jit(solution)/shard_map/ppermute | solution.py:23
  52.4 16.4 %collective-permute-start.18 = (bf16[2,128,1152]{2,1,0:T(8,128)(2,1)S(1)}, bf16[2,128,1152]{2,1,0:T(8,128)(2,1)S(1)}, u32[]{:S(2)}, u32[]{:S(2)}) collective-permute-start(bf16[2,128,1152]{2,1,0:T(8,128)(2,1)S(1)} %get-tuple-element.57), channel_id=1, source_target_pairs={{0,8},{8,16},{16,24},{24,0},{1,9},{9,17},{17,25},{25,1},{2,10},{10... | collective-permute-start | bytes 1769480 | tf_op jit(solution)/shard_map/ppermute | solution.py:23
  54.4 15.8 %collective-permute-start.10 = (bf16[2,144,1024]{2,1,0:T(8,128)(2,1)S(1)}, bf16[2,144,1024]{2,1,0:T(8,128)(2,1)S(1)}, u32[]{:S(2)}, u32[]{:S(2)}) collective-permute-start(bf16[2,144,1024]{2,1,0:T(8,128)(2,1)S(1)} %get-tuple-element.73), channel_id=1, source_target_pairs={{0,32},{32,64},{64,96},{96,0},{1,33},{33,65},{65,97},{97,1},{2,34}... | collective-permute-start | bytes 1769480 | tf_op jit(solution)/shard_map/ppermute | solution.py:23
  58.9 33.1 %collective-permute-start.6 = (bf16[1,4,144,1024]{3,2,1,0:T(8,128)(2,1)S(1)}, bf16[1,4,144,1024]{3,2,1,0:T(8,128)(2,1)S(1)}, u32[]{:S(2)}, u32[]{:S(2)}) collective-permute-start(bf16[1,4,144,1024]{3,2,1,0:T(8,128)(2,1)S(1)} %get-tuple-element.70), channel_id=1, source_target_pairs={{0,4},{4,0},{1,5},{5,1},{2,6},{6,2},{3,7},{7,3},{8,12},{12,8},{9,1... | collective-permute-start | bytes 3538952 | tf_op jit(solution)/shard_map/ppermute | solution.py:23
  60.5 15.2 %collective-permute-start.11 = (bf16[2,144,1024]{2,1,0:T(8,128)(2,1)S(1)}, bf16[2,144,1024]{2,1,0:T(8,128)(2,1)S(1)}, u32[]{:S(2)}, u32[]{:S(2)}) collective-permute-start(bf16[2,144,1024]{2,1,0:T(8,128)(2,1)S(1)} %get-tuple-element.74), channel_id=1, source_target_pairs={{0,96},{32,0},{64,32},{96,64},{1,97},{33,1},{65,33},{97,65},{2,98}... | collective-permute-start | bytes 1769480 | tf_op jit(solution)/shard_map/ppermute | solution.py:23
  63.2 25.2 %collective-permute-start.8 = (bf16[2,144,1024]{2,1,0:T(8,128)(2,1)S(1)}, bf16[2,144,1024]{2,1,0:T(8,128)(2,1)S(1)}, u32[]{:S(2)}, u32[]{:S(2)}) collective-permute-start(bf16[2,144,1024]{2,1,0:T(8,128)(2,1)S(1)} %get-tuple-element.71), channel_id=1, source_target_pairs={{0,96},{32,0},{64,32},{96,64},{1,97},{33,1},{65,33},{97,65},{2,98}... | collective-permute-start | bytes 1769480 | tf_op jit(solution)/shard_map/ppermute | solution.py:23
  68.7 35.3 %collective-permute-start.15 = (bf16[1,4,128,1152]{3,2,1,0:T(8,128)(2,1)S(1)}, bf16[1,4,128,1152]{3,2,1,0:T(8,128)(2,1)S(1)}, u32[]{:S(2)}, u32[]{:S(2)}) collective-permute-start(bf16[1,4,128,1152]{3,2,1,0:T(8,128)(2,1)S(1)} %get-tuple-element.80), channel_id=1, source_target_pairs={{0,4},{4,0},{1,5},{5,1},{2,6},{6,2},{3,7},{7,3},{8,12},{12,8},{9,1... | collective-permute-start | bytes 3538952 | tf_op jit(solution)/shard_map/ppermute | solution.py:23
  70.3 20.7 %collective-permute-start.7 = (bf16[2,144,1024]{2,1,0:T(8,128)(2,1)S(1)}, bf16[2,144,1024]{2,1,0:T(8,128)(2,1)S(1)}, u32[]{:S(2)}, u32[]{:S(2)}) collective-permute-start(bf16[2,144,1024]{2,1,0:T(8,128)(2,1)S(1)} %get-tuple-element.62), channel_id=1, source_target_pairs={{0,32},{32,64},{64,96},{96,0},{1,33},{33,65},{65,97},{97,1},{2,34}... | collective-permute-start | bytes 1769480 | tf_op jit(solution)/shard_map/ppermute | solution.py:23
  75.8 17.0 %collective-permute-start.19 = (bf16[2,128,1152]{2,1,0:T(8,128)(2,1)S(1)}, bf16[2,128,1152]{2,1,0:T(8,128)(2,1)S(1)}, u32[]{:S(2)}, u32[]{:S(2)}) collective-permute-start(bf16[2,128,1152]{2,1,0:T(8,128)(2,1)S(1)} %get-tuple-element.83), channel_id=1, source_target_pairs={{0,8},{8,16},{16,24},{24,0},{1,9},{9,17},{17,25},{25,1},{2,10},{10... | collective-permute-start | bytes 1769480 | tf_op jit(solution)/shard_map/ppermute | solution.py:23
  88.4 14.3 %collective-permute-start.20 = (bf16[2,128,1152]{2,1,0:T(8,128)(2,1)S(1)}, bf16[2,128,1152]{2,1,0:T(8,128)(2,1)S(1)}, u32[]{:S(2)}, u32[]{:S(2)}) collective-permute-start(bf16[2,128,1152]{2,1,0:T(8,128)(2,1)S(1)} %get-tuple-element.84), channel_id=1, source_target_pairs={{0,24},{8,0},{16,8},{24,16},{1,25},{9,1},{17,9},{25,17},{2,26},{10... | collective-permute-start | bytes 1769480 | tf_op jit(solution)/shard_map/ppermute | solution.py:23
  90.9 24.9 %collective-permute-start.17 = (bf16[2,128,1152]{2,1,0:T(8,128)(2,1)S(1)}, bf16[2,128,1152]{2,1,0:T(8,128)(2,1)S(1)}, u32[]{:S(2)}, u32[]{:S(2)}) collective-permute-start(bf16[2,128,1152]{2,1,0:T(8,128)(2,1)S(1)} %get-tuple-element.81), channel_id=1, source_target_pairs={{0,24},{8,0},{16,8},{24,16},{1,25},{9,1},{17,9},{25,17},{2,26},{10... | collective-permute-start | bytes 1769480 | tf_op jit(solution)/shard_map/ppermute | solution.py:23
  92.0 25.5 %collective-permute-start.16 = (bf16[2,128,1152]{2,1,0:T(8,128)(2,1)S(1)}, bf16[2,128,1152]{2,1,0:T(8,128)(2,1)S(1)}, u32[]{:S(2)}, u32[]{:S(2)}) collective-permute-start(bf16[2,128,1152]{2,1,0:T(8,128)(2,1)S(1)} %get-tuple-element.67), channel_id=1, source_target_pairs={{0,8},{8,16},{16,24},{24,0},{1,9},{9,17},{17,25},{25,1},{2,10},{10... | collective-permute-start | bytes 1769480 | tf_op jit(solution)/shard_map/ppermute | solution.py:23
  92.8 26.9 %collective-permute-start.12 = (bf16[1,144,1024]{2,1,0:T(8,128)(2,1)S(1)}, bf16[1,144,1024]{2,1,0:T(8,128)(2,1)S(1)}, u32[]{:S(2)}, u32[]{:S(2)}) collective-permute-start(bf16[1,144,1024]{2,1,0:T(8,128)(2,1)S(1)} %get-tuple-element.75), channel_id=1, source_target_pairs={{0,16},{8,24},{16,0},{24,8},{1,17},{9,25},{17,1},{25,9},{2,18},{10... | collective-permute-start | bytes 884744 | tf_op jit(solution)/shard_map/ppermute | solution.py:23
  102.7 17.9 %collective-permute-start.13 = (bf16[1,144,1024]{2,1,0:T(8,128)(2,1)S(1)}, bf16[1,144,1024]{2,1,0:T(8,128)(2,1)S(1)}, u32[]{:S(2)}, u32[]{:S(2)}) collective-permute-start(bf16[1,144,1024]{2,1,0:T(8,128)(2,1)S(1)} %get-tuple-element.76), channel_id=1, source_target_pairs={{0,8},{8,16},{16,24},{24,0},{1,9},{9,17},{17,25},{25,1},{2,10},{10... | collective-permute-start | bytes 884744 | tf_op jit(solution)/shard_map/ppermute | solution.py:23
  104.0 24.0 %collective-permute-start.14 = (bf16[1,144,1024]{2,1,0:T(8,128)(2,1)S(1)}, bf16[1,144,1024]{2,1,0:T(8,128)(2,1)S(1)}, u32[]{:S(2)}, u32[]{:S(2)}) collective-permute-start(bf16[1,144,1024]{2,1,0:T(8,128)(2,1)S(1)} %get-tuple-element.77), channel_id=1, source_target_pairs={{0,24},{8,0},{16,8},{24,16},{1,25},{9,1},{17,9},{25,17},{2,26},{10... | collective-permute-start | bytes 884744 | tf_op jit(solution)/shard_map/ppermute | solution.py:23
  115.8 12.5 %collective-permute-start.21 = (bf16[1,128,1152]{2,1,0:T(8,128)(2,1)S(1)}, bf16[1,128,1152]{2,1,0:T(8,128)(2,1)S(1)}, u32[]{:S(2)}, u32[]{:S(2)}) collective-permute-start(bf16[1,128,1152]{2,1,0:T(8,128)(2,1)S(1)} %get-tuple-element.85), channel_id=1, source_target_pairs={{0,64},{32,96},{64,0},{96,32},{1,65},{33,97},{65,1},{97,33},{2,66}... | collective-permute-start | bytes 884744 | tf_op jit(solution)/shard_map/ppermute | solution.py:23
  117.5 10.9 %collective-permute-start.22 = (bf16[1,128,1152]{2,1,0:T(8,128)(2,1)S(1)}, bf16[1,128,1152]{2,1,0:T(8,128)(2,1)S(1)}, u32[]{:S(2)}, u32[]{:S(2)}) collective-permute-start(bf16[1,128,1152]{2,1,0:T(8,128)(2,1)S(1)} %get-tuple-element.86), channel_id=1, source_target_pairs={{0,32},{32,64},{64,96},{96,0},{1,33},{33,65},{65,97},{97,1},{2,34}... | collective-permute-start | bytes 884744 | tf_op jit(solution)/shard_map/ppermute | solution.py:23
  119.7 8.6 %collective-permute-start.23 = (bf16[1,128,1152]{2,1,0:T(8,128)(2,1)S(1)}, bf16[1,128,1152]{2,1,0:T(8,128)(2,1)S(1)}, u32[]{:S(2)}, u32[]{:S(2)}) collective-permute-start(bf16[1,128,1152]{2,1,0:T(8,128)(2,1)S(1)} %get-tuple-element.87), channel_id=1, source_target_pairs={{0,96},{32,0},{64,32},{96,64},{1,97},{33,1},{65,33},{97,65},{2,98}... | collective-permute-start | bytes 884744 | tf_op jit(solution)/shard_map/ppermute | solution.py:23
  136.0 26.1 %all-to-all-start = ((f32[32,1,2304]{2,1,0:T(1,128)}), f32[32,1,2304]{2,1,0:T(1,128)S(1)}, u32[]{:S(2)}, u32[]{:S(2)}) async-start(f32[32,1,2304]{2,1,0:T(1,128)} %get-tuple-element.88), calls=%async_computation | async-start | bytes 589824 | tf_op jit(solution)/shard_map/all_to_all | solution.py:416
  (15 other events, 129.7 us)
where the time goes:
time: 164 us
  waiting for transfers between devices  66.5 us (41%)
  starting transfers between devices  52 us (32%)
  Pallas kernels  42.5 us (26%)
    ppermute x27, waiting for transfers between devices, shift(): lax.ppermute(value, axis, [(i, (i + by) % size) for i in range(size)])  57.3 us
    ppermute x27, starting transfers between devices, shift(): lax.ppermute(value, axis, [(i, (i + by) % size) for i in range(size)])  35.2 us
    pallas_call x4, Pallas kernels, partial_blocks(): pl.pallas_call(functools.partial(kernel, blocks[0], group), out_shape=[sh...  19 us
    pallas_call x2, Pallas kernels, first_blocks(): pl.pallas_call(functools.partial(first_kernel, aligned, first, group), ou...  16.9 us
    all_to_all x1, starting transfers between devices, shards(): packed = lax.all_to_all(packed, ROW, 0, 0, tiled=True)  16.8 us
    all_to_all x1, waiting for transfers between devices, shards(): packed = lax.all_to_all(packed, ROW, 0, 0, tiled=True)  9.27 us
    pallas_call x10, Pallas kernels, add_entries(): pl.pallas_call(functools.partial(add_kernel, plan, 16), out_shape=[jax.Sh...  4.66 us
  transfers between devices with their start and end apart: 28, of which 10 were waited for; matrix products, arithmetic and copies ran while one was open for 0% of the time, Pallas kernels for 15%

commit v1 on v0

--- a/solution.py
+++ b/solution.py
@@ -13,7 +13,7 @@
 Y, Z, CORE, X = "row_0", "row_1", "row_2", "col"
 ROW = (Y, Z, CORE)
 
-GRANTS = 59, 44, 10, 10, 10, 10
+GRANTS = 30, 30, 12, 12, 12, 12
 decay_rate = 0.81
 epsilon_one = 1e-30
 
@@ -80,88 +80,6 @@
         return carry
 
     lax.fori_loop(0, keep_ref.shape[0], block, 0)
-
-
-def first_kernel(
-    aligned, first, group, where_ref, left_ref, right_ref,
-    keep_ref, give_ref, left_copy, right_copy, total, sem,
-):
-    core = where_ref[0]
-    steps = sem.shape[0] - 1
-    tokens = left_ref.shape[0] // steps
-    pieces, width = total.shape[:2]
-    runs = [pl.ds(i * tokens, tokens) for i in range(steps)]
-    loads = [pltpu.make_async_copy(right_ref, right_copy, sem.at[steps])]
-    loads += [
-        pltpu.make_async_copy(left_ref.at[run], left_copy.at[run], sem.at[i])
-        for i, run in enumerate(runs)
-    ]
-    for load in loads:
-        load.start()
-    loads[0].wait()
-    start = where_ref[(5 if aligned else 1) + first]
-    for i, run in enumerate(runs):
-        loads[1 + i].wait()
-
-        def slab(s, carry, i=i, run=run):
-            if aligned:
-                half = lax.rem(1 - core + s, 2)
-                starts = [start + where_ref[13 + e] * (8 * group) + half * group for e in range(4)]
-            else:
-                starts = [start + s * width]
-            part = width // len(starts)
-            left = [left_copy[run, pl.ds(pl.multiple_of(c, 128), part)] for c in starts]
-            product = lax.dot_general(
-                left[0] if len(left) == 1 else jnp.concatenate(left, axis=1),
-                right_copy[run, :],
-                (((0,), (0,)), ((), ())),
-                preferred_element_type=jnp.float32,
-            )
-            total[s] = product if i == 0 else total[s] + product
-            return carry
-
-        lax.fori_loop(0, pieces, slab, 0)
-    if aligned:
-        for e in range(4):
-            rows = slice(e * group, (e + 1) * group)
-            give_ref[0, e] = total[0, rows].astype(jnp.bfloat16)
-            keep_ref[0, e] = total[1, rows].astype(jnp.bfloat16)
-        return
-    for side in (0, 1):
-
-        @pl.when(core == side)
-        def _(side=side):
-            for s in range(pieces):
-                for j in range(8):
-                    low, high = max(j * group, s * width), min((j + 1) * group, (s + 1) * width)
-                    if low < high:
-                        target = keep_ref if j % 2 == side else give_ref
-                        rows = slice(low - j * group, high - j * group)
-                        piece = total[s, low - s * width : high - s * width]
-                        target[0, where_ref[9 + j // 2], rows, :] = piece.astype(jnp.bfloat16)
-
-
-def first_blocks(aligned, where, left, right, first, group, vmem):
-    tokens, columns = right.shape
-    shape = jax.ShapeDtypeStruct((1, 4, group, columns), jnp.bfloat16)
-    pieces = 2 if aligned else 3
-    return pl.pallas_call(
-        functools.partial(first_kernel, aligned, first, group),
-        out_shape=[shape, shape],
-        in_specs=[pl.BlockSpec(memory_space=pltpu.SMEM)]
-        + [pl.BlockSpec(memory_space=pl.ANY)] * 2,
-        out_specs=[pl.BlockSpec(memory_space=pltpu.VMEM)] * 2,
-        scratch_shapes=[
-            pltpu.VMEM(left.shape, left.dtype),
-            pltpu.VMEM(right.shape, right.dtype),
-            pltpu.VMEM((pieces, 8 * group // pieces, columns), jnp.float32),
-            pltpu.SemaphoreType.DMA((5,)),
-        ],
-        compiler_params=pltpu.CompilerParams(vmem_limit_bytes=vmem * 2**20),
-        cost_estimate=pl.CostEstimate(
-            flops=16 * group * tokens * columns, bytes_accessed=16 * group * tokens, transcendentals=0
-        ),
-    )(where, left, right)
 
 
 def partial_blocks(kernel, where, left, right, blocks, group, vmem):
@@ -354,12 +272,8 @@
     last_one = [[[(0, e), (1, e), (2, i), (3, i)]] for i, e in enumerate(one)]
     last_two = [[[(0, e), (1, e), (2, i), (3, i)]] for i, e in enumerate(two)]
 
-    keep, give = first_blocks(False, where, acts_in, grad_query, 2, query_rows, GRANTS[0])
-    query_block = flat(keep), flat(shift(give, CORE, 1))
-    keep, give = first_blocks(
-        True, after(where, keep), attn_out, grad_out, 2, output_rows, GRANTS[1]
-    )
-    output_block = flat(keep), flat(shift(give, CORE, 1))
+    query_made, *query_block = query_blocks(where, (2,), GRANTS[0])
+    output_made, *output_block = output_blocks(after(where, query_made), (2,), GRANTS[1])
     query_far_one, query_far_two = add_entries(query_block, far_plan)
     query_low = shift(query_far_one, Y, 1)
     query_high = shift(query_far_two, Y, -1)
@@ -381,8 +295,8 @@
     output_plus, output_two = near(output_block, output_high, two, 1, Z)
 
     ready = after(where, query_plus, output_plus)
-    query_made, *query_block = query_blocks(ready, (0,), GRANTS[4])
-    output_made, *output_block = output_blocks(after(where, query_made), (0,), GRANTS[5])
+    output_made, *output_block = output_blocks(ready, (0,), GRANTS[4])
+    query_made, *query_block = query_blocks(after(where, output_made), (0,), GRANTS[5])
     wide_own = [jnp.bfloat16, jnp.float32]
     query_2, query_1 = add_entries((*query_block, *query_one), last_one)
     query_sent = [shift(query_2, Z, 2), shift(query_1, Z, 1)]

time: 164 us -> 159 us (0.970)
  Pallas kernels: 42.5 us -> 32.4 us
  local copies, waits for them, and re-layouts: 0.66 us -> 9.89 us
  waiting for transfers between devices: 66.5 us -> 63.1 us
    pallas_call x2 -> x0, Pallas kernels: 16.9 us -> none  [first_blocks(): pl.pallas_call(functools.partial(first_kernel, aligned, first, group), ou...]
    unnamed x22 -> x24, local copies, waits for them, and re-layouts: 0.06 us -> 9.78 us
    pallas_call x4 -> x6, Pallas kernels: 19 us -> 25.8 us  [partial_blocks(): pl.pallas_call(functools.partial(kernel, blocks[0], group), out_shape=[sh...]
    ppermute x27, waiting for transfers between devices: 57.3 us -> 53.8 us  [shift(): lax.ppermute(value, axis, [(i, (i + by) % size) for i in range(size)])]
    ppermute x27, starting transfers between devices: 35.2 us -> 33.4 us  [shift(): lax.ppermute(value, axis, [(i, (i + by) % size) for i in range(size)])]
  transfers between devices with their start and end apart: 28 -> 28, of which waited for: 10 -> 12; matrix products, arithmetic and copies ran while one was open for 0% -> 0% of each run, Pallas kernels for 15% -> 13%
where the time goes in v1:
time: 159 us
  waiting for transfers between devices  63.1 us (40%)
  starting transfers between devices  51.4 us (32%)
  Pallas kernels  32.4 us (20%)
  local copies, waits for them, and re-layouts  9.89 us (6%)
    ppermute x27, waiting for transfers between devices, shift(): lax.ppermute(value, axis, [(i, (i + by) % size) for i in range(size)])  53.8 us
    ppermute x27, starting transfers between devices, shift(): lax.ppermute(value, axis, [(i, (i + by) % size) for i in range(size)])  33.4 us
    pallas_call x6, Pallas kernels, partial_blocks(): pl.pallas_call(functools.partial(kernel, blocks[0], group), out_shape=[sh...  25.8 us
    all_to_all x1, starting transfers between devices, shards(): packed = lax.all_to_all(packed, ROW, 0, 0, tiled=True)  18 us
    unnamed x24, local copies, waits for them, and re-layouts  9.78 us
    all_to_all x1, waiting for transfers between devices, shards(): packed = lax.all_to_all(packed, ROW, 0, 0, tiled=True)  9.27 us
    pallas_call x10, Pallas kernels, add_entries(): pl.pallas_call(functools.partial(add_kernel, plan, 16), out_shape=[jax.Sh...  4.66 us
  transfers between devices with their start and end apart: 28, of which 12 were waited for; matrix products, arithmetic and copies ran while one was open for 0% of the time, Pallas kernels for 13%

profile of v1, /device:TPU:1, one launch (start us, length us, event | category | flops | bytes accessed | tf_op | source)
XLA Modules:
  0.0 158.9 jit_solution(1050723149550842330)
XLA Ops:
  0.8 3.7 %copy-done = bf16[1024,4608]{1,0:T(8,128)(2,1)S(1)} copy-done((bf16[1024,4608]{1,0:T(8,128)(2,1)S(1)}, bf16[1024,4608]{1,0:T(8,128)(2,1)}, u32[]{:S(2)}) %copy-start) | copy-done | bytes 9437208
  6.0 3.2 %shard_map.127 = (bf16[1,4,144,1024]{3,2,1,0:T(8,128)(2,1)S(1)}, bf16[1,4,144,1024]{3,2,1,0:T(8,128)(2,1)S(1)}) custom-call(s32[17]{0:T(128)S(1)} %stack.71.where_ref, bf16[1024,4608]{1,0:T(8,128)(2,1)S(1)} %copy-done, bf16[1024,1024]{1,0:T(8,128)(2,1)S(1)} %copy-done.3), custom_call_target="tpu_custom_call" | custom-call | flops 2415919104 | bytes 2359296 | tf_op jit(solution)/shard_map/pallas_call | solution.py:89
  10.7 3.4 %copy-done.1 = bf16[1024,4096]{1,0:T(8,128)(2,1)S(1)} copy-done((bf16[1024,4096]{1,0:T(8,128)(2,1)S(1)}, bf16[1024,4096]{1,0:T(8,128)(2,1)}, u32[]{:S(2)}) %copy-start.1) | copy-done | bytes 8388632
  14.1 3.5 %shard_map.129 = (bf16[1,4,128,1152]{3,2,1,0:T(8,128)(2,1)S(1)}, bf16[1,4,128,1152]{3,2,1,0:T(8,128)(2,1)S(1)}) custom-call(s32[17]{0:T(128)S(1)} %stack.71.where_ref, bf16[1024,4096]{1,0:T(8,128)(2,1)S(1)} %copy-done.1, bf16[1024,1152]{1,0:T(8,128)(2,1)S(1)} %copy-done.2), custom_call_target="tpu_custom_call" | custom-call | flops 2415919104 | bytes 2097152 | tf_op jit(solution)/shard_map/pallas_call | solution.py:89
  18.2 2.3 %collective-permute-done.1 = bf16[1,4,128,1152]{3,2,1,0:T(8,128)(2,1)S(1)} collective-permute-done((bf16[1,4,128,1152]{3,2,1,0:T(8,128)(2,1)S(1)}, bf16[1,4,128,1152]{3,2,1,0:T(8,128)(2,1)S(1)}, u32[]{:S(2)}, u32[]{:S(2)}) %collective-permute-start.1) | collective-permute-done | bytes 1179680 | tf_op jit(solution)/shard_map/ppermute | solution.py:23
  22.1 5.9 %shard_map.131 = (bf16[2,4,144,1024]{3,2,1,0:T(8,128)(2,1)S(1)}, bf16[2,4,144,1024]{3,2,1,0:T(8,128)(2,1)S(1)}) custom-call(s32[17]{0:T(128)S(1)} %stack.71.where_ref, bf16[1024,4608]{1,0:T(8,128)(2,1)S(1)} %bitcast.43, bf16[1024,1024]{1,0:T(8,128)(2,1)S(1)} %copy-done.4), custom_call_target="tpu_custom_call" | custom-call | flops 4831838208 | bytes 4718592 | tf_op jit(solution)/shard_map/pallas_call | solution.py:89
  28.5 6.4 %shard_map.133 = (bf16[2,4,128,1152]{3,2,1,0:T(8,128)(2,1)S(1)}, bf16[2,4,128,1152]{3,2,1,0:T(8,128)(2,1)S(1)}) custom-call(s32[17]{0:T(128)S(1)} %stack.71.where_ref, bf16[1024,4096]{1,0:T(8,128)(2,1)S(1)} %copy-done.1, bf16[1024,1152]{1,0:T(8,128)(2,1)S(1)} %copy-done.2), custom_call_target="tpu_custom_call" | custom-call | flops 4831838208 | bytes 4194304 | tf_op jit(solution)/shard_map/pallas_call | solution.py:89
  38.2 3.7 %collective-permute-start.5 = (bf16[2,128,1152]{2,1,0:T(8,128)(2,1)S(1)}, bf16[2,128,1152]{2,1,0:T(8,128)(2,1)S(1)}, u32[]{:S(2)}, u32[]{:S(2)}) collective-permute-start(bf16[2,128,1152]{2,1,0:T(8,128)(2,1)S(1)} %get-tuple-element.66), channel_id=1, source_target_pairs={{0,24},{8,0},{16,8},{24,16},{1,25},{9,1},{17,9},{25,17},{2,26},{10... | collective-permute-start | bytes 1769480 | tf_op jit(solution)/shard_map/ppermute | solution.py:23
  41.9 9.7 %collective-permute-done.9.refs_2_ = bf16[2,144,1024]{2,1,0:T(8,128)(2,1)S(1)} collective-permute-done((bf16[2,144,1024]{2,1,0:T(8,128)(2,1)S(1)}, bf16[2,144,1024]{2,1,0:T(8,128)(2,1)S(1)}, u32[]{:S(2)}, u32[]{:S(2)}) %collective-permute-start.9) | collective-permute-done | bytes 589856 | tf_op jit(solution)/shard_map/ppermute | solution.py:23
  54.9 3.5 %shard_map.135 = (bf16[1,4,128,1152]{3,2,1,0:T(8,128)(2,1)S(1)}, bf16[1,4,128,1152]{3,2,1,0:T(8,128)(2,1)S(1)}) custom-call(s32[17]{0:T(128)S(1)} %stack.71.where_ref, bf16[1024,4096]{1,0:T(8,128)(2,1)S(1)} %copy-done.1, bf16[1024,1152]{1,0:T(8,128)(2,1)S(1)} %copy-done.2), custom_call_target="tpu_custom_call" | custom-call | flops 2415919104 | bytes 2097152 | tf_op jit(solution)/shard_map/pallas_call | solution.py:89
  60.0 7.9 %collective-permute-done.18.refs_2_ = bf16[2,128,1152]{2,1,0:T(8,128)(2,1)S(1)} collective-permute-done((bf16[2,128,1152]{2,1,0:T(8,128)(2,1)S(1)}, bf16[2,128,1152]{2,1,0:T(8,128)(2,1)S(1)}, u32[]{:S(2)}, u32[]{:S(2)}) %collective-permute-start.18) | collective-permute-done | bytes 589856 | tf_op jit(solution)/shard_map/ppermute | solution.py:23
  68.6 2.7 %collective-permute-start.20 = (bf16[2,128,1152]{2,1,0:T(8,128)(2,1)S(1)}, bf16[2,128,1152]{2,1,0:T(8,128)(2,1)S(1)}, u32[]{:S(2)}, u32[]{:S(2)}) collective-permute-start(bf16[2,128,1152]{2,1,0:T(8,128)(2,1)S(1)} %get-tuple-element.84), channel_id=1, source_target_pairs={{0,24},{8,0},{16,8},{24,16},{1,25},{9,1},{17,9},{25,17},{2,26},{10... | collective-permute-start | bytes 1769480 | tf_op jit(solution)/shard_map/ppermute | solution.py:23
  71.3 3.2 %shard_map.136 = (bf16[1,4,144,1024]{3,2,1,0:T(8,128)(2,1)S(1)}, bf16[1,4,144,1024]{3,2,1,0:T(8,128)(2,1)S(1)}) custom-call(s32[17]{0:T(128)S(1)} %stack.71.where_ref, bf16[1024,4608]{1,0:T(8,128)(2,1)S(1)} %bitcast.43, bf16[1024,1024]{1,0:T(8,128)(2,1)S(1)} %copy-done.4), custom_call_target="tpu_custom_call" | custom-call | flops 2415919104 | bytes 2359296 | tf_op jit(solution)/shard_map/pallas_call | solution.py:89
  74.5 2.2 %collective-permute-start.6 = (bf16[1,4,144,1024]{3,2,1,0:T(8,128)(2,1)S(1)}, bf16[1,4,144,1024]{3,2,1,0:T(8,128)(2,1)S(1)}, u32[]{:S(2)}, u32[]{:S(2)}) collective-permute-start(bf16[1,4,144,1024]{3,2,1,0:T(8,128)(2,1)S(1)} %get-tuple-element.72), channel_id=1, source_target_pairs={{0,4},{4,0},{1,5},{5,1},{2,6},{6,2},{3,7},{7,3},{8,12},{12,8},{9,1... | collective-permute-start | bytes 3538952 | tf_op jit(solution)/shard_map/ppermute | solution.py:23
  76.9 6.2 %collective-permute-done.19.refs_2_ = bf16[2,128,1152]{2,1,0:T(8,128)(2,1)S(1)} collective-permute-done((bf16[2,128,1152]{2,1,0:T(8,128)(2,1)S(1)}, bf16[2,128,1152]{2,1,0:T(8,128)(2,1)S(1)}, u32[]{:S(2)}, u32[]{:S(2)}) %collective-permute-start.19) | collective-permute-done | bytes 589856 | tf_op jit(solution)/shard_map/ppermute | solution.py:23
  84.5 10.3 %collective-permute-done.17.refs_3_ = bf16[2,128,1152]{2,1,0:T(8,128)(2,1)S(1)} collective-permute-done((bf16[2,128,1152]{2,1,0:T(8,128)(2,1)S(1)}, bf16[2,128,1152]{2,1,0:T(8,128)(2,1)S(1)}, u32[]{:S(2)}, u32[]{:S(2)}) %collective-permute-start.17) | collective-permute-done | bytes 589856 | tf_op jit(solution)/shard_map/ppermute | solution.py:23
  101.9 7.1 %collective-permute-done.8.refs_3_ = bf16[2,144,1024]{2,1,0:T(8,128)(2,1)S(1)} collective-permute-done((bf16[2,144,1024]{2,1,0:T(8,128)(2,1)S(1)}, bf16[2,144,1024]{2,1,0:T(8,128)(2,1)S(1)}, u32[]{:S(2)}, u32[]{:S(2)}) %collective-permute-start.8) | collective-permute-done | bytes 589856 | tf_op jit(solution)/shard_map/ppermute | solution.py:23
  112.0 2.3 %collective-permute-done.21 = bf16[1,128,1152]{2,1,0:T(8,128)(2,1)S(1)} collective-permute-done((bf16[1,128,1152]{2,1,0:T(8,128)(2,1)S(1)}, bf16[1,128,1152]{2,1,0:T(8,128)(2,1)S(1)}, u32[]{:S(2)}, u32[]{:S(2)}) %collective-permute-start.21) | collective-permute-done | bytes 294944 | tf_op jit(solution)/shard_map/ppermute | solution.py:23
  114.3 3.4 %collective-permute-start.14 = (bf16[1,144,1024]{2,1,0:T(8,128)(2,1)S(1)}, bf16[1,144,1024]{2,1,0:T(8,128)(2,1)S(1)}, u32[]{:S(2)}, u32[]{:S(2)}) collective-permute-start(bf16[1,144,1024]{2,1,0:T(8,128)(2,1)S(1)} %get-tuple-element.79), channel_id=1, source_target_pairs={{0,24},{8,0},{16,8},{24,16},{1,25},{9,1},{17,9},{25,17},{2,26},{10... | collective-permute-start | bytes 884744 | tf_op jit(solution)/shard_map/ppermute | solution.py:23
  117.7 4.2 %collective-permute-done.22 = bf16[1,128,1152]{2,1,0:T(8,128)(2,1)S(1)} collective-permute-done((bf16[1,128,1152]{2,1,0:T(8,128)(2,1)S(1)}, bf16[1,128,1152]{2,1,0:T(8,128)(2,1)S(1)}, u32[]{:S(2)}, u32[]{:S(2)}) %collective-permute-start.22) | collective-permute-done | bytes 294944 | tf_op jit(solution)/shard_map/ppermute | solution.py:23
  122.6 2.5 %collective-permute-start.26 = (f32[1,384]{1,0:T(1,128)S(1)}, f32[1,384]{1,0:T(1,128)S(1)}, u32[]{:S(2)}, u32[]{:S(2)}) collective-permute-start(f32[1,384]{1,0:T(1,128)S(1)} %reshape.107.refs_0_), channel_id=1, source_target_pairs={{0,3},{1,0},{2,1},{3,2},{4,7},{5,4},{6,5},{7,6},{8,11},{9,8},{10,9... | collective-permute-start | bytes 4616 | tf_op jit(solution)/shard_map/ppermute | solution.py:23
  126.9 2.2 %collective-permute-done.25.refs_2_ = f32[1,384]{1,0:T(1,128)S(1)} collective-permute-done((f32[1,384]{1,0:T(1,128)S(1)}, f32[1,384]{1,0:T(1,128)S(1)}, u32[]{:S(2)}, u32[]{:S(2)}) %collective-permute-start.25) | collective-permute-done | bytes 1568 | tf_op jit(solution)/shard_map/ppermute | solution.py:23
  129.9 18.0 %all-to-all-start = ((f32[32,1,2304]{2,1,0:T(1,128)}), f32[32,1,2304]{2,1,0:T(1,128)S(1)}, u32[]{:S(2)}, u32[]{:S(2)}) async-start(f32[32,1,2304]{2,1,0:T(1,128)} %get-tuple-element.88), calls=%async_computation | async-start | bytes 589824 | tf_op jit(solution)/shard_map/all_to_all | solution.py:330
  147.9 9.3 %all-to-all-done.sums_ref = f32[32,1,2304]{2,1,0:T(1,128)S(1)} async-done(((f32[32,1,2304]{2,1,0:T(1,128)}), f32[32,1,2304]{2,1,0:T(1,128)S(1)}, u32[]{:S(2)}, u32[]{:S(2)}) %all-to-all-start) | async-done | bytes 294944 | tf_op jit(solution)/shard_map/all_to_all | solution.py:330
  (84 shorter events, 31.1 us)
Async XLA Ops:
  9.3 8.5 %collective-permute-start = (bf16[1,4,144,1024]{3,2,1,0:T(8,128)(2,1)S(1)}, bf16[1,4,144,1024]{3,2,1,0:T(8,128)(2,1)S(1)}, u32[]{:S(2)}, u32[]{:S(2)}) collective-permute-start(bf16[1,4,144,1024]{3,2,1,0:T(8,128)(2,1)S(1)} %get-tuple-element.52), channel_id=1, source_target_pairs={{0,4},{4,0},{1,5},{5,1},{2,6},{6,2},{3,7},{7,3},{8,12},{12,8},{9,1... | collective-permute-start | bytes 3538952 | tf_op jit(solution)/shard_map/ppermute | solution.py:23
  28.1 25.1 %collective-permute-start.2 = (bf16[2,4,144,1024]{3,2,1,0:T(8,128)(2,1)S(1)}, bf16[2,4,144,1024]{3,2,1,0:T(8,128)(2,1)S(1)}, u32[]{:S(2)}, u32[]{:S(2)}) collective-permute-start(bf16[2,4,144,1024]{3,2,1,0:T(8,128)(2,1)S(1)} %get-tuple-element.60), channel_id=1, source_target_pairs={{0,4},{4,0},{1,5},{5,1},{2,6},{6,2},{3,7},{7,3},{8,12},{12,8},{9,1... | collective-permute-start | bytes 7077896 | tf_op jit(solution)/shard_map/ppermute | solution.py:23
  34.9 19.4 %collective-permute-start.4 = (bf16[2,4,128,1152]{3,2,1,0:T(8,128)(2,1)S(1)}, bf16[2,4,128,1152]{3,2,1,0:T(8,128)(2,1)S(1)}, u32[]{:S(2)}, u32[]{:S(2)}) collective-permute-start(bf16[2,4,128,1152]{3,2,1,0:T(8,128)(2,1)S(1)} %get-tuple-element.65), channel_id=1, source_target_pairs={{0,4},{4,0},{1,5},{5,1},{2,6},{6,2},{3,7},{7,3},{8,12},{12,8},{9,1... | collective-permute-start | bytes 7077896 | tf_op jit(solution)/shard_map/ppermute | solution.py:23
  35.4 16.3 %collective-permute-start.9 = (bf16[2,144,1024]{2,1,0:T(8,128)(2,1)S(1)}, bf16[2,144,1024]{2,1,0:T(8,128)(2,1)S(1)}, u32[]{:S(2)}, u32[]{:S(2)}) collective-permute-start(bf16[2,144,1024]{2,1,0:T(8,128)(2,1)S(1)} %get-tuple-element.53), channel_id=1, source_target_pairs={{0,32},{32,64},{64,96},{96,0},{1,33},{33,65},{65,97},{97,1},{2,34}... | collective-permute-start | bytes 1769480 | tf_op jit(solution)/shard_map/ppermute | solution.py:23
  36.8 17.0 %collective-permute-start.3 = (bf16[2,144,1024]{2,1,0:T(8,128)(2,1)S(1)}, bf16[2,144,1024]{2,1,0:T(8,128)(2,1)S(1)}, u32[]{:S(2)}, u32[]{:S(2)}) collective-permute-start(bf16[2,144,1024]{2,1,0:T(8,128)(2,1)S(1)} %get-tuple-element.61), channel_id=1, source_target_pairs={{0,96},{32,0},{64,32},{96,64},{1,97},{33,1},{65,33},{97,65},{2,98}... | collective-permute-start | bytes 1769480 | tf_op jit(solution)/shard_map/ppermute | solution.py:23
  38.2 16.1 %collective-permute-start.5 = (bf16[2,128,1152]{2,1,0:T(8,128)(2,1)S(1)}, bf16[2,128,1152]{2,1,0:T(8,128)(2,1)S(1)}, u32[]{:S(2)}, u32[]{:S(2)}) collective-permute-start(bf16[2,128,1152]{2,1,0:T(8,128)(2,1)S(1)} %get-tuple-element.66), channel_id=1, source_target_pairs={{0,24},{8,0},{16,8},{24,16},{1,25},{9,1},{17,9},{25,17},{2,26},{10... | collective-permute-start | bytes 1769480 | tf_op jit(solution)/shard_map/ppermute | solution.py:23
  51.6 16.4 %collective-permute-start.18 = (bf16[2,128,1152]{2,1,0:T(8,128)(2,1)S(1)}, bf16[2,128,1152]{2,1,0:T(8,128)(2,1)S(1)}, u32[]{:S(2)}, u32[]{:S(2)}) collective-permute-start(bf16[2,128,1152]{2,1,0:T(8,128)(2,1)S(1)} %get-tuple-element.57), channel_id=1, source_target_pairs={{0,8},{8,16},{16,24},{24,0},{1,9},{9,17},{17,25},{25,1},{2,10},{10... | collective-permute-start | bytes 1769480 | tf_op jit(solution)/shard_map/ppermute | solution.py:23
  53.7 23.0 %collective-permute-start.10 = (bf16[2,144,1024]{2,1,0:T(8,128)(2,1)S(1)}, bf16[2,144,1024]{2,1,0:T(8,128)(2,1)S(1)}, u32[]{:S(2)}, u32[]{:S(2)}) collective-permute-start(bf16[2,144,1024]{2,1,0:T(8,128)(2,1)S(1)} %get-tuple-element.75), channel_id=1, source_target_pairs={{0,32},{32,64},{64,96},{96,0},{1,33},{33,65},{65,97},{97,1},{2,34}... | collective-permute-start | bytes 1769480 | tf_op jit(solution)/shard_map/ppermute | solution.py:23
  58.4 37.7 %collective-permute-start.15 = (bf16[1,4,128,1152]{3,2,1,0:T(8,128)(2,1)S(1)}, bf16[1,4,128,1152]{3,2,1,0:T(8,128)(2,1)S(1)}, u32[]{:S(2)}, u32[]{:S(2)}) collective-permute-start(bf16[1,4,128,1152]{3,2,1,0:T(8,128)(2,1)S(1)} %get-tuple-element.80), channel_id=1, source_target_pairs={{0,4},{4,0},{1,5},{5,1},{2,6},{6,2},{3,7},{7,3},{8,12},{12,8},{9,1... | collective-permute-start | bytes 3538952 | tf_op jit(solution)/shard_map/ppermute | solution.py:23
  68.5 14.6 %collective-permute-start.19 = (bf16[2,128,1152]{2,1,0:T(8,128)(2,1)S(1)}, bf16[2,128,1152]{2,1,0:T(8,128)(2,1)S(1)}, u32[]{:S(2)}, u32[]{:S(2)}) collective-permute-start(bf16[2,128,1152]{2,1,0:T(8,128)(2,1)S(1)} %get-tuple-element.83), channel_id=1, source_target_pairs={{0,8},{8,16},{16,24},{24,0},{1,9},{9,17},{17,25},{25,1},{2,10},{10... | collective-permute-start | bytes 1769480 | tf_op jit(solution)/shard_map/ppermute | solution.py:23
  68.6 14.6 %collective-permute-start.20 = (bf16[2,128,1152]{2,1,0:T(8,128)(2,1)S(1)}, bf16[2,128,1152]{2,1,0:T(8,128)(2,1)S(1)}, u32[]{:S(2)}, u32[]{:S(2)}) collective-permute-start(bf16[2,128,1152]{2,1,0:T(8,128)(2,1)S(1)} %get-tuple-element.84), channel_id=1, source_target_pairs={{0,24},{8,0},{16,8},{24,16},{1,25},{9,1},{17,9},{25,17},{2,26},{10... | collective-permute-start | bytes 1769480 | tf_op jit(solution)/shard_map/ppermute | solution.py:23
  74.5 25.9 %collective-permute-start.6 = (bf16[1,4,144,1024]{3,2,1,0:T(8,128)(2,1)S(1)}, bf16[1,4,144,1024]{3,2,1,0:T(8,128)(2,1)S(1)}, u32[]{:S(2)}, u32[]{:S(2)}) collective-permute-start(bf16[1,4,144,1024]{3,2,1,0:T(8,128)(2,1)S(1)} %get-tuple-element.72), channel_id=1, source_target_pairs={{0,4},{4,0},{1,5},{5,1},{2,6},{6,2},{3,7},{7,3},{8,12},{12,8},{9,1... | collective-permute-start | bytes 3538952 | tf_op jit(solution)/shard_map/ppermute | solution.py:23
  76.7 18.1 %collective-permute-start.17 = (bf16[2,128,1152]{2,1,0:T(8,128)(2,1)S(1)}, bf16[2,128,1152]{2,1,0:T(8,128)(2,1)S(1)}, u32[]{:S(2)}, u32[]{:S(2)}) collective-permute-start(bf16[2,128,1152]{2,1,0:T(8,128)(2,1)S(1)} %get-tuple-element.81), channel_id=1, source_target_pairs={{0,24},{8,0},{16,8},{24,16},{1,25},{9,1},{17,9},{25,17},{2,26},{10... | collective-permute-start | bytes 1769480 | tf_op jit(solution)/shard_map/ppermute | solution.py:23
  83.2 13.7 %collective-permute-start.16 = (bf16[2,128,1152]{2,1,0:T(8,128)(2,1)S(1)}, bf16[2,128,1152]{2,1,0:T(8,128)(2,1)S(1)}, u32[]{:S(2)}, u32[]{:S(2)}) collective-permute-start(bf16[2,128,1152]{2,1,0:T(8,128)(2,1)S(1)} %get-tuple-element.67), channel_id=1, source_target_pairs={{0,8},{8,16},{16,24},{24,0},{1,9},{9,17},{17,25},{25,1},{2,10},{10... | collective-permute-start | bytes 1769480 | tf_op jit(solution)/shard_map/ppermute | solution.py:23
  83.2 15.6 %collective-permute-start.11 = (bf16[2,144,1024]{2,1,0:T(8,128)(2,1)S(1)}, bf16[2,144,1024]{2,1,0:T(8,128)(2,1)S(1)}, u32[]{:S(2)}, u32[]{:S(2)}) collective-permute-start(bf16[2,144,1024]{2,1,0:T(8,128)(2,1)S(1)} %get-tuple-element.76), channel_id=1, source_target_pairs={{0,96},{32,0},{64,32},{96,64},{1,97},{33,1},{65,33},{97,65},{2,98}... | collective-permute-start | bytes 1769480 | tf_op jit(solution)/shard_map/ppermute | solution.py:23
  94.8 14.3 %collective-permute-start.8 = (bf16[2,144,1024]{2,1,0:T(8,128)(2,1)S(1)}, bf16[2,144,1024]{2,1,0:T(8,128)(2,1)S(1)}, u32[]{:S(2)}, u32[]{:S(2)}) collective-permute-start(bf16[2,144,1024]{2,1,0:T(8,128)(2,1)S(1)} %get-tuple-element.73), channel_id=1, source_target_pairs={{0,96},{32,0},{64,32},{96,64},{1,97},{33,1},{65,33},{97,65},{2,98}... | collective-permute-start | bytes 1769480 | tf_op jit(solution)/shard_map/ppermute | solution.py:23
  96.1 14.1 %collective-permute-start.7 = (bf16[2,144,1024]{2,1,0:T(8,128)(2,1)S(1)}, bf16[2,144,1024]{2,1,0:T(8,128)(2,1)S(1)}, u32[]{:S(2)}, u32[]{:S(2)}) collective-permute-start(bf16[2,144,1024]{2,1,0:T(8,128)(2,1)S(1)} %get-tuple-element.62), channel_id=1, source_target_pairs={{0,32},{32,64},{64,96},{96,0},{1,33},{33,65},{65,97},{97,1},{2,34}... | collective-permute-start | bytes 1769480 | tf_op jit(solution)/shard_map/ppermute | solution.py:23
  96.9 17.4 %collective-permute-start.21 = (bf16[1,128,1152]{2,1,0:T(8,128)(2,1)S(1)}, bf16[1,128,1152]{2,1,0:T(8,128)(2,1)S(1)}, u32[]{:S(2)}, u32[]{:S(2)}) collective-permute-start(bf16[1,128,1152]{2,1,0:T(8,128)(2,1)S(1)} %get-tuple-element.85), channel_id=1, source_target_pairs={{0,64},{32,96},{64,0},{96,32},{1,65},{33,97},{65,1},{97,33},{2,66}... | collective-permute-start | bytes 884744 | tf_op jit(solution)/shard_map/ppermute | solution.py:23
  98.8 23.1 %collective-permute-start.22 = (bf16[1,128,1152]{2,1,0:T(8,128)(2,1)S(1)}, bf16[1,128,1152]{2,1,0:T(8,128)(2,1)S(1)}, u32[]{:S(2)}, u32[]{:S(2)}) collective-permute-start(bf16[1,128,1152]{2,1,0:T(8,128)(2,1)S(1)} %get-tuple-element.86), channel_id=1, source_target_pairs={{0,32},{32,64},{64,96},{96,0},{1,33},{33,65},{65,97},{97,1},{2,34}... | collective-permute-start | bytes 884744 | tf_op jit(solution)/shard_map/ppermute | solution.py:23
  100.4 21.5 %collective-permute-start.23 = (bf16[1,128,1152]{2,1,0:T(8,128)(2,1)S(1)}, bf16[1,128,1152]{2,1,0:T(8,128)(2,1)S(1)}, u32[]{:S(2)}, u32[]{:S(2)}) collective-permute-start(bf16[1,128,1152]{2,1,0:T(8,128)(2,1)S(1)} %get-tuple-element.87), channel_id=1, source_target_pairs={{0,96},{32,0},{64,32},{96,64},{1,97},{33,1},{65,33},{97,65},{2,98}... | collective-permute-start | bytes 884744 | tf_op jit(solution)/shard_map/ppermute | solution.py:23
  109.1 13.1 %collective-permute-start.12 = (bf16[1,144,1024]{2,1,0:T(8,128)(2,1)S(1)}, bf16[1,144,1024]{2,1,0:T(8,128)(2,1)S(1)}, u32[]{:S(2)}, u32[]{:S(2)}) collective-permute-start(bf16[1,144,1024]{2,1,0:T(8,128)(2,1)S(1)} %get-tuple-element.77), channel_id=1, source_target_pairs={{0,16},{8,24},{16,0},{24,8},{1,17},{9,25},{17,1},{25,9},{2,18},{10... | collective-permute-start | bytes 884744 | tf_op jit(solution)/shard_map/ppermute | solution.py:23
  110.3 11.9 %collective-permute-start.13 = (bf16[1,144,1024]{2,1,0:T(8,128)(2,1)S(1)}, bf16[1,144,1024]{2,1,0:T(8,128)(2,1)S(1)}, u32[]{:S(2)}, u32[]{:S(2)}) collective-permute-start(bf16[1,144,1024]{2,1,0:T(8,128)(2,1)S(1)} %get-tuple-element.78), channel_id=1, source_target_pairs={{0,8},{8,16},{16,24},{24,0},{1,9},{9,17},{17,25},{25,1},{2,10},{10... | collective-permute-start | bytes 884744 | tf_op jit(solution)/shard_map/ppermute | solution.py:23
  114.3 7.9 %collective-permute-start.14 = (bf16[1,144,1024]{2,1,0:T(8,128)(2,1)S(1)}, bf16[1,144,1024]{2,1,0:T(8,128)(2,1)S(1)}, u32[]{:S(2)}, u32[]{:S(2)}) collective-permute-start(bf16[1,144,1024]{2,1,0:T(8,128)(2,1)S(1)} %get-tuple-element.79), channel_id=1, source_target_pairs={{0,24},{8,0},{16,8},{24,16},{1,25},{9,1},{17,9},{25,17},{2,26},{10... | collective-permute-start | bytes 884744 | tf_op jit(solution)/shard_map/ppermute | solution.py:23
  129.9 27.3 %all-to-all-start = ((f32[32,1,2304]{2,1,0:T(1,128)}), f32[32,1,2304]{2,1,0:T(1,128)S(1)}, u32[]{:S(2)}, u32[]{:S(2)}) async-start(f32[32,1,2304]{2,1,0:T(1,128)} %get-tuple-element.88), calls=%async_computation | async-start | bytes 589824 | tf_op jit(solution)/shard_map/all_to_all | solution.py:330
  (16 other events, 127.7 us)

commit v2 on v1

--- a/solution.py
+++ b/solution.py
@@ -147,25 +147,57 @@
     return jnp.sum(square, axis=1), jnp.sum(square, axis=0)
 
 
-def pack_kernel(split, *refs):
-    rows_refs, (query_cols, output_cols, query_old, output_old, rows_ref, packed_ref) = refs[:4], refs[4:]
-    total = rows_refs[0][...] + rows_refs[1][...] + rows_refs[2][...] + rows_refs[3][...]
-    rows_ref[...] = total
+def halves_kernel(split, where_ref, rows, query_cols, output_cols, query_old, output_old, keep_ref, give_ref):
+    core = where_ref[0]
+    width = keep_ref.shape[1] - 128
     lane = lax.broadcasted_iota(jnp.int32, (1, 128), 1)
     scalars = jnp.zeros((1, 128), jnp.float32)
-    parts = (total[:, :split], total[:, split:], query_old[...], output_old[...])
+    parts = (rows[:, :split], rows[:, split:], query_old[...], output_old[...])
     for i, part in enumerate(parts):
         scalars = jnp.where(lane == i, jnp.sum(part, axis=1, keepdims=True), scalars)
-    row = jnp.concatenate([query_cols[...], output_cols[...], scalars], axis=1)
+    columns = query_cols.shape[1] + output_cols.shape[1]
+    pad = jnp.zeros((1, 2 * width - columns), jnp.float32)
+    whole = jnp.concatenate([query_cols[...], output_cols[...], pad], axis=1)
+    low, high = whole[:, :width], whole[:, width:]
+    keep_ref[...] = jnp.concatenate([jnp.where(core == 0, low, high), scalars], axis=1)
+    give_ref[...] = jnp.concatenate([jnp.where(core == 0, high, low), scalars], axis=1)
+
+
+def pack_kernel(keep, got, rows, packed_ref):
+    total = keep[...] + got[...]
+    width = total.shape[1] - 128
+    row = jnp.concatenate([total[:, :width], rows[...], total[:, width:]], axis=1)
     for i in range(packed_ref.shape[0]):
         packed_ref[i] = row
+
+
+def unpack_kernel(where_ref, packed, half_ref, rows_ref, scalars_ref):
+    place, column = where_ref[17], where_ref[18]
+    width, length = half_ref.shape[1], rows_ref.shape[1]
+    peers = packed.shape[0] // 4
+    mine = packed[column]
+    for p in range(1, peers):
+        mine = mine + packed[4 * p + column]
+    rows = packed[4 * place]
+    for j in range(1, 4):
+        rows = rows + packed[4 * place + j]
+    everyone = packed[0, :, width + length :]
+    for p in range(1, 4 * peers):
+        everyone = everyone + packed[p, :, width + length :]
+    lane = lax.broadcasted_iota(jnp.int32, (1, 128), 1)
+    half_ref[...] = mine[:, :width]
+    rows_ref[...] = rows[:, width : width + length]
+    scalars_ref[...] = jnp.where(lane < 2, everyone, mine[:, width + length :])
 
 
 def finish_kernel(
     split,
     across,
     along,
-    sums_ref,
+    where_ref,
+    half_ref,
+    other_ref,
+    scalars_ref,
     rows_ref,
     query_row,
     query_col,
@@ -180,12 +212,13 @@
     output_row_new,
     output_col_new,
 ):
-    sums = sums_ref[0]
-    for i in range(1, sums_ref.shape[0]):
-        sums = sums + sums_ref[i]
-    query_width, output_width = query_col.shape[1], output_col.shape[1]
+    core = where_ref[0]
+    half, other = half_ref[...], other_ref[...]
+    first, second = jnp.where(core == 0, half, other), jnp.where(core == 0, other, half)
+    sums = jnp.concatenate([first, second], axis=1)
+    query_width = query_col.shape[1]
     lane = lax.broadcasted_iota(jnp.int32, (1, 128), 1)
-    tail = sums[:, query_width + output_width :]
+    tail = scalars_ref[...]
     query_squares, output_squares, query_old, output_old = (
         jnp.sum(jnp.where(lane == i, tail, 0.0), axis=1, keepdims=True) for i in range(4)
     )
@@ -224,15 +257,16 @@
     )
 
 
-def small_call(kernel, outs, *inputs):
+def small_call(kernel, outs, *inputs, where=None):
+    places = [] if where is None else [pl.BlockSpec(memory_space=pltpu.SMEM)]
     return pl.pallas_call(
         kernel,
         out_shape=[jax.ShapeDtypeStruct(shape, dtype) for shape, dtype in outs],
-        in_specs=[pl.BlockSpec(memory_space=pltpu.VMEM)] * len(inputs),
+        in_specs=places + [pl.BlockSpec(memory_space=pltpu.VMEM)] * len(inputs),
         out_specs=[pl.BlockSpec(memory_space=pltpu.VMEM)] * len(outs),
         compiler_params=pltpu.CompilerParams(vmem_limit_bytes=12 * 2**20),
         cost_estimate=pl.CostEstimate(flops=600_000_000, bytes_accessed=0, transcendentals=0),
-    )(*inputs)
+    )(*([] if where is None else [where]), *inputs)
 
 
 def shards(acts_in, grad_query, attn_out, grad_out, row_query, col_query, row_output, col_output):
@@ -248,6 +282,7 @@
         + [lax.rem(z + k, 4) * pair_output for k in range(4)]
         + [lax.rem(k + 4 - z, 4) for k in range(4)]
         + [lax.rem(y + k, 4) for k in range(4)]
+        + [4 * y + z, lax.axis_index(X)]
     ).astype(jnp.int32)
 
     def made(kernel, where, left, right, ks, group, vmem):
@@ -318,16 +353,26 @@
             [query_rowsum, jnp.zeros((split - query_rows,), jnp.float32), output_rowsum]
         )
     )
-    others = [shift(rows, X, k) for k in (2, 1, 3)]
-    width = query_width + output_width + 128
-    rows, packed = small_call(
-        functools.partial(pack_kernel, split),
-        [(rows.shape, jnp.float32), ((lax.axis_size(ROW), 1, width), jnp.float32)],
-        rows,
-        *others,
-        *(line(v) for v in (query_colsum, output_colsum, row_query, row_output)),
-    )
-    packed = lax.all_to_all(packed, ROW, 0, 0, tiled=True)
+    width = -(-(query_width + output_width) // 256) * 128
+    packet = ((1, width + 128), jnp.float32)
+    sums = [line(v) for v in (query_colsum, output_colsum, row_query, row_output)]
+    keep, give = small_call(
+        functools.partial(halves_kernel, split), [packet, packet], rows, *sums, where=where
+    )
+    got = shift(give, CORE, 1)
+    peers = (Y, Z, X)
+    count = lax.axis_size(peers)
+    (packed,) = small_call(
+        pack_kernel, [((count, 1, width + 128 + rows.shape[1]), jnp.float32)], keep, got, rows
+    )
+    packed = lax.all_to_all(packed, peers, 0, 0, tiled=True)
+    half, rows, scalars = small_call(
+        unpack_kernel,
+        [((1, width), jnp.float32), (rows.shape, jnp.float32), ((1, 128), jnp.float32)],
+        packed,
+        where=where,
+    )
+    other = shift(half, CORE, 1)
     olds = [line(v) for v in (row_query, col_query, row_output, col_output)]
     update_query, new_row_query, new_col_query, update_output, new_row_output, new_col_output = small_call(
         functools.partial(finish_kernel, split, lax.axis_size(X), lax.axis_size(ROW)),
@@ -339,11 +384,14 @@
             (olds[2].shape, jnp.float32),
             (olds[3].shape, jnp.float32),
         ],
-        packed,
+        half,
+        other,
+        scalars,
         rows,
         *olds,
         query_grad,
         output_grad,
+        where=where,
     )
     return (
         update_query,

time: 159 us -> 161 us (1.013)
  blocking collectives: 0 us -> 21.8 us
  starting transfers between devices: 51.4 us -> 40 us
  waiting for transfers between devices: 63.1 us -> 53.3 us
    all_to_all x0 -> x1, blocking collectives: none -> 21.8 us  [shards(): packed = lax.all_to_all(packed, peers, 0, 0, tiled=True)]
    all_to_all x1 -> x0, starting transfers between devices: 18 us -> none  [shards(): packed = lax.all_to_all(packed, ROW, 0, 0, tiled=True)]
    all_to_all x1 -> x0, waiting for transfers between devices: 9.27 us -> none  [shards(): packed = lax.all_to_all(packed, ROW, 0, 0, tiled=True)]
    ppermute x27 -> x26, starting transfers between devices: 33.4 us -> 40 us  [shift(): lax.ppermute(value, axis, [(i, (i + by) % size) for i in range(size)])]
    ppermute x27 -> x26, waiting for transfers between devices: 53.8 us -> 53.3 us  [shift(): lax.ppermute(value, axis, [(i, (i + by) % size) for i in range(size)])]
  transfers between devices with their start and end apart: 28 -> 26, of which waited for: 12 -> 12; matrix products, arithmetic and copies ran while one was open for 0% -> 0% of each run, Pallas kernels for 13% -> 13%
where the time goes in v2:
time: 161 us
  waiting for transfers between devices  53.3 us (33%)
  starting transfers between devices  40 us (25%)
  Pallas kernels  33.3 us (21%)
  blocking collectives  21.8 us (14%)
  local copies, waits for them, and re-layouts  10.1 us (6%)
    ppermute x26, waiting for transfers between devices, shift(): lax.ppermute(value, axis, [(i, (i + by) % size) for i in range(size)])  53.3 us
    ppermute x26, starting transfers between devices, shift(): lax.ppermute(value, axis, [(i, (i + by) % size) for i in range(size)])  40 us
    pallas_call x6, Pallas kernels, partial_blocks(): pl.pallas_call(functools.partial(kernel, blocks[0], group), out_shape=[sh...  25.8 us
    all_to_all x1, blocking collectives, shards(): packed = lax.all_to_all(packed, peers, 0, 0, tiled=True)  21.8 us
    unnamed x24, local copies, waits for them, and re-layouts  10 us
    pallas_call x10, Pallas kernels, add_entries(): pl.pallas_call(functools.partial(add_kernel, plan, 16), out_shape=[jax.Sh...  4.67 us
  transfers between devices with their start and end apart: 26, of which 12 were waited for; matrix products, arithmetic and copies ran while one was open for 0% of the time, Pallas kernels for 13%

profile of v2, /device:TPU:1, one launch (start us, length us, event | category | flops | bytes accessed | tf_op | source)
XLA Modules:
  0.0 160.7 jit_solution(13599700507235859220)
XLA Ops:
  0.8 3.7 %copy-done = bf16[1024,4608]{1,0:T(8,128)(2,1)S(1)} copy-done((bf16[1024,4608]{1,0:T(8,128)(2,1)S(1)}, bf16[1024,4608]{1,0:T(8,128)(2,1)}, u32[]{:S(2)}) %copy-start) | copy-done | bytes 9437208
  6.0 3.2 %shard_map.127 = (bf16[1,4,144,1024]{3,2,1,0:T(8,128)(2,1)S(1)}, bf16[1,4,144,1024]{3,2,1,0:T(8,128)(2,1)S(1)}) custom-call(s32[19]{0:T(128)S(1)} %stack.79.where_ref, bf16[1024,4608]{1,0:T(8,128)(2,1)S(1)} %copy-done, bf16[1024,1024]{1,0:T(8,128)(2,1)S(1)} %copy-done.3), custom_call_target="tpu_custom_call" | custom-call | flops 2415919104 | bytes 2359296 | tf_op jit(solution)/shard_map/pallas_call | solution.py:89
  10.7 3.4 %copy-done.1 = bf16[1024,4096]{1,0:T(8,128)(2,1)S(1)} copy-done((bf16[1024,4096]{1,0:T(8,128)(2,1)S(1)}, bf16[1024,4096]{1,0:T(8,128)(2,1)}, u32[]{:S(2)}) %copy-start.1) | copy-done | bytes 8388632
  14.1 3.5 %shard_map.129 = (bf16[1,4,128,1152]{3,2,1,0:T(8,128)(2,1)S(1)}, bf16[1,4,128,1152]{3,2,1,0:T(8,128)(2,1)S(1)}) custom-call(s32[19]{0:T(128)S(1)} %stack.79.where_ref, bf16[1024,4096]{1,0:T(8,128)(2,1)S(1)} %copy-done.1, bf16[1024,1152]{1,0:T(8,128)(2,1)S(1)} %copy-done.2), custom_call_target="tpu_custom_call" | custom-call | flops 2415919104 | bytes 2097152 | tf_op jit(solution)/shard_map/pallas_call | solution.py:89
  18.2 2.3 %collective-permute-done.1 = bf16[1,4,128,1152]{3,2,1,0:T(8,128)(2,1)S(1)} collective-permute-done((bf16[1,4,128,1152]{3,2,1,0:T(8,128)(2,1)S(1)}, bf16[1,4,128,1152]{3,2,1,0:T(8,128)(2,1)S(1)}, u32[]{:S(2)}, u32[]{:S(2)}) %collective-permute-start.1) | collective-permute-done | bytes 1179680 | tf_op jit(solution)/shard_map/ppermute | solution.py:23
  22.1 5.9 %shard_map.131 = (bf16[2,4,144,1024]{3,2,1,0:T(8,128)(2,1)S(1)}, bf16[2,4,144,1024]{3,2,1,0:T(8,128)(2,1)S(1)}) custom-call(s32[19]{0:T(128)S(1)} %stack.79.where_ref, bf16[1024,4608]{1,0:T(8,128)(2,1)S(1)} %bitcast.45, bf16[1024,1024]{1,0:T(8,128)(2,1)S(1)} %copy-done.4), custom_call_target="tpu_custom_call" | custom-call | flops 4831838208 | bytes 4718592 | tf_op jit(solution)/shard_map/pallas_call | solution.py:89
  28.5 6.5 %shard_map.133 = (bf16[2,4,128,1152]{3,2,1,0:T(8,128)(2,1)S(1)}, bf16[2,4,128,1152]{3,2,1,0:T(8,128)(2,1)S(1)}) custom-call(s32[19]{0:T(128)S(1)} %stack.79.where_ref, bf16[1024,4096]{1,0:T(8,128)(2,1)S(1)} %copy-done.1, bf16[1024,1152]{1,0:T(8,128)(2,1)S(1)} %copy-done.2), custom_call_target="tpu_custom_call" | custom-call | flops 4831838208 | bytes 4194304 | tf_op jit(solution)/shard_map/pallas_call | solution.py:89
  38.2 3.8 %collective-permute-start.5 = (bf16[2,128,1152]{2,1,0:T(8,128)(2,1)S(1)}, bf16[2,128,1152]{2,1,0:T(8,128)(2,1)S(1)}, u32[]{:S(2)}, u32[]{:S(2)}) collective-permute-start(bf16[2,128,1152]{2,1,0:T(8,128)(2,1)S(1)} %get-tuple-element.69), channel_id=1, source_target_pairs={{0,24},{8,0},{16,8},{24,16},{1,25},{9,1},{17,9},{25,17},{2,26},{10... | collective-permute-start | bytes 1769480 | tf_op jit(solution)/shard_map/ppermute | solution.py:23
  41.9 9.7 %collective-permute-done.9.refs_2_ = bf16[2,144,1024]{2,1,0:T(8,128)(2,1)S(1)} collective-permute-done((bf16[2,144,1024]{2,1,0:T(8,128)(2,1)S(1)}, bf16[2,144,1024]{2,1,0:T(8,128)(2,1)S(1)}, u32[]{:S(2)}, u32[]{:S(2)}) %collective-permute-start.9) | collective-permute-done | bytes 589856 | tf_op jit(solution)/shard_map/ppermute | solution.py:23
  54.9 3.5 %shard_map.135 = (bf16[1,4,128,1152]{3,2,1,0:T(8,128)(2,1)S(1)}, bf16[1,4,128,1152]{3,2,1,0:T(8,128)(2,1)S(1)}) custom-call(s32[19]{0:T(128)S(1)} %stack.79.where_ref, bf16[1024,4096]{1,0:T(8,128)(2,1)S(1)} %copy-done.1, bf16[1024,1152]{1,0:T(8,128)(2,1)S(1)} %copy-done.2), custom_call_target="tpu_custom_call" | custom-call | flops 2415919104 | bytes 2097152 | tf_op jit(solution)/shard_map/pallas_call | solution.py:89
  58.4 1.6 %collective-permute-start.15 = (bf16[1,4,128,1152]{3,2,1,0:T(8,128)(2,1)S(1)}, bf16[1,4,128,1152]{3,2,1,0:T(8,128)(2,1)S(1)}, u32[]{:S(2)}, u32[]{:S(2)}) collective-permute-start(bf16[1,4,128,1152]{3,2,1,0:T(8,128)(2,1)S(1)} %get-tuple-element.83), channel_id=1, source_target_pairs={{0,4},{4,0},{1,5},{5,1},{2,6},{6,2},{3,7},{7,3},{8,12},{12,8},{9,1... | collective-permute-start | bytes 3538952 | tf_op jit(solution)/shard_map/ppermute | solution.py:23
  60.0 8.0 %collective-permute-done.18.refs_2_ = bf16[2,128,1152]{2,1,0:T(8,128)(2,1)S(1)} collective-permute-done((bf16[2,128,1152]{2,1,0:T(8,128)(2,1)S(1)}, bf16[2,128,1152]{2,1,0:T(8,128)(2,1)S(1)}, u32[]{:S(2)}, u32[]{:S(2)}) %collective-permute-start.18) | collective-permute-done | bytes 589856 | tf_op jit(solution)/shard_map/ppermute | solution.py:23
  68.6 2.7 %collective-permute-start.20 = (bf16[2,128,1152]{2,1,0:T(8,128)(2,1)S(1)}, bf16[2,128,1152]{2,1,0:T(8,128)(2,1)S(1)}, u32[]{:S(2)}, u32[]{:S(2)}) collective-permute-start(bf16[2,128,1152]{2,1,0:T(8,128)(2,1)S(1)} %get-tuple-element.87), channel_id=1, source_target_pairs={{0,24},{8,0},{16,8},{24,16},{1,25},{9,1},{17,9},{25,17},{2,26},{10... | collective-permute-start | bytes 1769480 | tf_op jit(solution)/shard_map/ppermute | solution.py:23
  71.3 3.2 %shard_map.136 = (bf16[1,4,144,1024]{3,2,1,0:T(8,128)(2,1)S(1)}, bf16[1,4,144,1024]{3,2,1,0:T(8,128)(2,1)S(1)}) custom-call(s32[19]{0:T(128)S(1)} %stack.79.where_ref, bf16[1024,4608]{1,0:T(8,128)(2,1)S(1)} %bitcast.45, bf16[1024,1024]{1,0:T(8,128)(2,1)S(1)} %copy-done.4), custom_call_target="tpu_custom_call" | custom-call | flops 2415919104 | bytes 2359296 | tf_op jit(solution)/shard_map/pallas_call | solution.py:89
  74.5 2.2 %collective-permute-start.6 = (bf16[1,4,144,1024]{3,2,1,0:T(8,128)(2,1)S(1)}, bf16[1,4,144,1024]{3,2,1,0:T(8,128)(2,1)S(1)}, u32[]{:S(2)}, u32[]{:S(2)}) collective-permute-start(bf16[1,4,144,1024]{3,2,1,0:T(8,128)(2,1)S(1)} %get-tuple-element.75), channel_id=1, source_target_pairs={{0,4},{4,0},{1,5},{5,1},{2,6},{6,2},{3,7},{7,3},{8,12},{12,8},{9,1... | collective-permute-start | bytes 3538952 | tf_op jit(solution)/shard_map/ppermute | solution.py:23
  76.9 6.2 %collective-permute-done.19.refs_2_ = bf16[2,128,1152]{2,1,0:T(8,128)(2,1)S(1)} collective-permute-done((bf16[2,128,1152]{2,1,0:T(8,128)(2,1)S(1)}, bf16[2,128,1152]{2,1,0:T(8,128)(2,1)S(1)}, u32[]{:S(2)}, u32[]{:S(2)}) %collective-permute-start.19) | collective-permute-done | bytes 589856 | tf_op jit(solution)/shard_map/ppermute | solution.py:23
  84.6 10.3 %collective-permute-done.17.refs_3_ = bf16[2,128,1152]{2,1,0:T(8,128)(2,1)S(1)} collective-permute-done((bf16[2,128,1152]{2,1,0:T(8,128)(2,1)S(1)}, bf16[2,128,1152]{2,1,0:T(8,128)(2,1)S(1)}, u32[]{:S(2)}, u32[]{:S(2)}) %collective-permute-start.17) | collective-permute-done | bytes 589856 | tf_op jit(solution)/shard_map/ppermute | solution.py:23
  102.0 7.1 %collective-permute-done.8.refs_3_ = bf16[2,144,1024]{2,1,0:T(8,128)(2,1)S(1)} collective-permute-done((bf16[2,144,1024]{2,1,0:T(8,128)(2,1)S(1)}, bf16[2,144,1024]{2,1,0:T(8,128)(2,1)S(1)}, u32[]{:S(2)}, u32[]{:S(2)}) %collective-permute-start.8) | collective-permute-done | bytes 589856 | tf_op jit(solution)/shard_map/ppermute | solution.py:23
  112.0 2.3 %collective-permute-done.21 = bf16[1,128,1152]{2,1,0:T(8,128)(2,1)S(1)} collective-permute-done((bf16[1,128,1152]{2,1,0:T(8,128)(2,1)S(1)}, bf16[1,128,1152]{2,1,0:T(8,128)(2,1)S(1)}, u32[]{:S(2)}, u32[]{:S(2)}) %collective-permute-start.21) | collective-permute-done | bytes 294944 | tf_op jit(solution)/shard_map/ppermute | solution.py:23
  114.3 3.4 %collective-permute-start.14 = (bf16[1,144,1024]{2,1,0:T(8,128)(2,1)S(1)}, bf16[1,144,1024]{2,1,0:T(8,128)(2,1)S(1)}, u32[]{:S(2)}, u32[]{:S(2)}) collective-permute-start(bf16[1,144,1024]{2,1,0:T(8,128)(2,1)S(1)} %get-tuple-element.82), channel_id=1, source_target_pairs={{0,24},{8,0},{16,8},{24,16},{1,25},{9,1},{17,9},{25,17},{2,26},{10... | collective-permute-start | bytes 884744 | tf_op jit(solution)/shard_map/ppermute | solution.py:23
  117.7 4.2 %collective-permute-done.22 = bf16[1,128,1152]{2,1,0:T(8,128)(2,1)S(1)} collective-permute-done((bf16[1,128,1152]{2,1,0:T(8,128)(2,1)S(1)}, bf16[1,128,1152]{2,1,0:T(8,128)(2,1)S(1)}, u32[]{:S(2)}, u32[]{:S(2)}) %collective-permute-start.22) | collective-permute-done | bytes 294944 | tf_op jit(solution)/shard_map/ppermute | solution.py:23
  123.5 8.8 %collective-permute-start.24 = (f32[1,1280]{1,0:T(1,128)S(1)}, f32[1,1280]{1,0:T(1,128)S(1)}, u32[]{:S(2)}, u32[]{:S(2)}) collective-permute-start(f32[1,1280]{1,0:T(1,128)S(1)} %get-tuple-element.92), channel_id=1, source_target_pairs={{0,4},{4,0},{1,5},{5,1},{2,6},{6,2},{3,7},{7,3},{8,12},{12,8},{9,1... | collective-permute-start | bytes 15368 | tf_op jit(solution)/shard_map/ppermute | solution.py:23
  133.2 21.8 %all_to_all.5.packed = f32[64,1,1664]{2,1,0:T(1,128)S(1)} all-to-all(f32[64,1,1664]{2,1,0:T(1,128)S(1)} %shard_map.144), channel_id=1, replica_groups=mesh['row_0'=4,'row_1'=4,'row_2'=2,'col'=4] {'row_0','row_1','col'}, dimensions={0} | all-to-all | bytes 851968 | tf_op jit(solution)/shard_map/all_to_all | solution.py:368
  155.6 2.0 %collective-permute-start.25 = (f32[1,1152]{1,0:T(1,128)S(1)}, f32[1,1152]{1,0:T(1,128)S(1)}, u32[]{:S(2)}, u32[]{:S(2)}) collective-permute-start(f32[1,1152]{1,0:T(1,128)S(1)} %get-tuple-element.93.half_ref), channel_id=1, source_target_pairs={{0,4},{4,0},{1,5},{5,1},{2,6},{6,2},{3,7},{7,3},{8,12},{12,8},{9,1... | collective-permute-start | bytes 13832 | tf_op jit(solution)/shard_map/ppermute | solution.py:23
  (83 shorter events, 30.5 us)
Async XLA Ops:
  9.3 8.4 %collective-permute-start = (bf16[1,4,144,1024]{3,2,1,0:T(8,128)(2,1)S(1)}, bf16[1,4,144,1024]{3,2,1,0:T(8,128)(2,1)S(1)}, u32[]{:S(2)}, u32[]{:S(2)}) collective-permute-start(bf16[1,4,144,1024]{3,2,1,0:T(8,128)(2,1)S(1)} %get-tuple-element.55), channel_id=1, source_target_pairs={{0,4},{4,0},{1,5},{5,1},{2,6},{6,2},{3,7},{7,3},{8,12},{12,8},{9,1... | collective-permute-start | bytes 3538952 | tf_op jit(solution)/shard_map/ppermute | solution.py:23
  28.1 25.1 %collective-permute-start.2 = (bf16[2,4,144,1024]{3,2,1,0:T(8,128)(2,1)S(1)}, bf16[2,4,144,1024]{3,2,1,0:T(8,128)(2,1)S(1)}, u32[]{:S(2)}, u32[]{:S(2)}) collective-permute-start(bf16[2,4,144,1024]{3,2,1,0:T(8,128)(2,1)S(1)} %get-tuple-element.63), channel_id=1, source_target_pairs={{0,4},{4,0},{1,5},{5,1},{2,6},{6,2},{3,7},{7,3},{8,12},{12,8},{9,1... | collective-permute-start | bytes 7077896 | tf_op jit(solution)/shard_map/ppermute | solution.py:23
  34.9 19.4 %collective-permute-start.4 = (bf16[2,4,128,1152]{3,2,1,0:T(8,128)(2,1)S(1)}, bf16[2,4,128,1152]{3,2,1,0:T(8,128)(2,1)S(1)}, u32[]{:S(2)}, u32[]{:S(2)}) collective-permute-start(bf16[2,4,128,1152]{3,2,1,0:T(8,128)(2,1)S(1)} %get-tuple-element.68), channel_id=1, source_target_pairs={{0,4},{4,0},{1,5},{5,1},{2,6},{6,2},{3,7},{7,3},{8,12},{12,8},{9,1... | collective-permute-start | bytes 7077896 | tf_op jit(solution)/shard_map/ppermute | solution.py:23
  35.4 16.2 %collective-permute-start.9 = (bf16[2,144,1024]{2,1,0:T(8,128)(2,1)S(1)}, bf16[2,144,1024]{2,1,0:T(8,128)(2,1)S(1)}, u32[]{:S(2)}, u32[]{:S(2)}) collective-permute-start(bf16[2,144,1024]{2,1,0:T(8,128)(2,1)S(1)} %get-tuple-element.56), channel_id=1, source_target_pairs={{0,32},{32,64},{64,96},{96,0},{1,33},{33,65},{65,97},{97,1},{2,34}... | collective-permute-start | bytes 1769480 | tf_op jit(solution)/shard_map/ppermute | solution.py:23
  36.8 17.0 %collective-permute-start.3 = (bf16[2,144,1024]{2,1,0:T(8,128)(2,1)S(1)}, bf16[2,144,1024]{2,1,0:T(8,128)(2,1)S(1)}, u32[]{:S(2)}, u32[]{:S(2)}) collective-permute-start(bf16[2,144,1024]{2,1,0:T(8,128)(2,1)S(1)} %get-tuple-element.64), channel_id=1, source_target_pairs={{0,96},{32,0},{64,32},{96,64},{1,97},{33,1},{65,33},{97,65},{2,98}... | collective-permute-start | bytes 1769480 | tf_op jit(solution)/shard_map/ppermute | solution.py:23
  38.2 16.2 %collective-permute-start.5 = (bf16[2,128,1152]{2,1,0:T(8,128)(2,1)S(1)}, bf16[2,128,1152]{2,1,0:T(8,128)(2,1)S(1)}, u32[]{:S(2)}, u32[]{:S(2)}) collective-permute-start(bf16[2,128,1152]{2,1,0:T(8,128)(2,1)S(1)} %get-tuple-element.69), channel_id=1, source_target_pairs={{0,24},{8,0},{16,8},{24,16},{1,25},{9,1},{17,9},{25,17},{2,26},{10... | collective-permute-start | bytes 1769480 | tf_op jit(solution)/shard_map/ppermute | solution.py:23
  51.6 16.4 %collective-permute-start.18 = (bf16[2,128,1152]{2,1,0:T(8,128)(2,1)S(1)}, bf16[2,128,1152]{2,1,0:T(8,128)(2,1)S(1)}, u32[]{:S(2)}, u32[]{:S(2)}) collective-permute-start(bf16[2,128,1152]{2,1,0:T(8,128)(2,1)S(1)} %get-tuple-element.60), channel_id=1, source_target_pairs={{0,8},{8,16},{16,24},{24,0},{1,9},{9,17},{17,25},{25,1},{2,10},{10... | collective-permute-start | bytes 1769480 | tf_op jit(solution)/shard_map/ppermute | solution.py:23
  53.7 23.0 %collective-permute-start.10 = (bf16[2,144,1024]{2,1,0:T(8,128)(2,1)S(1)}, bf16[2,144,1024]{2,1,0:T(8,128)(2,1)S(1)}, u32[]{:S(2)}, u32[]{:S(2)}) collective-permute-start(bf16[2,144,1024]{2,1,0:T(8,128)(2,1)S(1)} %get-tuple-element.78), channel_id=1, source_target_pairs={{0,32},{32,64},{64,96},{96,0},{1,33},{33,65},{65,97},{97,1},{2,34}... | collective-permute-start | bytes 1769480 | tf_op jit(solution)/shard_map/ppermute | solution.py:23
  58.4 37.8 %collective-permute-start.15 = (bf16[1,4,128,1152]{3,2,1,0:T(8,128)(2,1)S(1)}, bf16[1,4,128,1152]{3,2,1,0:T(8,128)(2,1)S(1)}, u32[]{:S(2)}, u32[]{:S(2)}) collective-permute-start(bf16[1,4,128,1152]{3,2,1,0:T(8,128)(2,1)S(1)} %get-tuple-element.83), channel_id=1, source_target_pairs={{0,4},{4,0},{1,5},{5,1},{2,6},{6,2},{3,7},{7,3},{8,12},{12,8},{9,1... | collective-permute-start | bytes 3538952 | tf_op jit(solution)/shard_map/ppermute | solution.py:23
  68.6 14.6 %collective-permute-start.19 = (bf16[2,128,1152]{2,1,0:T(8,128)(2,1)S(1)}, bf16[2,128,1152]{2,1,0:T(8,128)(2,1)S(1)}, u32[]{:S(2)}, u32[]{:S(2)}) collective-permute-start(bf16[2,128,1152]{2,1,0:T(8,128)(2,1)S(1)} %get-tuple-element.86), channel_id=1, source_target_pairs={{0,8},{8,16},{16,24},{24,0},{1,9},{9,17},{17,25},{25,1},{2,10},{10... | collective-permute-start | bytes 1769480 | tf_op jit(solution)/shard_map/ppermute | solution.py:23
  68.6 14.6 %collective-permute-start.20 = (bf16[2,128,1152]{2,1,0:T(8,128)(2,1)S(1)}, bf16[2,128,1152]{2,1,0:T(8,128)(2,1)S(1)}, u32[]{:S(2)}, u32[]{:S(2)}) collective-permute-start(bf16[2,128,1152]{2,1,0:T(8,128)(2,1)S(1)} %get-tuple-element.87), channel_id=1, source_target_pairs={{0,24},{8,0},{16,8},{24,16},{1,25},{9,1},{17,9},{25,17},{2,26},{10... | collective-permute-start | bytes 1769480 | tf_op jit(solution)/shard_map/ppermute | solution.py:23
  74.5 25.9 %collective-permute-start.6 = (bf16[1,4,144,1024]{3,2,1,0:T(8,128)(2,1)S(1)}, bf16[1,4,144,1024]{3,2,1,0:T(8,128)(2,1)S(1)}, u32[]{:S(2)}, u32[]{:S(2)}) collective-permute-start(bf16[1,4,144,1024]{3,2,1,0:T(8,128)(2,1)S(1)} %get-tuple-element.75), channel_id=1, source_target_pairs={{0,4},{4,0},{1,5},{5,1},{2,6},{6,2},{3,7},{7,3},{8,12},{12,8},{9,1... | collective-permute-start | bytes 3538952 | tf_op jit(solution)/shard_map/ppermute | solution.py:23
  76.7 18.1 %collective-permute-start.17 = (bf16[2,128,1152]{2,1,0:T(8,128)(2,1)S(1)}, bf16[2,128,1152]{2,1,0:T(8,128)(2,1)S(1)}, u32[]{:S(2)}, u32[]{:S(2)}) collective-permute-start(bf16[2,128,1152]{2,1,0:T(8,128)(2,1)S(1)} %get-tuple-element.84), channel_id=1, source_target_pairs={{0,24},{8,0},{16,8},{24,16},{1,25},{9,1},{17,9},{25,17},{2,26},{10... | collective-permute-start | bytes 1769480 | tf_op jit(solution)/shard_map/ppermute | solution.py:23
  83.2 13.7 %collective-permute-start.16 = (bf16[2,128,1152]{2,1,0:T(8,128)(2,1)S(1)}, bf16[2,128,1152]{2,1,0:T(8,128)(2,1)S(1)}, u32[]{:S(2)}, u32[]{:S(2)}) collective-permute-start(bf16[2,128,1152]{2,1,0:T(8,128)(2,1)S(1)} %get-tuple-element.70), channel_id=1, source_target_pairs={{0,8},{8,16},{16,24},{24,0},{1,9},{9,17},{17,25},{25,1},{2,10},{10... | collective-permute-start | bytes 1769480 | tf_op jit(solution)/shard_map/ppermute | solution.py:23
  83.2 15.6 %collective-permute-start.11 = (bf16[2,144,1024]{2,1,0:T(8,128)(2,1)S(1)}, bf16[2,144,1024]{2,1,0:T(8,128)(2,1)S(1)}, u32[]{:S(2)}, u32[]{:S(2)}) collective-permute-start(bf16[2,144,1024]{2,1,0:T(8,128)(2,1)S(1)} %get-tuple-element.79), channel_id=1, source_target_pairs={{0,96},{32,0},{64,32},{96,64},{1,97},{33,1},{65,33},{97,65},{2,98}... | collective-permute-start | bytes 1769480 | tf_op jit(solution)/shard_map/ppermute | solution.py:23
  94.8 14.3 %collective-permute-start.8 = (bf16[2,144,1024]{2,1,0:T(8,128)(2,1)S(1)}, bf16[2,144,1024]{2,1,0:T(8,128)(2,1)S(1)}, u32[]{:S(2)}, u32[]{:S(2)}) collective-permute-start(bf16[2,144,1024]{2,1,0:T(8,128)(2,1)S(1)} %get-tuple-element.76), channel_id=1, source_target_pairs={{0,96},{32,0},{64,32},{96,64},{1,97},{33,1},{65,33},{97,65},{2,98}... | collective-permute-start | bytes 1769480 | tf_op jit(solution)/shard_map/ppermute | solution.py:23
  96.2 14.1 %collective-permute-start.7 = (bf16[2,144,1024]{2,1,0:T(8,128)(2,1)S(1)}, bf16[2,144,1024]{2,1,0:T(8,128)(2,1)S(1)}, u32[]{:S(2)}, u32[]{:S(2)}) collective-permute-start(bf16[2,144,1024]{2,1,0:T(8,128)(2,1)S(1)} %get-tuple-element.65), channel_id=1, source_target_pairs={{0,32},{32,64},{64,96},{96,0},{1,33},{33,65},{65,97},{97,1},{2,34}... | collective-permute-start | bytes 1769480 | tf_op jit(solution)/shard_map/ppermute | solution.py:23
  96.9 17.4 %collective-permute-start.21 = (bf16[1,128,1152]{2,1,0:T(8,128)(2,1)S(1)}, bf16[1,128,1152]{2,1,0:T(8,128)(2,1)S(1)}, u32[]{:S(2)}, u32[]{:S(2)}) collective-permute-start(bf16[1,128,1152]{2,1,0:T(8,128)(2,1)S(1)} %get-tuple-element.88), channel_id=1, source_target_pairs={{0,64},{32,96},{64,0},{96,32},{1,65},{33,97},{65,1},{97,33},{2,66}... | collective-permute-start | bytes 884744 | tf_op jit(solution)/shard_map/ppermute | solution.py:23
  98.8 23.1 %collective-permute-start.22 = (bf16[1,128,1152]{2,1,0:T(8,128)(2,1)S(1)}, bf16[1,128,1152]{2,1,0:T(8,128)(2,1)S(1)}, u32[]{:S(2)}, u32[]{:S(2)}) collective-permute-start(bf16[1,128,1152]{2,1,0:T(8,128)(2,1)S(1)} %get-tuple-element.89), channel_id=1, source_target_pairs={{0,32},{32,64},{64,96},{96,0},{1,33},{33,65},{65,97},{97,1},{2,34}... | collective-permute-start | bytes 884744 | tf_op jit(solution)/shard_map/ppermute | solution.py:23
  100.4 21.5 %collective-permute-start.23 = (bf16[1,128,1152]{2,1,0:T(8,128)(2,1)S(1)}, bf16[1,128,1152]{2,1,0:T(8,128)(2,1)S(1)}, u32[]{:S(2)}, u32[]{:S(2)}) collective-permute-start(bf16[1,128,1152]{2,1,0:T(8,128)(2,1)S(1)} %get-tuple-element.90), channel_id=1, source_target_pairs={{0,96},{32,0},{64,32},{96,64},{1,97},{33,1},{65,33},{97,65},{2,98}... | collective-permute-start | bytes 884744 | tf_op jit(solution)/shard_map/ppermute | solution.py:23
  109.1 13.2 %collective-permute-start.12 = (bf16[1,144,1024]{2,1,0:T(8,128)(2,1)S(1)}, bf16[1,144,1024]{2,1,0:T(8,128)(2,1)S(1)}, u32[]{:S(2)}, u32[]{:S(2)}) collective-permute-start(bf16[1,144,1024]{2,1,0:T(8,128)(2,1)S(1)} %get-tuple-element.80), channel_id=1, source_target_pairs={{0,16},{8,24},{16,0},{24,8},{1,17},{9,25},{17,1},{25,9},{2,18},{10... | collective-permute-start | bytes 884744 | tf_op jit(solution)/shard_map/ppermute | solution.py:23
  110.3 11.9 %collective-permute-start.13 = (bf16[1,144,1024]{2,1,0:T(8,128)(2,1)S(1)}, bf16[1,144,1024]{2,1,0:T(8,128)(2,1)S(1)}, u32[]{:S(2)}, u32[]{:S(2)}) collective-permute-start(bf16[1,144,1024]{2,1,0:T(8,128)(2,1)S(1)} %get-tuple-element.81), channel_id=1, source_target_pairs={{0,8},{8,16},{16,24},{24,0},{1,9},{9,17},{17,25},{25,1},{2,10},{10... | collective-permute-start | bytes 884744 | tf_op jit(solution)/shard_map/ppermute | solution.py:23
  114.3 7.9 %collective-permute-start.14 = (bf16[1,144,1024]{2,1,0:T(8,128)(2,1)S(1)}, bf16[1,144,1024]{2,1,0:T(8,128)(2,1)S(1)}, u32[]{:S(2)}, u32[]{:S(2)}) collective-permute-start(bf16[1,144,1024]{2,1,0:T(8,128)(2,1)S(1)} %get-tuple-element.82), channel_id=1, source_target_pairs={{0,24},{8,0},{16,8},{24,16},{1,25},{9,1},{17,9},{25,17},{2,26},{10... | collective-permute-start | bytes 884744 | tf_op jit(solution)/shard_map/ppermute | solution.py:23
  123.5 9.7 %collective-permute-start.24 = (f32[1,1280]{1,0:T(1,128)S(1)}, f32[1,1280]{1,0:T(1,128)S(1)}, u32[]{:S(2)}, u32[]{:S(2)}) collective-permute-start(f32[1,1280]{1,0:T(1,128)S(1)} %get-tuple-element.92), channel_id=1, source_target_pairs={{0,4},{4,0},{1,5},{5,1},{2,6},{6,2},{3,7},{7,3},{8,12},{12,8},{9,1... | collective-permute-start | bytes 15368 | tf_op jit(solution)/shard_map/ppermute | solution.py:23
  (14 other events, 65.0 us)

commit v3 on v2

--- a/solution.py
+++ b/solution.py
@@ -163,31 +163,12 @@
     give_ref[...] = jnp.concatenate([jnp.where(core == 0, high, low), scalars], axis=1)
 
 
-def pack_kernel(keep, got, rows, packed_ref):
-    total = keep[...] + got[...]
-    width = total.shape[1] - 128
-    row = jnp.concatenate([total[:, :width], rows[...], total[:, width:]], axis=1)
-    for i in range(packed_ref.shape[0]):
-        packed_ref[i] = row
-
-
-def unpack_kernel(where_ref, packed, half_ref, rows_ref, scalars_ref):
-    place, column = where_ref[17], where_ref[18]
-    width, length = half_ref.shape[1], rows_ref.shape[1]
-    peers = packed.shape[0] // 4
-    mine = packed[column]
-    for p in range(1, peers):
-        mine = mine + packed[4 * p + column]
-    rows = packed[4 * place]
-    for j in range(1, 4):
-        rows = rows + packed[4 * place + j]
-    everyone = packed[0, :, width + length :]
-    for p in range(1, 4 * peers):
-        everyone = everyone + packed[p, :, width + length :]
-    lane = lax.broadcasted_iota(jnp.int32, (1, 128), 1)
-    half_ref[...] = mine[:, :width]
-    rows_ref[...] = rows[:, width : width + length]
-    scalars_ref[...] = jnp.where(lane < 2, everyone, mine[:, width + length :])
+def exchanged(value, axis):
+    return [shift(value, axis, k) for k in (2, 1, 3)]
+
+
+def four(own, far, near, after):
+    return (own + far) + (near + after)
 
 
 def finish_kernel(
@@ -197,8 +178,10 @@
     where_ref,
     half_ref,
     other_ref,
-    scalars_ref,
-    rows_ref,
+    row_0,
+    row_1,
+    row_2,
+    row_3,
     query_row,
     query_col,
     output_row,
@@ -213,12 +196,14 @@
     output_col_new,
 ):
     core = where_ref[0]
-    half, other = half_ref[...], other_ref[...]
+    other = other_ref[...]
+    half, old = half_ref[:, : other.shape[1]], half_ref[:, other.shape[1] :]
+    all_rows = four(row_0[...], row_1[...], row_2[...], row_3[...])
     first, second = jnp.where(core == 0, half, other), jnp.where(core == 0, other, half)
     sums = jnp.concatenate([first, second], axis=1)
     query_width = query_col.shape[1]
     lane = lax.broadcasted_iota(jnp.int32, (1, 128), 1)
-    tail = scalars_ref[...]
+    tail = jnp.where(lane < 2, all_rows[:, all_rows.shape[1] - 128 :], old)
     query_squares, output_squares, query_old, output_old = (
         jnp.sum(jnp.where(lane == i, tail, 0.0), axis=1, keepdims=True) for i in range(4)
     )
@@ -235,7 +220,7 @@
             return squared_scale * value / count + epsilon_one
 
         level = decay_rate * old / whole_rows + fresh * mean(squares, whole_rows * whole_cols)
-        row_next = decay_rate * row[...] + fresh * mean(rows_ref[:, at : at + rows], whole_cols)
+        row_next = decay_rate * row[...] + fresh * mean(all_rows[:, at : at + rows], whole_cols)
         col_next = decay_rate * col[...] + fresh * mean(sums[:, offset : offset + columns], whole_rows)
         row_new[...] = row_next
         col_new[...] = col_next
@@ -282,7 +267,6 @@
         + [lax.rem(z + k, 4) * pair_output for k in range(4)]
         + [lax.rem(k + 4 - z, 4) for k in range(4)]
         + [lax.rem(y + k, 4) for k in range(4)]
-        + [4 * y + z, lax.axis_index(X)]
     ).astype(jnp.int32)
 
     def made(kernel, where, left, right, ks, group, vmem):
@@ -360,19 +344,12 @@
         functools.partial(halves_kernel, split), [packet, packet], rows, *sums, where=where
     )
     got = shift(give, CORE, 1)
-    peers = (Y, Z, X)
-    count = lax.axis_size(peers)
-    (packed,) = small_call(
-        pack_kernel, [((count, 1, width + 128 + rows.shape[1]), jnp.float32)], keep, got, rows
-    )
-    packed = lax.all_to_all(packed, peers, 0, 0, tiled=True)
-    half, rows, scalars = small_call(
-        unpack_kernel,
-        [((1, width), jnp.float32), (rows.shape, jnp.float32), ((1, 128), jnp.float32)],
-        packed,
-        where=where,
-    )
-    other = shift(half, CORE, 1)
+    half = keep + got
+    for axis in (Y, Z):
+        half = four(half, *exchanged(half, axis))
+    other = shift(half[:, :width], CORE, 1)
+    rows = jnp.concatenate([rows, half[:, width:]], axis=1)
+    others = exchanged(rows, X)
     olds = [line(v) for v in (row_query, col_query, row_output, col_output)]
     update_query, new_row_query, new_col_query, update_output, new_row_output, new_col_output = small_call(
         functools.partial(finish_kernel, split, lax.axis_size(X), lax.axis_size(ROW)),
@@ -386,8 +363,8 @@
         ],
         half,
         other,
-        scalars,
         rows,
+        *others,
         *olds,
         query_grad,
         output_grad,

time: 161 us -> 160 us (level)
  blocking collectives: 21.8 us -> 0 us
  starting transfers between devices: 40 us -> 54.4 us
  waiting for transfers between devices: 53.3 us -> 59.9 us
    all_to_all x1 -> x0, blocking collectives: 21.8 us -> none  [shards(): packed = lax.all_to_all(packed, peers, 0, 0, tiled=True)]
    ppermute x26 -> x35, starting transfers between devices: 40 us -> 54.4 us  [shift(): lax.ppermute(value, axis, [(i, (i + by) % size) for i in range(size)])]
    ppermute x26 -> x35, waiting for transfers between devices: 53.3 us -> 59.9 us  [shift(): lax.ppermute(value, axis, [(i, (i + by) % size) for i in range(size)])]
  transfers between devices with their start and end apart: 26 -> 35, of which waited for: 12 -> 17; matrix products, arithmetic and copies ran while one was open for 0% -> 0% of each run, Pallas kernels for 13% -> 13%
where the time goes in v3:
time: 160 us; the launch traced here: 159 us
  waiting for transfers between devices  59.9 us (37%)
  starting transfers between devices  54.4 us (34%)
  Pallas kernels  32.7 us (20%)
  local copies, waits for them, and re-layouts  10.1 us (6%)
    ppermute x35, waiting for transfers between devices, shift(): lax.ppermute(value, axis, [(i, (i + by) % size) for i in range(size)])  59.9 us
    ppermute x35, starting transfers between devices, shift(): lax.ppermute(value, axis, [(i, (i + by) % size) for i in range(size)])  54.4 us
    pallas_call x6, Pallas kernels, partial_blocks(): pl.pallas_call(functools.partial(kernel, blocks[0], group), out_shape=[sh...  25.8 us
    unnamed x24, local copies, waits for them, and re-layouts  9.98 us
    pallas_call x10, Pallas kernels, add_entries(): pl.pallas_call(functools.partial(add_kernel, plan, 16), out_shape=[jax.Sh...  4.66 us
  transfers between devices with their start and end apart: 35, of which 17 were waited for; matrix products, arithmetic and copies ran while one was open for 0% of the time, Pallas kernels for 13%

profile of v3, /device:TPU:1, one launch (start us, length us, event | category | flops | bytes accessed | tf_op | source)
XLA Modules:
  0.0 159.4 jit_solution(9474856633013450227)
XLA Ops:
  0.8 3.7 %copy-done = bf16[1024,4608]{1,0:T(8,128)(2,1)S(1)} copy-done((bf16[1024,4608]{1,0:T(8,128)(2,1)S(1)}, bf16[1024,4608]{1,0:T(8,128)(2,1)}, u32[]{:S(2)}) %copy-start) | copy-done | bytes 9437208
  6.0 3.2 %shard_map.127 = (bf16[1,4,144,1024]{3,2,1,0:T(8,128)(2,1)S(1)}, bf16[1,4,144,1024]{3,2,1,0:T(8,128)(2,1)S(1)}) custom-call(s32[17]{0:T(128)S(1)} %stack.71.where_ref, bf16[1024,4608]{1,0:T(8,128)(2,1)S(1)} %copy-done, bf16[1024,1024]{1,0:T(8,128)(2,1)S(1)} %copy-done.3), custom_call_target="tpu_custom_call" | custom-call | flops 2415919104 | bytes 2359296 | tf_op jit(solution)/shard_map/pallas_call | solution.py:89
  10.7 3.4 %copy-done.1 = bf16[1024,4096]{1,0:T(8,128)(2,1)S(1)} copy-done((bf16[1024,4096]{1,0:T(8,128)(2,1)S(1)}, bf16[1024,4096]{1,0:T(8,128)(2,1)}, u32[]{:S(2)}) %copy-start.1) | copy-done | bytes 8388632
  14.1 3.5 %shard_map.129 = (bf16[1,4,128,1152]{3,2,1,0:T(8,128)(2,1)S(1)}, bf16[1,4,128,1152]{3,2,1,0:T(8,128)(2,1)S(1)}) custom-call(s32[17]{0:T(128)S(1)} %stack.71.where_ref, bf16[1024,4096]{1,0:T(8,128)(2,1)S(1)} %copy-done.1, bf16[1024,1152]{1,0:T(8,128)(2,1)S(1)} %copy-done.2), custom_call_target="tpu_custom_call" | custom-call | flops 2415919104 | bytes 2097152 | tf_op jit(solution)/shard_map/pallas_call | solution.py:89
  22.1 5.9 %shard_map.131 = (bf16[2,4,144,1024]{3,2,1,0:T(8,128)(2,1)S(1)}, bf16[2,4,144,1024]{3,2,1,0:T(8,128)(2,1)S(1)}) custom-call(s32[17]{0:T(128)S(1)} %stack.71.where_ref, bf16[1024,4608]{1,0:T(8,128)(2,1)S(1)} %bitcast.43, bf16[1024,1024]{1,0:T(8,128)(2,1)S(1)} %copy-done.4), custom_call_target="tpu_custom_call" | custom-call | flops 4831838208 | bytes 4718592 | tf_op jit(solution)/shard_map/pallas_call | solution.py:89
  28.5 6.4 %shard_map.133 = (bf16[2,4,128,1152]{3,2,1,0:T(8,128)(2,1)S(1)}, bf16[2,4,128,1152]{3,2,1,0:T(8,128)(2,1)S(1)}) custom-call(s32[17]{0:T(128)S(1)} %stack.71.where_ref, bf16[1024,4096]{1,0:T(8,128)(2,1)S(1)} %copy-done.1, bf16[1024,1152]{1,0:T(8,128)(2,1)S(1)} %copy-done.2), custom_call_target="tpu_custom_call" | custom-call | flops 4831838208 | bytes 4194304 | tf_op jit(solution)/shard_map/pallas_call | solution.py:89
  38.2 3.7 %collective-permute-start.5 = (bf16[2,128,1152]{2,1,0:T(8,128)(2,1)S(1)}, bf16[2,128,1152]{2,1,0:T(8,128)(2,1)S(1)}, u32[]{:S(2)}, u32[]{:S(2)}) collective-permute-start(bf16[2,128,1152]{2,1,0:T(8,128)(2,1)S(1)} %get-tuple-element.66), channel_id=1, source_target_pairs={{0,24},{8,0},{16,8},{24,16},{1,25},{9,1},{17,9},{25,17},{2,26},{10... | collective-permute-start | bytes 1769480 | tf_op jit(solution)/shard_map/ppermute | solution.py:23
  41.9 9.7 %collective-permute-done.9.refs_2_ = bf16[2,144,1024]{2,1,0:T(8,128)(2,1)S(1)} collective-permute-done((bf16[2,144,1024]{2,1,0:T(8,128)(2,1)S(1)}, bf16[2,144,1024]{2,1,0:T(8,128)(2,1)S(1)}, u32[]{:S(2)}, u32[]{:S(2)}) %collective-permute-start.9) | collective-permute-done | bytes 589856 | tf_op jit(solution)/shard_map/ppermute | solution.py:23
  54.9 3.5 %shard_map.135 = (bf16[1,4,128,1152]{3,2,1,0:T(8,128)(2,1)S(1)}, bf16[1,4,128,1152]{3,2,1,0:T(8,128)(2,1)S(1)}) custom-call(s32[17]{0:T(128)S(1)} %stack.71.where_ref, bf16[1024,4096]{1,0:T(8,128)(2,1)S(1)} %copy-done.1, bf16[1024,1152]{1,0:T(8,128)(2,1)S(1)} %copy-done.2), custom_call_target="tpu_custom_call" | custom-call | flops 2415919104 | bytes 2097152 | tf_op jit(solution)/shard_map/pallas_call | solution.py:89
  60.0 7.9 %collective-permute-done.18.refs_2_ = bf16[2,128,1152]{2,1,0:T(8,128)(2,1)S(1)} collective-permute-done((bf16[2,128,1152]{2,1,0:T(8,128)(2,1)S(1)}, bf16[2,128,1152]{2,1,0:T(8,128)(2,1)S(1)}, u32[]{:S(2)}, u32[]{:S(2)}) %collective-permute-start.18) | collective-permute-done | bytes 589856 | tf_op jit(solution)/shard_map/ppermute | solution.py:23
  68.6 2.7 %collective-permute-start.20 = (bf16[2,128,1152]{2,1,0:T(8,128)(2,1)S(1)}, bf16[2,128,1152]{2,1,0:T(8,128)(2,1)S(1)}, u32[]{:S(2)}, u32[]{:S(2)}) collective-permute-start(bf16[2,128,1152]{2,1,0:T(8,128)(2,1)S(1)} %get-tuple-element.84), channel_id=1, source_target_pairs={{0,24},{8,0},{16,8},{24,16},{1,25},{9,1},{17,9},{25,17},{2,26},{10... | collective-permute-start | bytes 1769480 | tf_op jit(solution)/shard_map/ppermute | solution.py:23
  71.3 3.2 %shard_map.136 = (bf16[1,4,144,1024]{3,2,1,0:T(8,128)(2,1)S(1)}, bf16[1,4,144,1024]{3,2,1,0:T(8,128)(2,1)S(1)}) custom-call(s32[17]{0:T(128)S(1)} %stack.71.where_ref, bf16[1024,4608]{1,0:T(8,128)(2,1)S(1)} %bitcast.43, bf16[1024,1024]{1,0:T(8,128)(2,1)S(1)} %copy-done.4), custom_call_target="tpu_custom_call" | custom-call | flops 2415919104 | bytes 2359296 | tf_op jit(solution)/shard_map/pallas_call | solution.py:89
  76.9 6.2 %collective-permute-done.19.refs_2_ = bf16[2,128,1152]{2,1,0:T(8,128)(2,1)S(1)} collective-permute-done((bf16[2,128,1152]{2,1,0:T(8,128)(2,1)S(1)}, bf16[2,128,1152]{2,1,0:T(8,128)(2,1)S(1)}, u32[]{:S(2)}, u32[]{:S(2)}) %collective-permute-start.19) | collective-permute-done | bytes 589856 | tf_op jit(solution)/shard_map/ppermute | solution.py:23
  84.5 10.2 %collective-permute-done.17.refs_3_ = bf16[2,128,1152]{2,1,0:T(8,128)(2,1)S(1)} collective-permute-done((bf16[2,128,1152]{2,1,0:T(8,128)(2,1)S(1)}, bf16[2,128,1152]{2,1,0:T(8,128)(2,1)S(1)}, u32[]{:S(2)}, u32[]{:S(2)}) %collective-permute-start.17) | collective-permute-done | bytes 589856 | tf_op jit(solution)/shard_map/ppermute | solution.py:23
  102.0 7.0 %collective-permute-done.8.refs_3_ = bf16[2,144,1024]{2,1,0:T(8,128)(2,1)S(1)} collective-permute-done((bf16[2,144,1024]{2,1,0:T(8,128)(2,1)S(1)}, bf16[2,144,1024]{2,1,0:T(8,128)(2,1)S(1)}, u32[]{:S(2)}, u32[]{:S(2)}) %collective-permute-start.8) | collective-permute-done | bytes 589856 | tf_op jit(solution)/shard_map/ppermute | solution.py:23
  114.3 3.4 %collective-permute-start.14 = (bf16[1,144,1024]{2,1,0:T(8,128)(2,1)S(1)}, bf16[1,144,1024]{2,1,0:T(8,128)(2,1)S(1)}, u32[]{:S(2)}, u32[]{:S(2)}) collective-permute-start(bf16[1,144,1024]{2,1,0:T(8,128)(2,1)S(1)} %get-tuple-element.79), channel_id=1, source_target_pairs={{0,24},{8,0},{16,8},{24,16},{1,25},{9,1},{17,9},{25,17},{2,26},{10... | collective-permute-start | bytes 884744 | tf_op jit(solution)/shard_map/ppermute | solution.py:23
  117.7 4.2 %collective-permute-done.22 = bf16[1,128,1152]{2,1,0:T(8,128)(2,1)S(1)} collective-permute-done((bf16[1,128,1152]{2,1,0:T(8,128)(2,1)S(1)}, bf16[1,128,1152]{2,1,0:T(8,128)(2,1)S(1)}, u32[]{:S(2)}, u32[]{:S(2)}) %collective-permute-start.22) | collective-permute-done | bytes 294944 | tf_op jit(solution)/shard_map/ppermute | solution.py:23
  123.5 8.9 %collective-permute-start.24 = (f32[1,1280]{1,0:T(1,128)S(1)}, f32[1,1280]{1,0:T(1,128)S(1)}, u32[]{:S(2)}, u32[]{:S(2)}) collective-permute-start(f32[1,1280]{1,0:T(1,128)S(1)} %get-tuple-element.89), channel_id=1, source_target_pairs={{0,4},{4,0},{1,5},{5,1},{2,6},{6,2},{3,7},{7,3},{8,12},{12,8},{9,1... | collective-permute-start | bytes 15368 | tf_op jit(solution)/shard_map/ppermute | solution.py:23
  133.2 3.7 %collective-permute-start.27 = (f32[1,1280]{1,0:T(1,128)S(1)}, f32[1,1280]{1,0:T(1,128)S(1)}, u32[]{:S(2)}, u32[]{:S(2)}) collective-permute-start(f32[1,1280]{1,0:T(1,128)S(1)} %add.82), channel_id=1, source_target_pairs={{0,96},{32,0},{64,32},{96,64},{1,97},{33,1},{65,33},{97,65},{2,98}... | collective-permute-start | bytes 15368 | tf_op jit(solution)/shard_map/ppermute | solution.py:23
  138.2 2.4 %collective-permute-done.26 = f32[1,1280]{1,0:T(1,128)S(1)} collective-permute-done((f32[1,1280]{1,0:T(1,128)S(1)}, f32[1,1280]{1,0:T(1,128)S(1)}, u32[]{:S(2)}, u32[]{:S(2)}) %collective-permute-start.26) | collective-permute-done | bytes 5152 | tf_op jit(solution)/shard_map/ppermute | solution.py:23
  140.9 2.5 %collective-permute-start.30 = (f32[1,1280]{1,0:T(1,128)S(1)}, f32[1,1280]{1,0:T(1,128)S(1)}, u32[]{:S(2)}, u32[]{:S(2)}) collective-permute-start(f32[1,1280]{1,0:T(1,128)S(1)} %add_add_fusion.1), channel_id=1, source_target_pairs={{0,24},{8,0},{16,8},{24,16},{1,25},{9,1},{17,9},{25,17},{2,26},{10... | collective-permute-start | bytes 15368 | tf_op jit(solution)/shard_map/ppermute | solution.py:23
  144.6 2.4 %collective-permute-done.29 = f32[1,1280]{1,0:T(1,128)S(1)} collective-permute-done((f32[1,1280]{1,0:T(1,128)S(1)}, f32[1,1280]{1,0:T(1,128)S(1)}, u32[]{:S(2)}, u32[]{:S(2)}) %collective-permute-start.29) | collective-permute-done | bytes 5152 | tf_op jit(solution)/shard_map/ppermute | solution.py:23
  147.4 3.3 %collective-permute-start.31 = (f32[1,1152]{1,0:T(1,128)S(1)}, f32[1,1152]{1,0:T(1,128)S(1)}, u32[]{:S(2)}, u32[]{:S(2)}) collective-permute-start(f32[1,1152]{1,0:T(1,128)S(1)} %slice.8), channel_id=1, source_target_pairs={{0,4},{4,0},{1,5},{5,1},{2,6},{6,2},{3,7},{7,3},{8,12},{12,8},{9,1... | collective-permute-start | bytes 13832 | tf_op jit(solution)/shard_map/ppermute | solution.py:23
  150.7 2.5 %collective-permute-start.34 = (f32[1,512]{1,0:T(1,128)S(1)}, f32[1,512]{1,0:T(1,128)S(1)}, u32[]{:S(2)}, u32[]{:S(2)}) collective-permute-start(f32[1,512]{1,0:T(1,128)S(1)} %pad_maximum_fusion.1.row_0), channel_id=1, source_target_pairs={{0,3},{1,0},{2,1},{3,2},{4,7},{5,4},{6,5},{7,6},{8,11},{9,8},{10,9... | collective-permute-start | bytes 6152 | tf_op jit(solution)/shard_map/ppermute | solution.py:23
  (104 shorter events, 44.8 us)
Async XLA Ops:
  9.3 8.5 %collective-permute-start = (bf16[1,4,144,1024]{3,2,1,0:T(8,128)(2,1)S(1)}, bf16[1,4,144,1024]{3,2,1,0:T(8,128)(2,1)S(1)}, u32[]{:S(2)}, u32[]{:S(2)}) collective-permute-start(bf16[1,4,144,1024]{3,2,1,0:T(8,128)(2,1)S(1)} %get-tuple-element.52), channel_id=1, source_target_pairs={{0,4},{4,0},{1,5},{5,1},{2,6},{6,2},{3,7},{7,3},{8,12},{12,8},{9,1... | collective-permute-start | bytes 3538952 | tf_op jit(solution)/shard_map/ppermute | solution.py:23
  28.1 25.1 %collective-permute-start.2 = (bf16[2,4,144,1024]{3,2,1,0:T(8,128)(2,1)S(1)}, bf16[2,4,144,1024]{3,2,1,0:T(8,128)(2,1)S(1)}, u32[]{:S(2)}, u32[]{:S(2)}) collective-permute-start(bf16[2,4,144,1024]{3,2,1,0:T(8,128)(2,1)S(1)} %get-tuple-element.60), channel_id=1, source_target_pairs={{0,4},{4,0},{1,5},{5,1},{2,6},{6,2},{3,7},{7,3},{8,12},{12,8},{9,1... | collective-permute-start | bytes 7077896 | tf_op jit(solution)/shard_map/ppermute | solution.py:23
  34.9 19.4 %collective-permute-start.4 = (bf16[2,4,128,1152]{3,2,1,0:T(8,128)(2,1)S(1)}, bf16[2,4,128,1152]{3,2,1,0:T(8,128)(2,1)S(1)}, u32[]{:S(2)}, u32[]{:S(2)}) collective-permute-start(bf16[2,4,128,1152]{3,2,1,0:T(8,128)(2,1)S(1)} %get-tuple-element.65), channel_id=1, source_target_pairs={{0,4},{4,0},{1,5},{5,1},{2,6},{6,2},{3,7},{7,3},{8,12},{12,8},{9,1... | collective-permute-start | bytes 7077896 | tf_op jit(solution)/shard_map/ppermute | solution.py:23
  35.4 16.3 %collective-permute-start.9 = (bf16[2,144,1024]{2,1,0:T(8,128)(2,1)S(1)}, bf16[2,144,1024]{2,1,0:T(8,128)(2,1)S(1)}, u32[]{:S(2)}, u32[]{:S(2)}) collective-permute-start(bf16[2,144,1024]{2,1,0:T(8,128)(2,1)S(1)} %get-tuple-element.53), channel_id=1, source_target_pairs={{0,32},{32,64},{64,96},{96,0},{1,33},{33,65},{65,97},{97,1},{2,34}... | collective-permute-start | bytes 1769480 | tf_op jit(solution)/shard_map/ppermute | solution.py:23
  36.8 17.0 %collective-permute-start.3 = (bf16[2,144,1024]{2,1,0:T(8,128)(2,1)S(1)}, bf16[2,144,1024]{2,1,0:T(8,128)(2,1)S(1)}, u32[]{:S(2)}, u32[]{:S(2)}) collective-permute-start(bf16[2,144,1024]{2,1,0:T(8,128)(2,1)S(1)} %get-tuple-element.61), channel_id=1, source_target_pairs={{0,96},{32,0},{64,32},{96,64},{1,97},{33,1},{65,33},{97,65},{2,98}... | collective-permute-start | bytes 1769480 | tf_op jit(solution)/shard_map/ppermute | solution.py:23
  38.2 16.1 %collective-permute-start.5 = (bf16[2,128,1152]{2,1,0:T(8,128)(2,1)S(1)}, bf16[2,128,1152]{2,1,0:T(8,128)(2,1)S(1)}, u32[]{:S(2)}, u32[]{:S(2)}) collective-permute-start(bf16[2,128,1152]{2,1,0:T(8,128)(2,1)S(1)} %get-tuple-element.66), channel_id=1, source_target_pairs={{0,24},{8,0},{16,8},{24,16},{1,25},{9,1},{17,9},{25,17},{2,26},{10... | collective-permute-start | bytes 1769480 | tf_op jit(solution)/shard_map/ppermute | solution.py:23
  51.6 16.3 %collective-permute-start.18 = (bf16[2,128,1152]{2,1,0:T(8,128)(2,1)S(1)}, bf16[2,128,1152]{2,1,0:T(8,128)(2,1)S(1)}, u32[]{:S(2)}, u32[]{:S(2)}) collective-permute-start(bf16[2,128,1152]{2,1,0:T(8,128)(2,1)S(1)} %get-tuple-element.57), channel_id=1, source_target_pairs={{0,8},{8,16},{16,24},{24,0},{1,9},{9,17},{17,25},{25,1},{2,10},{10... | collective-permute-start | bytes 1769480 | tf_op jit(solution)/shard_map/ppermute | solution.py:23
  53.7 23.0 %collective-permute-start.10 = (bf16[2,144,1024]{2,1,0:T(8,128)(2,1)S(1)}, bf16[2,144,1024]{2,1,0:T(8,128)(2,1)S(1)}, u32[]{:S(2)}, u32[]{:S(2)}) collective-permute-start(bf16[2,144,1024]{2,1,0:T(8,128)(2,1)S(1)} %get-tuple-element.75), channel_id=1, source_target_pairs={{0,32},{32,64},{64,96},{96,0},{1,33},{33,65},{65,97},{97,1},{2,34}... | collective-permute-start | bytes 1769480 | tf_op jit(solution)/shard_map/ppermute | solution.py:23
  58.4 37.7 %collective-permute-start.15 = (bf16[1,4,128,1152]{3,2,1,0:T(8,128)(2,1)S(1)}, bf16[1,4,128,1152]{3,2,1,0:T(8,128)(2,1)S(1)}, u32[]{:S(2)}, u32[]{:S(2)}) collective-permute-start(bf16[1,4,128,1152]{3,2,1,0:T(8,128)(2,1)S(1)} %get-tuple-element.80), channel_id=1, source_target_pairs={{0,4},{4,0},{1,5},{5,1},{2,6},{6,2},{3,7},{7,3},{8,12},{12,8},{9,1... | collective-permute-start | bytes 3538952 | tf_op jit(solution)/shard_map/ppermute | solution.py:23
  68.5 14.6 %collective-permute-start.19 = (bf16[2,128,1152]{2,1,0:T(8,128)(2,1)S(1)}, bf16[2,128,1152]{2,1,0:T(8,128)(2,1)S(1)}, u32[]{:S(2)}, u32[]{:S(2)}) collective-permute-start(bf16[2,128,1152]{2,1,0:T(8,128)(2,1)S(1)} %get-tuple-element.83), channel_id=1, source_target_pairs={{0,8},{8,16},{16,24},{24,0},{1,9},{9,17},{17,25},{25,1},{2,10},{10... | collective-permute-start | bytes 1769480 | tf_op jit(solution)/shard_map/ppermute | solution.py:23
  68.6 14.5 %collective-permute-start.20 = (bf16[2,128,1152]{2,1,0:T(8,128)(2,1)S(1)}, bf16[2,128,1152]{2,1,0:T(8,128)(2,1)S(1)}, u32[]{:S(2)}, u32[]{:S(2)}) collective-permute-start(bf16[2,128,1152]{2,1,0:T(8,128)(2,1)S(1)} %get-tuple-element.84), channel_id=1, source_target_pairs={{0,24},{8,0},{16,8},{24,16},{1,25},{9,1},{17,9},{25,17},{2,26},{10... | collective-permute-start | bytes 1769480 | tf_op jit(solution)/shard_map/ppermute | solution.py:23
  74.5 25.9 %collective-permute-start.6 = (bf16[1,4,144,1024]{3,2,1,0:T(8,128)(2,1)S(1)}, bf16[1,4,144,1024]{3,2,1,0:T(8,128)(2,1)S(1)}, u32[]{:S(2)}, u32[]{:S(2)}) collective-permute-start(bf16[1,4,144,1024]{3,2,1,0:T(8,128)(2,1)S(1)} %get-tuple-element.72), channel_id=1, source_target_pairs={{0,4},{4,0},{1,5},{5,1},{2,6},{6,2},{3,7},{7,3},{8,12},{12,8},{9,1... | collective-permute-start | bytes 3538952 | tf_op jit(solution)/shard_map/ppermute | solution.py:23
  76.7 18.1 %collective-permute-start.17 = (bf16[2,128,1152]{2,1,0:T(8,128)(2,1)S(1)}, bf16[2,128,1152]{2,1,0:T(8,128)(2,1)S(1)}, u32[]{:S(2)}, u32[]{:S(2)}) collective-permute-start(bf16[2,128,1152]{2,1,0:T(8,128)(2,1)S(1)} %get-tuple-element.81), channel_id=1, source_target_pairs={{0,24},{8,0},{16,8},{24,16},{1,25},{9,1},{17,9},{25,17},{2,26},{10... | collective-permute-start | bytes 1769480 | tf_op jit(solution)/shard_map/ppermute | solution.py:23
  83.1 13.7 %collective-permute-start.16 = (bf16[2,128,1152]{2,1,0:T(8,128)(2,1)S(1)}, bf16[2,128,1152]{2,1,0:T(8,128)(2,1)S(1)}, u32[]{:S(2)}, u32[]{:S(2)}) collective-permute-start(bf16[2,128,1152]{2,1,0:T(8,128)(2,1)S(1)} %get-tuple-element.67), channel_id=1, source_target_pairs={{0,8},{8,16},{16,24},{24,0},{1,9},{9,17},{17,25},{25,1},{2,10},{10... | collective-permute-start | bytes 1769480 | tf_op jit(solution)/shard_map/ppermute | solution.py:23
  83.1 15.7 %collective-permute-start.11 = (bf16[2,144,1024]{2,1,0:T(8,128)(2,1)S(1)}, bf16[2,144,1024]{2,1,0:T(8,128)(2,1)S(1)}, u32[]{:S(2)}, u32[]{:S(2)}) collective-permute-start(bf16[2,144,1024]{2,1,0:T(8,128)(2,1)S(1)} %get-tuple-element.76), channel_id=1, source_target_pairs={{0,96},{32,0},{64,32},{96,64},{1,97},{33,1},{65,33},{97,65},{2,98}... | collective-permute-start | bytes 1769480 | tf_op jit(solution)/shard_map/ppermute | solution.py:23
  94.8 14.2 %collective-permute-start.8 = (bf16[2,144,1024]{2,1,0:T(8,128)(2,1)S(1)}, bf16[2,144,1024]{2,1,0:T(8,128)(2,1)S(1)}, u32[]{:S(2)}, u32[]{:S(2)}) collective-permute-start(bf16[2,144,1024]{2,1,0:T(8,128)(2,1)S(1)} %get-tuple-element.73), channel_id=1, source_target_pairs={{0,96},{32,0},{64,32},{96,64},{1,97},{33,1},{65,33},{97,65},{2,98}... | collective-permute-start | bytes 1769480 | tf_op jit(solution)/shard_map/ppermute | solution.py:23
  96.1 14.1 %collective-permute-start.7 = (bf16[2,144,1024]{2,1,0:T(8,128)(2,1)S(1)}, bf16[2,144,1024]{2,1,0:T(8,128)(2,1)S(1)}, u32[]{:S(2)}, u32[]{:S(2)}) collective-permute-start(bf16[2,144,1024]{2,1,0:T(8,128)(2,1)S(1)} %get-tuple-element.62), channel_id=1, source_target_pairs={{0,32},{32,64},{64,96},{96,0},{1,33},{33,65},{65,97},{97,1},{2,34}... | collective-permute-start | bytes 1769480 | tf_op jit(solution)/shard_map/ppermute | solution.py:23
  96.8 17.5 %collective-permute-start.21 = (bf16[1,128,1152]{2,1,0:T(8,128)(2,1)S(1)}, bf16[1,128,1152]{2,1,0:T(8,128)(2,1)S(1)}, u32[]{:S(2)}, u32[]{:S(2)}) collective-permute-start(bf16[1,128,1152]{2,1,0:T(8,128)(2,1)S(1)} %get-tuple-element.85), channel_id=1, source_target_pairs={{0,64},{32,96},{64,0},{96,32},{1,65},{33,97},{65,1},{97,33},{2,66}... | collective-permute-start | bytes 884744 | tf_op jit(solution)/shard_map/ppermute | solution.py:23
  98.8 23.1 %collective-permute-start.22 = (bf16[1,128,1152]{2,1,0:T(8,128)(2,1)S(1)}, bf16[1,128,1152]{2,1,0:T(8,128)(2,1)S(1)}, u32[]{:S(2)}, u32[]{:S(2)}) collective-permute-start(bf16[1,128,1152]{2,1,0:T(8,128)(2,1)S(1)} %get-tuple-element.86), channel_id=1, source_target_pairs={{0,32},{32,64},{64,96},{96,0},{1,33},{33,65},{65,97},{97,1},{2,34}... | collective-permute-start | bytes 884744 | tf_op jit(solution)/shard_map/ppermute | solution.py:23
  100.4 21.5 %collective-permute-start.23 = (bf16[1,128,1152]{2,1,0:T(8,128)(2,1)S(1)}, bf16[1,128,1152]{2,1,0:T(8,128)(2,1)S(1)}, u32[]{:S(2)}, u32[]{:S(2)}) collective-permute-start(bf16[1,128,1152]{2,1,0:T(8,128)(2,1)S(1)} %get-tuple-element.87), channel_id=1, source_target_pairs={{0,96},{32,0},{64,32},{96,64},{1,97},{33,1},{65,33},{97,65},{2,98}... | collective-permute-start | bytes 884744 | tf_op jit(solution)/shard_map/ppermute | solution.py:23
  109.0 13.2 %collective-permute-start.12 = (bf16[1,144,1024]{2,1,0:T(8,128)(2,1)S(1)}, bf16[1,144,1024]{2,1,0:T(8,128)(2,1)S(1)}, u32[]{:S(2)}, u32[]{:S(2)}) collective-permute-start(bf16[1,144,1024]{2,1,0:T(8,128)(2,1)S(1)} %get-tuple-element.77), channel_id=1, source_target_pairs={{0,16},{8,24},{16,0},{24,8},{1,17},{9,25},{17,1},{25,9},{2,18},{10... | collective-permute-start | bytes 884744 | tf_op jit(solution)/shard_map/ppermute | solution.py:23
  110.2 12.0 %collective-permute-start.13 = (bf16[1,144,1024]{2,1,0:T(8,128)(2,1)S(1)}, bf16[1,144,1024]{2,1,0:T(8,128)(2,1)S(1)}, u32[]{:S(2)}, u32[]{:S(2)}) collective-permute-start(bf16[1,144,1024]{2,1,0:T(8,128)(2,1)S(1)} %get-tuple-element.78), channel_id=1, source_target_pairs={{0,8},{8,16},{16,24},{24,0},{1,9},{9,17},{17,25},{25,1},{2,10},{10... | collective-permute-start | bytes 884744 | tf_op jit(solution)/shard_map/ppermute | solution.py:23
  123.5 9.7 %collective-permute-start.24 = (f32[1,1280]{1,0:T(1,128)S(1)}, f32[1,1280]{1,0:T(1,128)S(1)}, u32[]{:S(2)}, u32[]{:S(2)}) collective-permute-start(f32[1,1280]{1,0:T(1,128)S(1)} %get-tuple-element.89), channel_id=1, source_target_pairs={{0,4},{4,0},{1,5},{5,1},{2,6},{6,2},{3,7},{7,3},{8,12},{12,8},{9,1... | collective-permute-start | bytes 15368 | tf_op jit(solution)/shard_map/ppermute | solution.py:23
  147.4 9.8 %collective-permute-start.31 = (f32[1,1152]{1,0:T(1,128)S(1)}, f32[1,1152]{1,0:T(1,128)S(1)}, u32[]{:S(2)}, u32[]{:S(2)}) collective-permute-start(f32[1,1152]{1,0:T(1,128)S(1)} %slice.8), channel_id=1, source_target_pairs={{0,4},{4,0},{1,5},{5,1},{2,6},{6,2},{3,7},{7,3},{8,12},{12,8},{9,1... | collective-permute-start | bytes 13832 | tf_op jit(solution)/shard_map/ppermute | solution.py:23
  (23 other events, 166.9 us)

commit v4 on v1

--- a/solution.py
+++ b/solution.py
@@ -263,14 +263,19 @@
     one, two = (2, 1), (3, 0)
     far_plan = [[[(0, e), (1, e)] for e in half] for half in (one, two)]
 
-    def near_plan(half, relayed):
-        plan = [[[(0, base + e), (1, base + e)] for e in half] for base in (0, 4)]
-        for i, terms in enumerate(plan[relayed]):
-            terms.append((2, i))
-        return plan
-
-    last_one = [[[(0, e), (1, e), (2, i), (3, i)]] for i, e in enumerate(one)]
-    last_two = [[[(0, e), (1, e), (2, i), (3, i)]] for i, e in enumerate(two)]
+    forward, stay = (2, 1, 3), (0,)
+
+    def near_plan(entries):
+        plus, minus = [], []
+        for e in entries:
+            own_plus, own_minus = [(0, e), (1, e)], [(0, 4 + e), (1, 4 + e)]
+            plus.append(own_plus + ([(2, one.index(e))] if e in one else []))
+            minus.append(own_minus + ([(3, two.index(e))] if e in two else []))
+        return [plus, minus]
+
+    last_one, last_two = (
+        [[[(0, e), (1, e), (2, i), (3, i)]] for i, e in enumerate(half)] for half in (forward, stay)
+    )
 
     query_made, *query_block = query_blocks(where, (2,), GRANTS[0])
     output_made, *output_block = output_blocks(after(where, query_made), (2,), GRANTS[1])
@@ -285,27 +290,25 @@
     query_made, *query_block = query_blocks(ready, (1, 3), GRANTS[2])
     output_made, *output_block = output_blocks(after(where, query_made), (1, 3), GRANTS[3])
 
-    def near(block, arrived, half, relayed, axis):
-        plus, minus = add_entries((*block, arrived), near_plan(half, relayed))
+    def near(block, arrived, entries, axis):
+        plus, minus = add_entries((*block, *arrived), near_plan(entries))
         return plus, (shift(plus, axis, 1), shift(minus, axis, -1))
 
-    query_plus, query_one = near(query_block, query_low, one, 0, Y)
-    output_plus, output_one = near(output_block, output_low, one, 0, Z)
-    query_plus, query_two = near(query_block, query_high, two, 1, Y)
-    output_plus, output_two = near(output_block, output_high, two, 1, Z)
+    query_far, output_far = (query_low, query_high), (output_low, output_high)
+    query_plus, query_one = near(query_block, query_far, forward, Y)
+    output_plus, output_one = near(output_block, output_far, forward, Z)
+    query_plus, query_two = near(query_block, query_far, stay, Y)
+    output_plus, output_two = near(output_block, output_far, stay, Z)
 
     ready = after(where, query_plus, output_plus)
-    output_made, *output_block = output_blocks(ready, (0,), GRANTS[4])
-    query_made, *query_block = query_blocks(after(where, output_made), (0,), GRANTS[5])
-    wide_own = [jnp.bfloat16, jnp.float32]
-    query_2, query_1 = add_entries((*query_block, *query_one), last_one)
-    query_sent = [shift(query_2, Z, 2), shift(query_1, Z, 1)]
-    output_2, output_1 = add_entries((*output_block, *output_one), last_one)
-    output_sent = [shift(output_2, Y, 2), shift(output_1, Y, 1)]
-    query_3, query_own = add_entries((*query_block, *query_two), last_two, wide_own)
-    query_sent.append(shift(query_3, Z, 3))
-    output_3, output_own = add_entries((*output_block, *output_two), last_two, wide_own)
-    output_sent.append(shift(output_3, Y, 3))
+    query_made, *query_block = query_blocks(ready, (0,), GRANTS[4])
+    output_made, *output_block = output_blocks(after(where, query_made), (0,), GRANTS[5])
+    sends = add_entries((*output_block, *output_one), last_one)
+    output_sent = [shift(v, Y, k) for k, v in zip(forward, sends)]
+    sends = add_entries((*query_block, *query_one), last_one)
+    query_sent = [shift(v, Z, k) for k, v in zip(forward, sends)]
+    (query_own,) = add_entries((*query_block, *query_two), last_two, [jnp.float32])
+    (output_own,) = add_entries((*output_block, *output_two), last_two, [jnp.float32])
     query_grad = query_own[0] + sum(wide(p[0]) for p in query_sent)
     output_grad = output_own[0] + sum(wide(p[0]) for p in output_sent)
 

time: 159 us -> 156 us (0.981)
  waiting for transfers between devices: 63.1 us -> 56.7 us
  starting transfers between devices: 51.4 us -> 54.3 us
    ppermute x27, starting transfers between devices: 33.4 us -> 39.8 us  [shift(): lax.ppermute(value, axis, [(i, (i + by) % size) for i in range(size)])]
    ppermute x27, waiting for transfers between devices: 53.8 us -> 47.4 us  [shift(): lax.ppermute(value, axis, [(i, (i + by) % size) for i in range(size)])]
    all_to_all x1, starting transfers between devices: 18 us -> 14.5 us  [shards(): packed = lax.all_to_all(packed, ROW, 0, 0, tiled=True)]
  transfers between devices with their start and end apart: 28 -> 28, of which waited for: 12 -> 14; matrix products, arithmetic and copies ran while one was open for 0% -> 0% of each run, Pallas kernels for 13% -> 13%
where the time goes in v4:
time: 156 us; the launch traced here: 155 us
  waiting for transfers between devices  56.7 us (36%)
  starting transfers between devices  54.3 us (35%)
  Pallas kernels  32.4 us (21%)
  local copies, waits for them, and re-layouts  9.89 us (6%)
    ppermute x27, waiting for transfers between devices, shift(): lax.ppermute(value, axis, [(i, (i + by) % size) for i in range(size)])  47.4 us
    ppermute x27, starting transfers between devices, shift(): lax.ppermute(value, axis, [(i, (i + by) % size) for i in range(size)])  39.8 us
    pallas_call x6, Pallas kernels, partial_blocks(): pl.pallas_call(functools.partial(kernel, blocks[0], group), out_shape=[sh...  25.8 us
    all_to_all x1, starting transfers between devices, shards(): packed = lax.all_to_all(packed, ROW, 0, 0, tiled=True)  14.5 us
    unnamed x24, local copies, waits for them, and re-layouts  9.78 us
    all_to_all x1, waiting for transfers between devices, shards(): packed = lax.all_to_all(packed, ROW, 0, 0, tiled=True)  9.27 us
    pallas_call x10, Pallas kernels, add_entries(): pl.pallas_call(functools.partial(add_kernel, plan, 16), out_shape=[jax.Sh...  4.67 us
  transfers between devices with their start and end apart: 28, of which 14 were waited for; matrix products, arithmetic and copies ran while one was open for 0% of the time, Pallas kernels for 13%

profile of v4, /device:TPU:1, one launch (start us, length us, event | category | flops | bytes accessed | tf_op | source)
XLA Modules:
  0.0 155.4 jit_solution(10630637990546562872)
XLA Ops:
  0.8 3.7 %copy-done = bf16[1024,4608]{1,0:T(8,128)(2,1)S(1)} copy-done((bf16[1024,4608]{1,0:T(8,128)(2,1)S(1)}, bf16[1024,4608]{1,0:T(8,128)(2,1)}, u32[]{:S(2)}) %copy-start) | copy-done | bytes 9437208
  6.0 3.2 %shard_map.127 = (bf16[1,4,144,1024]{3,2,1,0:T(8,128)(2,1)S(1)}, bf16[1,4,144,1024]{3,2,1,0:T(8,128)(2,1)S(1)}) custom-call(s32[17]{0:T(128)S(1)} %stack.71.where_ref, bf16[1024,4608]{1,0:T(8,128)(2,1)S(1)} %copy-done, bf16[1024,1024]{1,0:T(8,128)(2,1)S(1)} %copy-done.3), custom_call_target="tpu_custom_call" | custom-call | flops 2415919104 | bytes 2359296 | tf_op jit(solution)/shard_map/pallas_call | solution.py:89
  10.7 3.4 %copy-done.1 = bf16[1024,4096]{1,0:T(8,128)(2,1)S(1)} copy-done((bf16[1024,4096]{1,0:T(8,128)(2,1)S(1)}, bf16[1024,4096]{1,0:T(8,128)(2,1)}, u32[]{:S(2)}) %copy-start.1) | copy-done | bytes 8388632
  14.1 3.5 %shard_map.129 = (bf16[1,4,128,1152]{3,2,1,0:T(8,128)(2,1)S(1)}, bf16[1,4,128,1152]{3,2,1,0:T(8,128)(2,1)S(1)}) custom-call(s32[17]{0:T(128)S(1)} %stack.71.where_ref, bf16[1024,4096]{1,0:T(8,128)(2,1)S(1)} %copy-done.1, bf16[1024,1152]{1,0:T(8,128)(2,1)S(1)} %copy-done.2), custom_call_target="tpu_custom_call" | custom-call | flops 2415919104 | bytes 2097152 | tf_op jit(solution)/shard_map/pallas_call | solution.py:89
  22.1 5.9 %shard_map.131 = (bf16[2,4,144,1024]{3,2,1,0:T(8,128)(2,1)S(1)}, bf16[2,4,144,1024]{3,2,1,0:T(8,128)(2,1)S(1)}) custom-call(s32[17]{0:T(128)S(1)} %stack.71.where_ref, bf16[1024,4608]{1,0:T(8,128)(2,1)S(1)} %bitcast.43, bf16[1024,1024]{1,0:T(8,128)(2,1)S(1)} %copy-done.4), custom_call_target="tpu_custom_call" | custom-call | flops 4831838208 | bytes 4718592 | tf_op jit(solution)/shard_map/pallas_call | solution.py:89
  28.5 6.4 %shard_map.133 = (bf16[2,4,128,1152]{3,2,1,0:T(8,128)(2,1)S(1)}, bf16[2,4,128,1152]{3,2,1,0:T(8,128)(2,1)S(1)}) custom-call(s32[17]{0:T(128)S(1)} %stack.71.where_ref, bf16[1024,4096]{1,0:T(8,128)(2,1)S(1)} %copy-done.1, bf16[1024,1152]{1,0:T(8,128)(2,1)S(1)} %copy-done.2), custom_call_target="tpu_custom_call" | custom-call | flops 4831838208 | bytes 4194304 | tf_op jit(solution)/shard_map/pallas_call | solution.py:89
  35.4 2.8 %collective-permute-start.4 = (bf16[2,144,1024]{2,1,0:T(8,128)(2,1)S(1)}, bf16[2,144,1024]{2,1,0:T(8,128)(2,1)S(1)}, u32[]{:S(2)}, u32[]{:S(2)}) collective-permute-start(bf16[2,144,1024]{2,1,0:T(8,128)(2,1)S(1)} %get-tuple-element.59), channel_id=1, source_target_pairs={{0,96},{32,0},{64,32},{96,64},{1,97},{33,1},{65,33},{97,65},{2,98}... | collective-permute-start | bytes 1769480 | tf_op jit(solution)/shard_map/ppermute | solution.py:23
  38.2 3.7 %collective-permute-start.7 = (bf16[2,128,1152]{2,1,0:T(8,128)(2,1)S(1)}, bf16[2,128,1152]{2,1,0:T(8,128)(2,1)S(1)}, u32[]{:S(2)}, u32[]{:S(2)}) collective-permute-start(bf16[2,128,1152]{2,1,0:T(8,128)(2,1)S(1)} %get-tuple-element.64), channel_id=1, source_target_pairs={{0,24},{8,0},{16,8},{24,16},{1,25},{9,1},{17,9},{25,17},{2,26},{10... | collective-permute-start | bytes 1769480 | tf_op jit(solution)/shard_map/ppermute | solution.py:23
  41.9 8.8 %collective-permute-done.4.refs_3_ = bf16[2,144,1024]{2,1,0:T(8,128)(2,1)S(1)} collective-permute-done((bf16[2,144,1024]{2,1,0:T(8,128)(2,1)S(1)}, bf16[2,144,1024]{2,1,0:T(8,128)(2,1)S(1)}, u32[]{:S(2)}, u32[]{:S(2)}) %collective-permute-start.4) | collective-permute-done | bytes 589856 | tf_op jit(solution)/shard_map/ppermute | solution.py:23
  55.1 2.7 %collective-permute-start.10 = (bf16[1,144,1024]{2,1,0:T(8,128)(2,1)S(1)}, bf16[1,144,1024]{2,1,0:T(8,128)(2,1)S(1)}, u32[]{:S(2)}, u32[]{:S(2)}) collective-permute-start(bf16[1,144,1024]{2,1,0:T(8,128)(2,1)S(1)} %get-tuple-element.69), channel_id=1, source_target_pairs={{0,96},{32,0},{64,32},{96,64},{1,97},{33,1},{65,33},{97,65},{2,98}... | collective-permute-start | bytes 884744 | tf_op jit(solution)/shard_map/ppermute | solution.py:23
  58.5 8.7 %collective-permute-done.6.refs_2_ = bf16[2,128,1152]{2,1,0:T(8,128)(2,1)S(1)} collective-permute-done((bf16[2,128,1152]{2,1,0:T(8,128)(2,1)S(1)}, bf16[2,128,1152]{2,1,0:T(8,128)(2,1)S(1)}, u32[]{:S(2)}, u32[]{:S(2)}) %collective-permute-start.6) | collective-permute-done | bytes 589856 | tf_op jit(solution)/shard_map/ppermute | solution.py:23
  67.4 3.2 %shard_map.135 = (bf16[1,4,144,1024]{3,2,1,0:T(8,128)(2,1)S(1)}, bf16[1,4,144,1024]{3,2,1,0:T(8,128)(2,1)S(1)}) custom-call(s32[17]{0:T(128)S(1)} %stack.71.where_ref, bf16[1024,4608]{1,0:T(8,128)(2,1)S(1)} %bitcast.43, bf16[1024,1024]{1,0:T(8,128)(2,1)S(1)} %copy-done.4), custom_call_target="tpu_custom_call" | custom-call | flops 2415919104 | bytes 2359296 | tf_op jit(solution)/shard_map/pallas_call | solution.py:89
  72.3 3.5 %shard_map.139 = (bf16[1,4,128,1152]{3,2,1,0:T(8,128)(2,1)S(1)}, bf16[1,4,128,1152]{3,2,1,0:T(8,128)(2,1)S(1)}) custom-call(s32[17]{0:T(128)S(1)} %stack.71.where_ref, bf16[1024,4096]{1,0:T(8,128)(2,1)S(1)} %copy-done.1, bf16[1024,1152]{1,0:T(8,128)(2,1)S(1)} %copy-done.2), custom_call_target="tpu_custom_call" | custom-call | flops 2415919104 | bytes 2097152 | tf_op jit(solution)/shard_map/pallas_call | solution.py:89
  77.1 2.7 %collective-permute-start.20 = (bf16[3,128,1152]{2,1,0:T(8,128)(2,1)S(1)}, bf16[3,128,1152]{2,1,0:T(8,128)(2,1)S(1)}, u32[]{:S(2)}, u32[]{:S(2)}) collective-permute-start(bf16[3,128,1152]{2,1,0:T(8,128)(2,1)S(1)} %get-tuple-element.80), channel_id=1, source_target_pairs={{0,24},{8,0},{16,8},{24,16},{1,25},{9,1},{17,9},{25,17},{2,26},{10... | collective-permute-start | bytes 2654216 | tf_op jit(solution)/shard_map/ppermute | solution.py:23
  82.7 2.6 %collective-permute-start.18 = (bf16[1,128,1152]{2,1,0:T(8,128)(2,1)S(1)}, bf16[1,128,1152]{2,1,0:T(8,128)(2,1)S(1)}, u32[]{:S(2)}, u32[]{:S(2)}) collective-permute-start(bf16[1,128,1152]{2,1,0:T(8,128)(2,1)S(1)} %get-tuple-element.78), channel_id=1, source_target_pairs={{0,24},{8,0},{16,8},{24,16},{1,25},{9,1},{17,9},{25,17},{2,26},{10... | collective-permute-start | bytes 884744 | tf_op jit(solution)/shard_map/ppermute | solution.py:23
  85.9 4.0 %collective-permute-done.9.refs_2_ = bf16[1,144,1024]{2,1,0:T(8,128)(2,1)S(1)} collective-permute-done((bf16[1,144,1024]{2,1,0:T(8,128)(2,1)S(1)}, bf16[1,144,1024]{2,1,0:T(8,128)(2,1)S(1)}, u32[]{:S(2)}, u32[]{:S(2)}) %collective-permute-start.9) | collective-permute-done | bytes 294944 | tf_op jit(solution)/shard_map/ppermute | solution.py:23
  91.6 7.4 %collective-permute-done.19.refs_2_ = bf16[3,128,1152]{2,1,0:T(8,128)(2,1)S(1)} collective-permute-done((bf16[3,128,1152]{2,1,0:T(8,128)(2,1)S(1)}, bf16[3,128,1152]{2,1,0:T(8,128)(2,1)S(1)}, u32[]{:S(2)}, u32[]{:S(2)}) %collective-permute-start.19) | collective-permute-done | bytes 884768 | tf_op jit(solution)/shard_map/ppermute | solution.py:23
  103.7 3.6 %collective-permute-start.21 = (bf16[1,128,1152]{2,1,0:T(8,128)(2,1)S(1)}, bf16[1,128,1152]{2,1,0:T(8,128)(2,1)S(1)}, u32[]{:S(2)}, u32[]{:S(2)}) collective-permute-start(bf16[1,128,1152]{2,1,0:T(8,128)(2,1)S(1)} %get-tuple-element.81), channel_id=1, source_target_pairs={{0,64},{32,96},{64,0},{96,32},{1,65},{33,97},{65,1},{97,33},{2,66}... | collective-permute-start | bytes 884744 | tf_op jit(solution)/shard_map/ppermute | solution.py:23
  108.9 2.7 %collective-permute-done.13 = bf16[1,144,1024]{2,1,0:T(8,128)(2,1)S(1)} collective-permute-done((bf16[1,144,1024]{2,1,0:T(8,128)(2,1)S(1)}, bf16[1,144,1024]{2,1,0:T(8,128)(2,1)S(1)}, u32[]{:S(2)}, u32[]{:S(2)}) %collective-permute-start.13) | collective-permute-done | bytes 294944 | tf_op jit(solution)/shard_map/ppermute | solution.py:23
  111.6 3.4 %collective-permute-start.23 = (bf16[1,128,1152]{2,1,0:T(8,128)(2,1)S(1)}, bf16[1,128,1152]{2,1,0:T(8,128)(2,1)S(1)}, u32[]{:S(2)}, u32[]{:S(2)}) collective-permute-start(bf16[1,128,1152]{2,1,0:T(8,128)(2,1)S(1)} %get-tuple-element.83), channel_id=1, source_target_pairs={{0,96},{32,0},{64,32},{96,64},{1,97},{33,1},{65,33},{97,65},{2,98}... | collective-permute-start | bytes 884744 | tf_op jit(solution)/shard_map/ppermute | solution.py:23
  115.2 2.7 %collective-permute-done.14 = bf16[1,144,1024]{2,1,0:T(8,128)(2,1)S(1)} collective-permute-done((bf16[1,144,1024]{2,1,0:T(8,128)(2,1)S(1)}, bf16[1,144,1024]{2,1,0:T(8,128)(2,1)S(1)}, u32[]{:S(2)}, u32[]{:S(2)}) %collective-permute-start.14) | collective-permute-done | bytes 294944 | tf_op jit(solution)/shard_map/ppermute | solution.py:23
  118.3 4.0 %collective-permute-done.23 = bf16[1,128,1152]{2,1,0:T(8,128)(2,1)S(1)} collective-permute-done((bf16[1,128,1152]{2,1,0:T(8,128)(2,1)S(1)}, bf16[1,128,1152]{2,1,0:T(8,128)(2,1)S(1)}, u32[]{:S(2)}, u32[]{:S(2)}) %collective-permute-start.23) | collective-permute-done | bytes 294944 | tf_op jit(solution)/shard_map/ppermute | solution.py:23
  129.8 14.5 %all-to-all-start = ((f32[32,1,2304]{2,1,0:T(1,128)}), f32[32,1,2304]{2,1,0:T(1,128)S(1)}, u32[]{:S(2)}, u32[]{:S(2)}) async-start(f32[32,1,2304]{2,1,0:T(1,128)} %get-tuple-element.84), calls=%async_computation | async-start | bytes 589824 | tf_op jit(solution)/shard_map/all_to_all | solution.py:333
  144.4 9.3 %all-to-all-done.sums_ref = f32[32,1,2304]{2,1,0:T(1,128)S(1)} async-done(((f32[32,1,2304]{2,1,0:T(1,128)}), f32[32,1,2304]{2,1,0:T(1,128)S(1)}, u32[]{:S(2)}, u32[]{:S(2)}) %all-to-all-start) | async-done | bytes 294944 | tf_op jit(solution)/shard_map/all_to_all | solution.py:333
  (84 shorter events, 38.0 us)
Async XLA Ops:
  9.3 8.5 %collective-permute-start = (bf16[1,4,144,1024]{3,2,1,0:T(8,128)(2,1)S(1)}, bf16[1,4,144,1024]{3,2,1,0:T(8,128)(2,1)S(1)}, u32[]{:S(2)}, u32[]{:S(2)}) collective-permute-start(bf16[1,4,144,1024]{3,2,1,0:T(8,128)(2,1)S(1)} %get-tuple-element.50), channel_id=1, source_target_pairs={{0,4},{4,0},{1,5},{5,1},{2,6},{6,2},{3,7},{7,3},{8,12},{12,8},{9,1... | collective-permute-start | bytes 3538952 | tf_op jit(solution)/shard_map/ppermute | solution.py:23
  28.1 25.8 %collective-permute-start.2 = (bf16[2,4,144,1024]{3,2,1,0:T(8,128)(2,1)S(1)}, bf16[2,4,144,1024]{3,2,1,0:T(8,128)(2,1)S(1)}, u32[]{:S(2)}, u32[]{:S(2)}) collective-permute-start(bf16[2,4,144,1024]{3,2,1,0:T(8,128)(2,1)S(1)} %get-tuple-element.58), channel_id=1, source_target_pairs={{0,4},{4,0},{1,5},{5,1},{2,6},{6,2},{3,7},{7,3},{8,12},{12,8},{9,1... | collective-permute-start | bytes 7077896 | tf_op jit(solution)/shard_map/ppermute | solution.py:23
  34.9 32.3 %collective-permute-start.5 = (bf16[2,4,128,1152]{3,2,1,0:T(8,128)(2,1)S(1)}, bf16[2,4,128,1152]{3,2,1,0:T(8,128)(2,1)S(1)}, u32[]{:S(2)}, u32[]{:S(2)}) collective-permute-start(bf16[2,4,128,1152]{3,2,1,0:T(8,128)(2,1)S(1)} %get-tuple-element.63), channel_id=1, source_target_pairs={{0,4},{4,0},{1,5},{5,1},{2,6},{6,2},{3,7},{7,3},{8,12},{12,8},{9,1... | collective-permute-start | bytes 7077896 | tf_op jit(solution)/shard_map/ppermute | solution.py:23
  35.4 15.4 %collective-permute-start.4 = (bf16[2,144,1024]{2,1,0:T(8,128)(2,1)S(1)}, bf16[2,144,1024]{2,1,0:T(8,128)(2,1)S(1)}, u32[]{:S(2)}, u32[]{:S(2)}) collective-permute-start(bf16[2,144,1024]{2,1,0:T(8,128)(2,1)S(1)} %get-tuple-element.59), channel_id=1, source_target_pairs={{0,96},{32,0},{64,32},{96,64},{1,97},{33,1},{65,33},{97,65},{2,98}... | collective-permute-start | bytes 1769480 | tf_op jit(solution)/shard_map/ppermute | solution.py:23
  38.2 15.7 %collective-permute-start.3 = (bf16[2,144,1024]{2,1,0:T(8,128)(2,1)S(1)}, bf16[2,144,1024]{2,1,0:T(8,128)(2,1)S(1)}, u32[]{:S(2)}, u32[]{:S(2)}) collective-permute-start(bf16[2,144,1024]{2,1,0:T(8,128)(2,1)S(1)} %get-tuple-element.51), channel_id=1, source_target_pairs={{0,32},{32,64},{64,96},{96,0},{1,33},{33,65},{65,97},{97,1},{2,34}... | collective-permute-start | bytes 1769480 | tf_op jit(solution)/shard_map/ppermute | solution.py:23
  38.2 19.6 %collective-permute-start.7 = (bf16[2,128,1152]{2,1,0:T(8,128)(2,1)S(1)}, bf16[2,128,1152]{2,1,0:T(8,128)(2,1)S(1)}, u32[]{:S(2)}, u32[]{:S(2)}) collective-permute-start(bf16[2,128,1152]{2,1,0:T(8,128)(2,1)S(1)} %get-tuple-element.64), channel_id=1, source_target_pairs={{0,24},{8,0},{16,8},{24,16},{1,25},{9,1},{17,9},{25,17},{2,26},{10... | collective-permute-start | bytes 1769480 | tf_op jit(solution)/shard_map/ppermute | solution.py:23
  50.7 16.4 %collective-permute-start.6 = (bf16[2,128,1152]{2,1,0:T(8,128)(2,1)S(1)}, bf16[2,128,1152]{2,1,0:T(8,128)(2,1)S(1)}, u32[]{:S(2)}, u32[]{:S(2)}) collective-permute-start(bf16[2,128,1152]{2,1,0:T(8,128)(2,1)S(1)} %get-tuple-element.55), channel_id=1, source_target_pairs={{0,8},{8,16},{16,24},{24,0},{1,9},{9,17},{17,25},{25,1},{2,10},{10... | collective-permute-start | bytes 1769480 | tf_op jit(solution)/shard_map/ppermute | solution.py:23
  54.7 22.3 %collective-permute-start.11 = (bf16[3,144,1024]{2,1,0:T(8,128)(2,1)S(1)}, bf16[3,144,1024]{2,1,0:T(8,128)(2,1)S(1)}, u32[]{:S(2)}, u32[]{:S(2)}) collective-permute-start(bf16[3,144,1024]{2,1,0:T(8,128)(2,1)S(1)} %get-tuple-element.70), channel_id=1, source_target_pairs={{0,32},{32,64},{64,96},{96,0},{1,33},{33,65},{65,97},{97,1},{2,34}... | collective-permute-start | bytes 2654216 | tf_op jit(solution)/shard_map/ppermute | solution.py:23
  55.1 21.7 %collective-permute-start.10 = (bf16[1,144,1024]{2,1,0:T(8,128)(2,1)S(1)}, bf16[1,144,1024]{2,1,0:T(8,128)(2,1)S(1)}, u32[]{:S(2)}, u32[]{:S(2)}) collective-permute-start(bf16[1,144,1024]{2,1,0:T(8,128)(2,1)S(1)} %get-tuple-element.69), channel_id=1, source_target_pairs={{0,96},{32,0},{64,32},{96,64},{1,97},{33,1},{65,33},{97,65},{2,98}... | collective-permute-start | bytes 884744 | tf_op jit(solution)/shard_map/ppermute | solution.py:23
  57.8 23.8 %collective-permute-start.12 = (bf16[3,144,1024]{2,1,0:T(8,128)(2,1)S(1)}, bf16[3,144,1024]{2,1,0:T(8,128)(2,1)S(1)}, u32[]{:S(2)}, u32[]{:S(2)}) collective-permute-start(bf16[3,144,1024]{2,1,0:T(8,128)(2,1)S(1)} %get-tuple-element.71), channel_id=1, source_target_pairs={{0,96},{32,0},{64,32},{96,64},{1,97},{33,1},{65,33},{97,65},{2,98}... | collective-permute-start | bytes 2654216 | tf_op jit(solution)/shard_map/ppermute | solution.py:23
  70.7 12.0 %collective-permute-start.8 = (bf16[1,4,144,1024]{3,2,1,0:T(8,128)(2,1)S(1)}, bf16[1,4,144,1024]{3,2,1,0:T(8,128)(2,1)S(1)}, u32[]{:S(2)}, u32[]{:S(2)}) collective-permute-start(bf16[1,4,144,1024]{3,2,1,0:T(8,128)(2,1)S(1)} %get-tuple-element.68), channel_id=1, source_target_pairs={{0,4},{4,0},{1,5},{5,1},{2,6},{6,2},{3,7},{7,3},{8,12},{12,8},{9,1... | collective-permute-start | bytes 3538952 | tf_op jit(solution)/shard_map/ppermute | solution.py:23
  75.8 24.0 %collective-permute-start.16 = (bf16[1,4,128,1152]{3,2,1,0:T(8,128)(2,1)S(1)}, bf16[1,4,128,1152]{3,2,1,0:T(8,128)(2,1)S(1)}, u32[]{:S(2)}, u32[]{:S(2)}) collective-permute-start(bf16[1,4,128,1152]{3,2,1,0:T(8,128)(2,1)S(1)} %get-tuple-element.77), channel_id=1, source_target_pairs={{0,4},{4,0},{1,5},{5,1},{2,6},{6,2},{3,7},{7,3},{8,12},{12,8},{9,1... | collective-permute-start | bytes 3538952 | tf_op jit(solution)/shard_map/ppermute | solution.py:23
  76.7 22.2 %collective-permute-start.19 = (bf16[3,128,1152]{2,1,0:T(8,128)(2,1)S(1)}, bf16[3,128,1152]{2,1,0:T(8,128)(2,1)S(1)}, u32[]{:S(2)}, u32[]{:S(2)}) collective-permute-start(bf16[3,128,1152]{2,1,0:T(8,128)(2,1)S(1)} %get-tuple-element.79), channel_id=1, source_target_pairs={{0,8},{8,16},{16,24},{24,0},{1,9},{9,17},{17,25},{25,1},{2,10},{10... | collective-permute-start | bytes 2654216 | tf_op jit(solution)/shard_map/ppermute | solution.py:23
  77.1 22.0 %collective-permute-start.20 = (bf16[3,128,1152]{2,1,0:T(8,128)(2,1)S(1)}, bf16[3,128,1152]{2,1,0:T(8,128)(2,1)S(1)}, u32[]{:S(2)}, u32[]{:S(2)}) collective-permute-start(bf16[3,128,1152]{2,1,0:T(8,128)(2,1)S(1)} %get-tuple-element.80), channel_id=1, source_target_pairs={{0,24},{8,0},{16,8},{24,16},{1,25},{9,1},{17,9},{25,17},{2,26},{10... | collective-permute-start | bytes 2654216 | tf_op jit(solution)/shard_map/ppermute | solution.py:23
  81.6 8.4 %collective-permute-start.9 = (bf16[1,144,1024]{2,1,0:T(8,128)(2,1)S(1)}, bf16[1,144,1024]{2,1,0:T(8,128)(2,1)S(1)}, u32[]{:S(2)}, u32[]{:S(2)}) collective-permute-start(bf16[1,144,1024]{2,1,0:T(8,128)(2,1)S(1)} %get-tuple-element.60), channel_id=1, source_target_pairs={{0,32},{32,64},{64,96},{96,0},{1,33},{33,65},{65,97},{97,1},{2,34}... | collective-permute-start | bytes 884744 | tf_op jit(solution)/shard_map/ppermute | solution.py:23
  82.7 21.1 %collective-permute-start.18 = (bf16[1,128,1152]{2,1,0:T(8,128)(2,1)S(1)}, bf16[1,128,1152]{2,1,0:T(8,128)(2,1)S(1)}, u32[]{:S(2)}, u32[]{:S(2)}) collective-permute-start(bf16[1,128,1152]{2,1,0:T(8,128)(2,1)S(1)} %get-tuple-element.78), channel_id=1, source_target_pairs={{0,24},{8,0},{16,8},{24,16},{1,25},{9,1},{17,9},{25,17},{2,26},{10... | collective-permute-start | bytes 884744 | tf_op jit(solution)/shard_map/ppermute | solution.py:23
  89.9 17.4 %collective-permute-start.17 = (bf16[1,128,1152]{2,1,0:T(8,128)(2,1)S(1)}, bf16[1,128,1152]{2,1,0:T(8,128)(2,1)S(1)}, u32[]{:S(2)}, u32[]{:S(2)}) collective-permute-start(bf16[1,128,1152]{2,1,0:T(8,128)(2,1)S(1)} %get-tuple-element.65), channel_id=1, source_target_pairs={{0,8},{8,16},{16,24},{24,0},{1,9},{9,17},{17,25},{25,1},{2,10},{10... | collective-permute-start | bytes 884744 | tf_op jit(solution)/shard_map/ppermute | solution.py:23
  99.0 12.7 %collective-permute-start.13 = (bf16[1,144,1024]{2,1,0:T(8,128)(2,1)S(1)}, bf16[1,144,1024]{2,1,0:T(8,128)(2,1)S(1)}, u32[]{:S(2)}, u32[]{:S(2)}) collective-permute-start(bf16[1,144,1024]{2,1,0:T(8,128)(2,1)S(1)} %get-tuple-element.72), channel_id=1, source_target_pairs={{0,16},{8,24},{16,0},{24,8},{1,17},{9,25},{17,1},{25,9},{2,18},{10... | collective-permute-start | bytes 884744 | tf_op jit(solution)/shard_map/ppermute | solution.py:23
  99.1 18.8 %collective-permute-start.14 = (bf16[1,144,1024]{2,1,0:T(8,128)(2,1)S(1)}, bf16[1,144,1024]{2,1,0:T(8,128)(2,1)S(1)}, u32[]{:S(2)}, u32[]{:S(2)}) collective-permute-start(bf16[1,144,1024]{2,1,0:T(8,128)(2,1)S(1)} %get-tuple-element.73), channel_id=1, source_target_pairs={{0,8},{8,16},{16,24},{24,0},{1,9},{9,17},{17,25},{25,1},{2,10},{10... | collective-permute-start | bytes 884744 | tf_op jit(solution)/shard_map/ppermute | solution.py:23
  99.8 18.1 %collective-permute-start.15 = (bf16[1,144,1024]{2,1,0:T(8,128)(2,1)S(1)}, bf16[1,144,1024]{2,1,0:T(8,128)(2,1)S(1)}, u32[]{:S(2)}, u32[]{:S(2)}) collective-permute-start(bf16[1,144,1024]{2,1,0:T(8,128)(2,1)S(1)} %get-tuple-element.74), channel_id=1, source_target_pairs={{0,24},{8,0},{16,8},{24,16},{1,25},{9,1},{17,9},{25,17},{2,26},{10... | collective-permute-start | bytes 884744 | tf_op jit(solution)/shard_map/ppermute | solution.py:23
  103.7 14.5 %collective-permute-start.21 = (bf16[1,128,1152]{2,1,0:T(8,128)(2,1)S(1)}, bf16[1,128,1152]{2,1,0:T(8,128)(2,1)S(1)}, u32[]{:S(2)}, u32[]{:S(2)}) collective-permute-start(bf16[1,128,1152]{2,1,0:T(8,128)(2,1)S(1)} %get-tuple-element.81), channel_id=1, source_target_pairs={{0,64},{32,96},{64,0},{96,32},{1,65},{33,97},{65,1},{97,33},{2,66}... | collective-permute-start | bytes 884744 | tf_op jit(solution)/shard_map/ppermute | solution.py:23
  107.3 10.9 %collective-permute-start.22 = (bf16[1,128,1152]{2,1,0:T(8,128)(2,1)S(1)}, bf16[1,128,1152]{2,1,0:T(8,128)(2,1)S(1)}, u32[]{:S(2)}, u32[]{:S(2)}) collective-permute-start(bf16[1,128,1152]{2,1,0:T(8,128)(2,1)S(1)} %get-tuple-element.82), channel_id=1, source_target_pairs={{0,32},{32,64},{64,96},{96,0},{1,33},{33,65},{65,97},{97,1},{2,34}... | collective-permute-start | bytes 884744 | tf_op jit(solution)/shard_map/ppermute | solution.py:23
  111.6 10.6 %collective-permute-start.23 = (bf16[1,128,1152]{2,1,0:T(8,128)(2,1)S(1)}, bf16[1,128,1152]{2,1,0:T(8,128)(2,1)S(1)}, u32[]{:S(2)}, u32[]{:S(2)}) collective-permute-start(bf16[1,128,1152]{2,1,0:T(8,128)(2,1)S(1)} %get-tuple-element.83), channel_id=1, source_target_pairs={{0,96},{32,0},{64,32},{96,64},{1,97},{33,1},{65,33},{97,65},{2,98}... | collective-permute-start | bytes 884744 | tf_op jit(solution)/shard_map/ppermute | solution.py:23
  129.8 23.8 %all-to-all-start = ((f32[32,1,2304]{2,1,0:T(1,128)}), f32[32,1,2304]{2,1,0:T(1,128)S(1)}, u32[]{:S(2)}, u32[]{:S(2)}) async-start(f32[32,1,2304]{2,1,0:T(1,128)} %get-tuple-element.84), calls=%async_computation | async-start | bytes 589824 | tf_op jit(solution)/shard_map/all_to_all | solution.py:333
  (16 other events, 128.2 us)
